TPU v7x, 32 devices: a whole 2x2x4 slice. The times are simulated.
32 devices in a mesh: groups: 2 (over x), patch: 16 (over z, y, core).
Axes of the slice: x: 2, y: 2, z: 4, core: 2. Of those that a mesh axis runs over, the one named last changes fastest.
Arguments:
- queries: bfloat16 [1024, 1536], P(('groups', 'patch')), parts along dimension 0, may hold values from -8 to 8
- fresh_keys: bfloat16 [1024, 1536], P(('groups', 'patch')), parts along dimension 0, may hold values from -8 to 8
- fresh_values: bfloat16 [1024, 1536], P(('groups', 'patch')), parts along dimension 0, may hold values from -128 to 128
- stale_keys: bfloat16 [1024, 1536], P(('groups', 'patch')), parts along dimension 0, may hold values from -8 to 8
- stale_values: bfloat16 [1024, 1536], P(('groups', 'patch')), parts along dimension 0, may hold values from -128 to 128
- text_keys: bfloat16 [452, 1536], P('groups'), parts along dimension 0, may hold values from -8 to 8
- text_values: bfloat16 [452, 1536], P('groups'), parts along dimension 0, may hold values from -128 to 128
- out_weight: bfloat16 [1536, 3072], P(None, 'patch'), may hold values from -0.15625 to 0.15625
- gate_table: float32 [50, 3072], replicated, may hold values from 0.1 to 1.9
- timestep: int32 [2], P('groups'), parts along dimension 0, may hold values from 0 to 49
Outputs:
- branch: bfloat16 [1024, 3072], P(('groups', 'patch')), parts along dimension 0
There are 2 independent parts, one for each index of `groups`. A program takes and returns all parts, laid end to end along the dimension named above; an argument that names none is the same for every part. Nothing has to cross between parts.
All inputs are finite; a program needn't handle non-finite values.
Results may differ from a plain program's by a relative error of at most 0.0095.
Values may be sent and summed in bfloat16 or wider, within the bound.
No kernel may reach another device: no remote copies, remote signals or barrier semaphores. Data moves between devices by JAX's collectives and lax.ppermute only.
A program may use at most 128 MiB of HBM per device.

v0:
```python
import functools
import math

import jax
import jax.numpy as jnp
from jax import lax
from jax.experimental import pallas as pl
from jax.experimental.pallas import tpu as pltpu
from jax.sharding import PartitionSpec as P


HEAD_DIM = 64
LANES = 128


def from_behind(shard, axis, by):
    peers = lax.axis_size(axis)
    return lax.ppermute(shard, axis, [(i, (i + by) % peers) for i in range(peers)])


def pick_group(stacked, position):
    return lax.dynamic_index_in_dim(stacked, position, 0, keepdims=False)


def by_group(matrix, group_count):
    width = matrix.shape[1] // group_count
    return matrix.reshape(matrix.shape[0], group_count, width).transpose(1, 0, 2)


def swap_block(stacked, group_count, position):
    received = [pick_group(stacked, position)]
    for step_size in range(1, group_count):
        payload = pick_group(stacked, (position + step_size) % group_count)
        arrived = []
        for offset_by in (step_size, step_size - group_count):
            arrived.append(from_behind(payload, "patch", offset_by))
        received.append(jnp.where(position >= step_size, arrived[0], arrived[1]))
    ordered = jnp.stack(received, 0)
    order = (position - jnp.arange(group_count, dtype=jnp.int32)) % group_count
    return jnp.take(ordered, order, axis=0)


def general_body(
    queries,
    fresh_keys,
    fresh_values,
    stale_keys,
    stale_values,
    text_keys,
    text_values,
    out_weight,
    gate_table,
    timestep,
):
    row_count = queries.shape[0]
    head_width = HEAD_DIM
    head_count = queries.shape[1] // head_width
    scaling = head_width ** (-0.5)
    device_count = lax.axis_size("patch")
    group_count = math.gcd(math.gcd(head_count, 8), device_count)
    group_heads = head_count // group_count
    group_width = group_heads * head_width
    position = lax.axis_index("patch") % group_count
    block_first = lax.axis_index("patch") // group_count * group_count
    local_stack = jnp.stack(
        [
            by_group(queries, group_count),
            by_group(fresh_keys, group_count),
            by_group(fresh_values, group_count),
        ],
        1,
    )
    block_stack = swap_block(local_stack, group_count, position)
    block_rows_count = group_count * row_count
    block_query = block_stack[:, 0].reshape(block_rows_count, group_heads, head_width)
    block_keys = block_stack[:, 1].reshape(block_rows_count, group_heads, head_width)
    block_values = block_stack[:, 2].reshape(block_rows_count, group_heads, head_width)
    copies = device_count // group_count
    spread_keys = jnp.tile(by_group(stale_keys, group_count), (copies, 1, 1))
    spread_values = jnp.tile(by_group(stale_values, group_count), (copies, 1, 1))
    every_keys, every_values = (
        lax.all_to_all(spread_keys, "patch", split_axis=0, concat_axis=0, tiled=True),
        lax.all_to_all(spread_values, "patch", split_axis=0, concat_axis=0, tiled=True),
    )
    every_keys = every_keys.reshape(device_count * row_count, group_heads, head_width)
    every_values = every_values.reshape(device_count * row_count, group_heads, head_width)
    text_k = pick_group(by_group(text_keys, group_count), position)
    text_k = text_k.reshape(-1, group_heads, head_width)
    text_v = pick_group(by_group(text_values, group_count), position)
    text_v = text_v.reshape(-1, group_heads, head_width)
    query_patch = jnp.arange(block_rows_count, dtype=jnp.int32) // row_count
    stale_patch = jnp.arange(device_count * row_count, dtype=jnp.int32) // row_count
    stale_mask = stale_patch[None, :] != (block_first + query_patch)[:, None]
    fresh_mask = query_patch[None, :] == query_patch[:, None]

    def scored(key_block):
        return (
            jnp.einsum("qhd,khd->qhk", block_query, key_block, preferred_element_type=jnp.float32)
            * scaling
        )

    text_scores = scored(text_k)
    fresh_scores = jnp.where(fresh_mask[:, None, :], scored(block_keys), -1e30)
    stale_scores = jnp.where(stale_mask[:, None, :], scored(every_keys), -1e30)
    highest = jnp.maximum(
        jnp.maximum(jnp.max(text_scores, -1), jnp.max(fresh_scores, -1)), jnp.max(stale_scores, -1)
    )
    text_expo = jnp.exp(text_scores - highest[..., None])
    fresh_expo = jnp.exp(fresh_scores - highest[..., None])
    stale_expo = jnp.exp(stale_scores - highest[..., None])
    total = jnp.sum(text_expo, -1) + jnp.sum(fresh_expo, -1) + jnp.sum(stale_expo, -1)

    def weigh_block(expo, value_block):
        return jnp.einsum(
            "qhk,khd->qhd",
            expo.astype(jnp.bfloat16),
            value_block,
            preferred_element_type=jnp.float32,
        )

    weighted = (
        weigh_block(text_expo, text_v)
        + weigh_block(fresh_expo, block_values)
        + weigh_block(stale_expo, every_values)
    )
    block_out = (
        (weighted / total[..., None])
        .reshape(group_count, row_count, group_width)
        .astype(jnp.bfloat16)
    )
    home = swap_block(block_out, group_count, position)
    attended = home.transpose(1, 0, 2).reshape(row_count, head_count * head_width)
    projected = jnp.dot(
        attended,
        lax.all_gather(out_weight, "patch", axis=1, tiled=True),
        preferred_element_type=jnp.float32,
    )
    selector = (jnp.arange(gate_table.shape[0], dtype=jnp.int32) == timestep[0]).astype(jnp.float32)
    gating = jnp.dot(selector, gate_table, precision=lax.Precision.HIGHEST)
    return (projected * gating[None, :]).astype(jnp.bfloat16)


QUAD = 4
GRANT = 8 * 2**20


def swap(shard, by):
    peers = lax.axis_size("patch")
    return lax.ppermute(shard, "patch", [(i, i ^ by) for i in range(peers)])


def pack_kernel(q_ref, fk_ref, fv_ref, sk_ref, sv_ref, *refs):
    outs, sem = refs[:-1], refs[-1]
    lines = len(outs) // 2
    line = lax.axis_index("patch") // QUAD
    width = q_ref.shape[1] // lines
    copies = []
    for half, sources in ((0, (sk_ref, sv_ref)), (lines, (q_ref, fk_ref, fv_ref))):
        for k in reversed(range(lines)):
            cols = pl.ds(pl.multiple_of((line ^ k) * width, LANES), width)
            for t, source in enumerate(sources):
                copy = pltpu.make_async_copy(
                    source.at[:, cols],
                    outs[half + k].at[:, t * width : (t + 1) * width],
                    sem.at[len(copies)],
                )
                copy.start()
                copies.append(copy)
    for copy in copies:
        copy.wait()


def fetch_kernel(step_ref, tk_ref, tv_ref, gate_ref, tk_out, tv_out, gate_out, sem):
    width, out_width = tk_out.shape[1], gate_out.shape[1]
    line = lax.axis_index("patch") // QUAD
    cols = pl.ds(pl.multiple_of(line * width, LANES), width)
    gate_cols = pl.ds(pl.multiple_of(line * out_width, LANES), out_width)
    copies = [
        pltpu.make_async_copy(tk_ref.at[:, cols], tk_out, sem.at[0]),
        pltpu.make_async_copy(tv_ref.at[:, cols], tv_out, sem.at[1]),
        pltpu.make_async_copy(gate_ref.at[pl.ds(step_ref[0], 1), gate_cols], gate_out, sem.at[2]),
    ]
    for copy in copies:
        copy.start()
    for copy in copies:
        copy.wait()


def join_kernel(*refs):
    parts, out = refs[:-1], refs[-1]
    rows = parts[0].shape[0]
    for k, part in enumerate(parts):
        out[k * rows : (k + 1) * rows, :] = part[...]


def attend_kernel(rows, tk_ref, tv_ref, *refs):
    lines = (len(refs) - 4) // 2
    fresh = refs[:lines]
    own = refs[lines : 2 * lines]
    far = refs[2 * lines : 2 * lines + 3]
    out = refs[-1]
    width = out.shape[1]
    count = rows * lines
    nt = (((1,), (1,)), ((), ()))
    nn = (((1,), (0,)), ((), ()))
    lane = lax.broadcasted_iota(jnp.int32, (1, LANES), 1)
    low = lane < HEAD_DIM
    row_block = (lax.broadcasted_iota(jnp.int32, (2 * count, count), 0) % count) // rows
    col_block = lax.broadcasted_iota(jnp.int32, (2 * count, count), 1) // rows
    same = row_block == col_block
    scaling = HEAD_DIM**-0.5
    f32 = jnp.float32
    for pair in range(width // LANES):
        cols = slice(pair * LANES, (pair + 1) * LANES)
        kcols = slice(width + pair * LANES, width + (pair + 1) * LANES)
        vcols = slice(2 * width + pair * LANES, 2 * width + (pair + 1) * LANES)
        q = jnp.concatenate([fresh[k][:, cols] for k in range(lines)], 0)
        q = (q.astype(f32) * scaling).astype(q.dtype)
        zero = jnp.zeros_like(q)
        q2 = jnp.concatenate([jnp.where(low, q, zero), jnp.where(low, zero, q)], 0)
        fk = jnp.concatenate([fresh[k][:, kcols] for k in range(lines)], 0)
        fv = jnp.concatenate([fresh[k][:, vcols] for k in range(lines)], 0)
        sk = jnp.concatenate([own[k][:, cols] for k in range(lines)], 0)
        sv = jnp.concatenate([own[k][:, kcols] for k in range(lines)], 0)
        s_fresh = lax.dot_general(q2, fk, nt, preferred_element_type=f32)
        s_own = lax.dot_general(q2, sk, nt, preferred_element_type=f32)
        s_near = jnp.where(same, s_fresh, s_own)
        s_far = [
            lax.dot_general(q2, ref[:, cols], nt, preferred_element_type=f32) for ref in far
        ]
        s_text = lax.dot_general(q2, tk_ref[:, cols], nt, preferred_element_type=f32)
        top = jnp.max(s_near, -1, keepdims=True)
        for s in s_far + [s_text]:
            top = jnp.maximum(top, jnp.max(s, -1, keepdims=True))
        e_near = jnp.exp(s_near - top)
        total = jnp.sum(e_near, -1, keepdims=True)
        p_near = e_near.astype(jnp.bfloat16)
        none = jnp.zeros_like(p_near)
        acc = lax.dot_general(jnp.where(same, p_near, none), fv, nn, preferred_element_type=f32)
        acc += lax.dot_general(jnp.where(same, none, p_near), sv, nn, preferred_element_type=f32)
        for s, ref in zip(s_far, far):
            e = jnp.exp(s - top)
            total += jnp.sum(e, -1, keepdims=True)
            acc += lax.dot_general(
                e.astype(jnp.bfloat16), ref[:, kcols], nn, preferred_element_type=f32
            )
        e = jnp.exp(s_text - top)
        total += jnp.sum(e, -1, keepdims=True)
        acc += lax.dot_general(
            e.astype(jnp.bfloat16), tv_ref[:, cols], nn, preferred_element_type=f32
        )
        acc = acc / total
        out[:, cols] = jnp.where(low, acc[:count], acc[count:]).astype(out.dtype)


def project_kernel(rows, gate_ref, *refs):
    lines = (len(refs) - QUAD) // 2
    att = refs[:lines]
    weights = refs[lines : lines + QUAD]
    outs = refs[lines + QUAD :]
    width = att[0].shape[1]
    nt = (((1,), (1,)), ((), ()))
    index = lax.axis_index("patch")
    line = index // QUAD
    odd = (index & 1) == 1
    high = (index & 2) == 2
    acc = [None] * QUAD
    for k in range(lines):
        a = jnp.concatenate(
            [att[k][(m ^ k) * rows : ((m ^ k) + 1) * rows, :] for m in range(lines)], 0
        )
        span = pl.ds(pl.multiple_of((line ^ k) * width, LANES), width)
        for j in range(QUAD):
            part = lax.dot_general(a, weights[j][:, span], nt, preferred_element_type=jnp.float32)
            acc[j] = part if acc[j] is None else acc[j] + part
    pairs = []
    for j in (0, 2):
        first = jnp.where(odd, acc[j + 1], acc[j])
        second = jnp.where(odd, acc[j], acc[j + 1])
        pairs.append(jnp.concatenate([first, second], 1))
    lower = jnp.where(high, pairs[1], pairs[0])
    upper = jnp.where(high, pairs[0], pairs[1])
    result = (jnp.concatenate([lower, upper], 1) * gate_ref[...]).astype(outs[0].dtype)
    for m in range(lines):
        outs[m][...] = result[m * rows : (m + 1) * rows, :]


def place_kernel(*refs):
    line = lax.axis_index("patch") // QUAD
    parts, out = refs[:-1], refs[-1]
    width = parts[0].shape[1]
    for m, part in enumerate(parts):
        out[:, pl.ds(pl.multiple_of((line ^ m) * width, LANES), width)] = part[...]


def square_body(
    queries,
    fresh_keys,
    fresh_values,
    stale_keys,
    stale_values,
    text_keys,
    text_values,
    out_weight,
    gate_table,
    timestep,
):
    rows, model = queries.shape
    lines = lax.axis_size("patch") // QUAD
    width = model // lines
    out_width = out_weight.shape[1] * QUAD
    count = rows * lines
    text = text_keys.shape[0]
    bf16 = queries.dtype
    vmem = pl.BlockSpec(memory_space=pltpu.VMEM)
    hbm = pl.BlockSpec(memory_space=pltpu.HBM)
    smem = pl.BlockSpec(memory_space=pltpu.SMEM)

    def shaped(*shape, dtype=bf16):
        return jax.ShapeDtypeStruct(shape, dtype)

    def in_hbm(*arrays):
        return [pltpu.with_memory_space_constraint(array, pltpu.HBM) for array in arrays]

    def kernel(body, outs, specs, scratch=(), grant=1):
        return pl.pallas_call(
            body,
            in_specs=specs,
            out_specs=jax.tree.map(lambda _: vmem, outs),
            out_shape=outs,
            scratch_shapes=scratch,
            compiler_params=pltpu.CompilerParams(vmem_limit_bytes=grant * GRANT),
        )

    others = list(reversed(range(1, lines)))
    packed = kernel(
        pack_kernel,
        [shaped(rows, 2 * width)] * lines + [shaped(rows, 3 * width)] * lines,
        [hbm] * 5,
        [pltpu.SemaphoreType.DMA((5 * lines,))],
    )(*in_hbm(queries, fresh_keys, fresh_values, stale_keys, stale_values))
    stale, fresh = list(packed[:lines]), list(packed[lines:])
    for k in others:
        stale[k] = swap(stale[k], QUAD * k)
    for k in others:
        fresh[k] = swap(fresh[k], QUAD * k)
    text_k, text_v, gate = kernel(
        fetch_kernel,
        [shaped(text, width), shaped(text, width), shaped(1, out_width, dtype=jnp.float32)],
        [smem, hbm, hbm, hbm],
        [pltpu.SemaphoreType.DMA((3,))],
    )(timestep, *in_hbm(text_keys, text_values, gate_table))
    line_stale = kernel(join_kernel, shaped(count, 2 * width), [vmem] * lines)(*stale)
    by_y = swap(line_stale, 2)
    by_core = swap(line_stale, 1)
    by_both = swap(by_y, 1)

    columns = out_weight.T
    late_columns, by_y = lax.optimization_barrier((columns, by_y))
    weight_y = swap(late_columns, 2)
    weight_core = swap(columns, 1)
    weight_both = swap(weight_y, 1)

    attended = kernel(
        functools.partial(attend_kernel, rows),
        shaped(count, width),
        [vmem] * (2 * lines + 5),
        grant=2,
    )(text_k, text_v, *fresh, *stale, by_core, by_y, by_both)

    gathered = [attended] * lines
    for k in others:
        gathered[k] = swap(attended, QUAD * k)
    parts = kernel(
        functools.partial(project_kernel, rows),
        [shaped(rows, out_width)] * lines,
        [vmem] * (1 + lines + QUAD),
        grant=2,
    )(gate, *gathered, columns, weight_core, weight_y, weight_both)
    parts = list(parts)
    for k in others:
        parts[k] = swap(parts[k], QUAD * k)
    return kernel(place_kernel, shaped(rows, out_width * lines), [vmem] * lines)(*parts)


def solution(mesh):
    in_specs = (
        P(("groups", "patch"), None),
        P(("groups", "patch"), None),
        P(("groups", "patch"), None),
        P(("groups", "patch"), None),
        P(("groups", "patch"), None),
        P("groups", None),
        P("groups", None),
        P(None, "patch"),
        P(),
        P("groups"),
    )
    out_specs = P(("groups", "patch"), None)
    lines = mesh.shape["patch"] // QUAD

    square = mesh.shape["patch"] == QUAD * lines and lines == QUAD

    def body(queries, *rest):
        if square and (queries.shape[1] // lines) % LANES == 0 and queries.shape[0] % 16 == 0:
            return square_body(queries, *rest)
        return general_body(queries, *rest)

    return jax.shard_map(body, mesh=mesh, in_specs=in_specs, out_specs=out_specs, check_vma=False)
```

profile of v0, /device:TPU:0, one launch (start us, length us, event | category | flops | bytes accessed | tf_op | source)
XLA Modules:
  0.0 69.0 jit_solution(6614135438997434866)
XLA Ops:
  0.0 0.0 copy-start
  0.0 1.2 %shard_map.101 = (bf16[32,768]{1,0:T(8,128)(2,1)S(1)}, bf16[32,768]{1,0:T(8,128)(2,1)S(1)}, bf16[32,768]{1,0:T(8,128)(2,1)S(1)}, bf16[32,768]{1,0:T(8,128)(2,1)S...) custom-call(bf16[32,1536]{1,0:T(8,128)(2,1)} %q_ref.1, ...), custom_call_target="tpu_custom_call" | custom-call | tf_op jit(solution)/shard_map/pallas_call | solution.py:336
  1.2 3.1 %collective-permute-start.3 = (bf16[32,768]{1,0:T(8,128)(2,1)S(1)}, bf16[32,768]{1,0:T(8,128)(2,1)S(1)}, u32[]{:S(2)}, u32[]{:S(2)}) collective-permute-start(bf16[32,768]{1,0:T(8,128)(2,1)S(1)} %get-tuple-element.30), channel_id=1, source_target_pairs={{0,4},{1,5},{2,6},{3,7},{4,0},{5,1},{6,2},{7,3},{8,12},{9,13},{10,... | collective-permute-start | bytes 147464 | tf_op jit(solution)/shard_map/ppermute | solution.py:149
  4.3 2.6 %collective-permute-start.4 = (bf16[32,768]{1,0:T(8,128)(2,1)S(1)}, bf16[32,768]{1,0:T(8,128)(2,1)S(1)}, u32[]{:S(2)}, u32[]{:S(2)}) collective-permute-start(bf16[32,768]{1,0:T(8,128)(2,1)S(1)} %get-tuple-element.31), channel_id=1, source_target_pairs={{0,8},{1,9},{2,10},{3,11},{4,12},{5,13},{6,14},{7,15},{8,0},{9,1},... | collective-permute-start | bytes 147464 | tf_op jit(solution)/shard_map/ppermute | solution.py:149
  6.9 0.0 collective-permute-start.5
  6.9 0.0 collective-permute-done.3.refs_1_.refs_5_
  6.9 3.3 %collective-permute-done.4.refs_2_.refs_6_ = bf16[32,768]{1,0:T(8,128)(2,1)S(1)} collective-permute-done((bf16[32,768]{1,0:T(8,128)(2,1)S(1)}, bf16[32,768]{1,0:T(8,128)(2,1)S(1)}, u32[]{:S(2)}, u32[]{:S(2)}) %collective-permute-start.4) | collective-permute-done | bytes 49184 | tf_op jit(solution)/shard_map/ppermute | solution.py:149
  10.3 2.6 %collective-permute-done.5.refs_3_.refs_7_ = bf16[32,768]{1,0:T(8,128)(2,1)S(1)} collective-permute-done((bf16[32,768]{1,0:T(8,128)(2,1)S(1)}, bf16[32,768]{1,0:T(8,128)(2,1)S(1)}, u32[]{:S(2)}, u32[]{:S(2)}) %collective-permute-start.5) | collective-permute-done | bytes 49184 | tf_op jit(solution)/shard_map/ppermute | solution.py:149
  12.8 1.6 %collective-permute-start.7 = (bf16[128,768]{1,0:T(8,128)(2,1)S(1)}, bf16[128,768]{1,0:T(8,128)(2,1)S(1)}, u32[]{:S(2)}, u32[]{:S(2)}) collective-permute-start(bf16[128,768]{1,0:T(8,128)(2,1)S(1)} %shard_map.102), channel_id=1, source_target_pairs={{0,2},{1,3},{2,0},{3,1},{4,6},{5,7},{6,4},{7,5},{8,10},{9,11},{10,... | collective-permute-start | bytes 589832 | tf_op jit(solution)/shard_map/ppermute | solution.py:149
  14.4 4.5 %collective-permute-done.7.refs_9_ = bf16[128,768]{1,0:T(8,128)(2,1)S(1)} collective-permute-done((bf16[128,768]{1,0:T(8,128)(2,1)S(1)}, bf16[128,768]{1,0:T(8,128)(2,1)S(1)}, u32[]{:S(2)}, u32[]{:S(2)}) %collective-permute-start.7) | collective-permute-done | bytes 196640 | tf_op jit(solution)/shard_map/ppermute | solution.py:149
  18.9 0.0 copy-done
  18.9 1.5 %collective-permute-start.13 = (bf16[192,1536]{1,0:T(8,128)(2,1)S(1)}, bf16[192,1536]{1,0:T(8,128)(2,1)S(1)}, u32[]{:S(2)}, u32[]{:S(2)}) collective-permute-start(bf16[192,1536]{1,0:T(8,128)(2,1)S(1)} %bitcast.1), channel_id=1, source_target_pairs={{0,2},{1,3},{2,0},{3,1},{4,6},{5,7},{6,4},{7,5},{8,10},{9,11},{10,... | collective-permute-start | bytes 1769480 | tf_op jit(solution)/shard_map/ppermute | solution.py:149
  20.4 0.0 collective-permute-start.12
  20.4 10.8 %collective-permute-done.13.refs_6_ = bf16[192,1536]{1,0:T(8,128)(2,1)S(1)} collective-permute-done((bf16[192,1536]{1,0:T(8,128)(2,1)S(1)}, bf16[192,1536]{1,0:T(8,128)(2,1)S(1)}, u32[]{:S(2)}, u32[]{:S(2)}) %collective-permute-start.13) | collective-permute-done | bytes 589856 | tf_op jit(solution)/shard_map/ppermute | solution.py:149
  31.2 0.0 collective-permute-start.14
  31.2 0.0 collective-permute-start
  31.2 0.5 collective-permute-start.6
  31.7 0.0 collective-permute-start.8
  31.7 4.2 %collective-permute-done.refs_1_ = bf16[32,1152]{1,0:T(8,128)(2,1)S(1)} collective-permute-done((bf16[32,1152]{1,0:T(8,128)(2,1)S(1)}, bf16[32,1152]{1,0:T(8,128)(2,1)S(1)}, u32[]{:S(2)}, u32[]{:S(2)}) %collective-permute-start) | collective-permute-done | bytes 73760 | tf_op jit(solution)/shard_map/ppermute | solution.py:149
  35.9 0.4 collective-permute-start.1
  36.2 5.9 %collective-permute-done.1.refs_2_ = bf16[32,1152]{1,0:T(8,128)(2,1)S(1)} collective-permute-done((bf16[32,1152]{1,0:T(8,128)(2,1)S(1)}, bf16[32,1152]{1,0:T(8,128)(2,1)S(1)}, u32[]{:S(2)}, u32[]{:S(2)}) %collective-permute-start.1) | collective-permute-done | bytes 73760 | tf_op jit(solution)/shard_map/ppermute | solution.py:149
  42.2 0.7 %collective-permute-start.2 = (bf16[32,1152]{1,0:T(8,128)(2,1)S(1)}, bf16[32,1152]{1,0:T(8,128)(2,1)S(1)}, u32[]{:S(2)}, u32[]{:S(2)}) collective-permute-start(bf16[32,1152]{1,0:T(8,128)(2,1)S(1)} %get-tuple-element.28), channel_id=1, source_target_pairs={{0,12},{1,13},{2,14},{3,15},{4,8},{5,9},{6,10},{7,11},{8,4},{9,5},... | collective-permute-start | bytes 221192 | tf_op jit(solution)/shard_map/ppermute | solution.py:149
  43.6 1.1 %shard_map.100 = (bf16[226,384]{1,0:T(8,128)(2,1)S(1)}, bf16[226,384]{1,0:T(8,128)(2,1)S(1)}, f32[1,768]{1,0:T(1,128)S(1)}) custom-call(s32[1]{0:T(128)S(6)} %copy.11.step_ref, bf16[226,1536]{1,0:T(8,128)(2,1)} %tk_ref.1, bf16[226,1536]{1,0:T(8,128)(2,1)} %tv_ref.1, f32[50,3072]{1,0:T(8,128)} %gate_ref.1), custom_call_target="tpu_custom_call" | custom-call | tf_op jit(solution)/shard_map/pallas_call | solution.py:347
  44.6 3.8 %collective-permute-done.2.refs_3_ = bf16[32,1152]{1,0:T(8,128)(2,1)S(1)} collective-permute-done((bf16[32,1152]{1,0:T(8,128)(2,1)S(1)}, bf16[32,1152]{1,0:T(8,128)(2,1)S(1)}, u32[]{:S(2)}, u32[]{:S(2)}) %collective-permute-start.2) | collective-permute-done | bytes 73760 | tf_op jit(solution)/shard_map/ppermute | solution.py:149
  48.4 0.0 collective-permute-done.6.refs_8_
  48.4 0.0 collective-permute-done.8.refs_10_
  48.4 1.8 %shard_map.103.refs_0_ = bf16[128,384]{1,0:T(8,128)(2,1)S(1)} custom-call(bf16[226,384]{1,0:T(8,128)(2,1)S(1)} %get-tuple-element.23.tk_ref, bf16[226,384]{1,0:T(8,128)(2,1)S(1)} %get-tuple-element.24.tv_ref, bf16[32,1152]{1,0:T(8,128)(2,1)S(1)} %get-tuple-element.25.refs_0_, bf16[32,1152]{1,0:T(8,128)(2,1)S(1)} %collective-permute-done.refs_1_, ...), custom_call_target="tpu_custom_call" | custom-call | tf_op jit(solution)/shard_map/pallas_call | solution.py:364
  50.2 0.7 %collective-permute-start.11 = (bf16[128,384]{1,0:T(8,128)(2,1)S(1)}, bf16[128,384]{1,0:T(8,128)(2,1)S(1)}, u32[]{:S(2)}, u32[]{:S(2)}) collective-permute-start(bf16[128,384]{1,0:T(8,128)(2,1)S(1)} %shard_map.103.refs_0_), channel_id=1, source_target_pairs={{0,12},{1,13},{2,14},{3,15},{4,8},{5,9},{6,10},{7,11},{8,4},{9,5},... | collective-permute-start | bytes 294920 | tf_op jit(solution)/shard_map/ppermute | solution.py:149
  50.9 0.0 collective-permute-start.10
  50.9 3.7 %collective-permute-start.9 = (bf16[128,384]{1,0:T(8,128)(2,1)S(1)}, bf16[128,384]{1,0:T(8,128)(2,1)S(1)}, u32[]{:S(2)}, u32[]{:S(2)}) collective-permute-start(bf16[128,384]{1,0:T(8,128)(2,1)S(1)} %shard_map.103.refs_0_), channel_id=1, source_target_pairs={{0,4},{1,5},{2,6},{3,7},{4,0},{5,1},{6,2},{7,3},{8,12},{9,13},{10,... | collective-permute-start | bytes 294920 | tf_op jit(solution)/shard_map/ppermute | solution.py:149
  54.7 3.0 %collective-permute-done.11.refs_3_ = bf16[128,384]{1,0:T(8,128)(2,1)S(1)} collective-permute-done((bf16[128,384]{1,0:T(8,128)(2,1)S(1)}, bf16[128,384]{1,0:T(8,128)(2,1)S(1)}, u32[]{:S(2)}, u32[]{:S(2)}) %collective-permute-start.11) | collective-permute-done | bytes 98336 | tf_op jit(solution)/shard_map/ppermute | solution.py:149
  57.6 1.2 %collective-permute-done.10.refs_2_ = bf16[128,384]{1,0:T(8,128)(2,1)S(1)} collective-permute-done((bf16[128,384]{1,0:T(8,128)(2,1)S(1)}, bf16[128,384]{1,0:T(8,128)(2,1)S(1)}, u32[]{:S(2)}, u32[]{:S(2)}) %collective-permute-start.10) | collective-permute-done | bytes 98336 | tf_op jit(solution)/shard_map/ppermute | solution.py:149
  58.8 0.0 collective-permute-done.9.refs_1_
  58.8 0.0 collective-permute-done.12.refs_5_
  58.8 0.0 collective-permute-done.14.refs_7_
  58.8 1.2 %shard_map.104 = (bf16[32,768]{1,0:T(8,128)(2,1)S(1)}, bf16[32,768]{1,0:T(8,128)(2,1)S(1)}, bf16[32,768]{1,0:T(8,128)(2,1)S(1)}, bf16[32,768]{1,0:T(8,128)(2,1)S(1)}) custom-call(f32[1,768]{1,0:T(1,128)S(1)} %get-tuple-element.22.gate_ref, bf16[128,384]{1,0:T(8,128)(2,1)S(1)} %shard_map.103.refs_0_, bf16[128,384]{1,0:T(8,128)(2,1)S(1)} %collective-permute-done.9.refs_1_, ...), custom_call_target="tpu_custom_call" | custom-call | tf_op jit(solution)/shard_map/pallas_call | solution.py:374
  60.0 0.5 collective-permute-start.15
  60.6 1.8 %collective-permute-start.16 = (bf16[32,768]{1,0:T(8,128)(2,1)S(1)}, bf16[32,768]{1,0:T(8,128)(2,1)S(1)}, u32[]{:S(2)}, u32[]{:S(2)}) collective-permute-start(bf16[32,768]{1,0:T(8,128)(2,1)S(1)} %get-tuple-element.37), channel_id=1, source_target_pairs={{0,8},{1,9},{2,10},{3,11},{4,12},{5,13},{6,14},{7,15},{8,0},{9,1},... | collective-permute-start | bytes 147464 | tf_op jit(solution)/shard_map/ppermute | solution.py:149
  62.4 2.1 %collective-permute-start.17 = (bf16[32,768]{1,0:T(8,128)(2,1)S(1)}, bf16[32,768]{1,0:T(8,128)(2,1)S(1)}, u32[]{:S(2)}, u32[]{:S(2)}) collective-permute-start(bf16[32,768]{1,0:T(8,128)(2,1)S(1)} %get-tuple-element.38), channel_id=1, source_target_pairs={{0,12},{1,13},{2,14},{3,15},{4,8},{5,9},{6,10},{7,11},{8,4},{9,5},... | collective-permute-start | bytes 147464 | tf_op jit(solution)/shard_map/ppermute | solution.py:149
  64.5 0.0 collective-permute-done.15.refs_1_
  64.5 1.1 %collective-permute-done.16.refs_2_ = bf16[32,768]{1,0:T(8,128)(2,1)S(1)} collective-permute-done((bf16[32,768]{1,0:T(8,128)(2,1)S(1)}, bf16[32,768]{1,0:T(8,128)(2,1)S(1)}, u32[]{:S(2)}, u32[]{:S(2)}) %collective-permute-start.16) | collective-permute-done | bytes 49184 | tf_op jit(solution)/shard_map/ppermute | solution.py:149
  65.6 2.7 %collective-permute-done.17.refs_3_ = bf16[32,768]{1,0:T(8,128)(2,1)S(1)} collective-permute-done((bf16[32,768]{1,0:T(8,128)(2,1)S(1)}, bf16[32,768]{1,0:T(8,128)(2,1)S(1)}, u32[]{:S(2)}, u32[]{:S(2)}) %collective-permute-start.17) | collective-permute-done | bytes 49184 | tf_op jit(solution)/shard_map/ppermute | solution.py:149
  68.3 0.7 %shard_map.105 = bf16[32,3072]{1,0:T(8,128)(2,1)} custom-call(bf16[32,768]{1,0:T(8,128)(2,1)S(1)} %get-tuple-element.35.refs_0_, bf16[32,768]{1,0:T(8,128)(2,1)S(1)} %collective-permute-done.15.refs_1_, bf16[32,768]{1,0:T(8,128)(2,1)S(1)} %collective-permute-done.16.refs_2_, bf16[32,768]{1,0:T(8,128)(2,1)S(1)} %collective-permute-done.17.refs_3_), custom_call_target="tpu_custom_call" | custom-call | tf_op jit(solution)/shard_map/pallas_call | solution.py:383
  (1 shorter events, 0.0 us)
Async XLA Ops:
  0.0 18.9 %copy-start = (bf16[1536,192]{0,1:T(8,128)(2,1)S(1)}, bf16[1536,192]{0,1:T(8,128)(2,1)}, u32[]{:S(2)}) copy-start(bf16[1536,192]{0,1:T(8,128)(2,1)} %param.17) | copy-start | bytes 1769476
  1.2 5.7 %collective-permute-start.3 = (bf16[32,768]{1,0:T(8,128)(2,1)S(1)}, bf16[32,768]{1,0:T(8,128)(2,1)S(1)}, u32[]{:S(2)}, u32[]{:S(2)}) collective-permute-start(bf16[32,768]{1,0:T(8,128)(2,1)S(1)} %get-tuple-element.30), channel_id=1, source_target_pairs={{0,4},{1,5},{2,6},{3,7},{4,0},{5,1},{6,2},{7,3},{8,12},{9,13},{10,... | collective-permute-start | bytes 147464 | tf_op jit(solution)/shard_map/ppermute | solution.py:149
  4.3 5.9 %collective-permute-start.4 = (bf16[32,768]{1,0:T(8,128)(2,1)S(1)}, bf16[32,768]{1,0:T(8,128)(2,1)S(1)}, u32[]{:S(2)}, u32[]{:S(2)}) collective-permute-start(bf16[32,768]{1,0:T(8,128)(2,1)S(1)} %get-tuple-element.31), channel_id=1, source_target_pairs={{0,8},{1,9},{2,10},{3,11},{4,12},{5,13},{6,14},{7,15},{8,0},{9,1},... | collective-permute-start | bytes 147464 | tf_op jit(solution)/shard_map/ppermute | solution.py:149
  6.9 5.9 %collective-permute-start.5 = (bf16[32,768]{1,0:T(8,128)(2,1)S(1)}, bf16[32,768]{1,0:T(8,128)(2,1)S(1)}, u32[]{:S(2)}, u32[]{:S(2)}) collective-permute-start(bf16[32,768]{1,0:T(8,128)(2,1)S(1)} %get-tuple-element.32), channel_id=1, source_target_pairs={{0,12},{1,13},{2,14},{3,15},{4,8},{5,9},{6,10},{7,11},{8,4},{9,5},... | collective-permute-start | bytes 147464 | tf_op jit(solution)/shard_map/ppermute | solution.py:149
  12.8 6.1 %collective-permute-start.7 = (bf16[128,768]{1,0:T(8,128)(2,1)S(1)}, bf16[128,768]{1,0:T(8,128)(2,1)S(1)}, u32[]{:S(2)}, u32[]{:S(2)}) collective-permute-start(bf16[128,768]{1,0:T(8,128)(2,1)S(1)} %shard_map.102), channel_id=1, source_target_pairs={{0,2},{1,3},{2,0},{3,1},{4,6},{5,7},{6,4},{7,5},{8,10},{9,11},{10,... | collective-permute-start | bytes 589832 | tf_op jit(solution)/shard_map/ppermute | solution.py:149
  18.9 12.3 %collective-permute-start.13 = (bf16[192,1536]{1,0:T(8,128)(2,1)S(1)}, bf16[192,1536]{1,0:T(8,128)(2,1)S(1)}, u32[]{:S(2)}, u32[]{:S(2)}) collective-permute-start(bf16[192,1536]{1,0:T(8,128)(2,1)S(1)} %bitcast.1), channel_id=1, source_target_pairs={{0,2},{1,3},{2,0},{3,1},{4,6},{5,7},{6,4},{7,5},{8,10},{9,11},{10,... | collective-permute-start | bytes 1769480 | tf_op jit(solution)/shard_map/ppermute | solution.py:149
  20.4 38.4 %collective-permute-start.12 = (bf16[192,1536]{1,0:T(8,128)(2,1)S(1)}, bf16[192,1536]{1,0:T(8,128)(2,1)S(1)}, u32[]{:S(2)}, u32[]{:S(2)}) collective-permute-start(bf16[192,1536]{1,0:T(8,128)(2,1)S(1)} %bitcast.2), channel_id=1, source_target_pairs={{0,1},{1,0},{2,3},{3,2},{4,5},{5,4},{6,7},{7,6},{8,9},{9,8},{10,11... | collective-permute-start | bytes 1769480 | tf_op jit(solution)/shard_map/ppermute | solution.py:149
  31.2 27.6 %collective-permute-start.14 = (bf16[192,1536]{1,0:T(8,128)(2,1)S(1)}, bf16[192,1536]{1,0:T(8,128)(2,1)S(1)}, u32[]{:S(2)}, u32[]{:S(2)}) collective-permute-start(bf16[192,1536]{1,0:T(8,128)(2,1)S(1)} %collective-permute-done.13.refs_6_), channel_id=1, source_target_pairs={{0,1},{1,0},{2,3},{3,2},{4,5},{5,4},{6,7},{7,6},{8,9},{9,8},{10,11... | collective-permute-start | bytes 1769480 | tf_op jit(solution)/shard_map/ppermute | solution.py:149
  31.2 4.7 %collective-permute-start = (bf16[32,1152]{1,0:T(8,128)(2,1)S(1)}, bf16[32,1152]{1,0:T(8,128)(2,1)S(1)}, u32[]{:S(2)}, u32[]{:S(2)}) collective-permute-start(bf16[32,1152]{1,0:T(8,128)(2,1)S(1)} %get-tuple-element.26), channel_id=1, source_target_pairs={{0,4},{1,5},{2,6},{3,7},{4,0},{5,1},{6,2},{7,3},{8,12},{9,13},{10,... | collective-permute-start | bytes 221192 | tf_op jit(solution)/shard_map/ppermute | solution.py:149
  31.2 17.2 %collective-permute-start.6 = (bf16[128,768]{1,0:T(8,128)(2,1)S(1)}, bf16[128,768]{1,0:T(8,128)(2,1)S(1)}, u32[]{:S(2)}, u32[]{:S(2)}) collective-permute-start(bf16[128,768]{1,0:T(8,128)(2,1)S(1)} %shard_map.102), channel_id=1, source_target_pairs={{0,1},{1,0},{2,3},{3,2},{4,5},{5,4},{6,7},{7,6},{8,9},{9,8},{10,11... | collective-permute-start | bytes 589832 | tf_op jit(solution)/shard_map/ppermute | solution.py:149
  31.7 16.7 %collective-permute-start.8 = (bf16[128,768]{1,0:T(8,128)(2,1)S(1)}, bf16[128,768]{1,0:T(8,128)(2,1)S(1)}, u32[]{:S(2)}, u32[]{:S(2)}) collective-permute-start(bf16[128,768]{1,0:T(8,128)(2,1)S(1)} %collective-permute-done.7.refs_9_), channel_id=1, source_target_pairs={{0,1},{1,0},{2,3},{3,2},{4,5},{5,4},{6,7},{7,6},{8,9},{9,8},{10,11... | collective-permute-start | bytes 589832 | tf_op jit(solution)/shard_map/ppermute | solution.py:149
  35.9 6.3 %collective-permute-start.1 = (bf16[32,1152]{1,0:T(8,128)(2,1)S(1)}, bf16[32,1152]{1,0:T(8,128)(2,1)S(1)}, u32[]{:S(2)}, u32[]{:S(2)}) collective-permute-start(bf16[32,1152]{1,0:T(8,128)(2,1)S(1)} %get-tuple-element.27), channel_id=1, source_target_pairs={{0,8},{1,9},{2,10},{3,11},{4,12},{5,13},{6,14},{7,15},{8,0},{9,1},... | collective-permute-start | bytes 221192 | tf_op jit(solution)/shard_map/ppermute | solution.py:149
  42.2 6.3 %collective-permute-start.2 = (bf16[32,1152]{1,0:T(8,128)(2,1)S(1)}, bf16[32,1152]{1,0:T(8,128)(2,1)S(1)}, u32[]{:S(2)}, u32[]{:S(2)}) collective-permute-start(bf16[32,1152]{1,0:T(8,128)(2,1)S(1)} %get-tuple-element.28), channel_id=1, source_target_pairs={{0,12},{1,13},{2,14},{3,15},{4,8},{5,9},{6,10},{7,11},{8,4},{9,5},... | collective-permute-start | bytes 221192 | tf_op jit(solution)/shard_map/ppermute | solution.py:149
  50.2 7.4 %collective-permute-start.11 = (bf16[128,384]{1,0:T(8,128)(2,1)S(1)}, bf16[128,384]{1,0:T(8,128)(2,1)S(1)}, u32[]{:S(2)}, u32[]{:S(2)}) collective-permute-start(bf16[128,384]{1,0:T(8,128)(2,1)S(1)} %shard_map.103.refs_0_), channel_id=1, source_target_pairs={{0,12},{1,13},{2,14},{3,15},{4,8},{5,9},{6,10},{7,11},{8,4},{9,5},... | collective-permute-start | bytes 294920 | tf_op jit(solution)/shard_map/ppermute | solution.py:149
  50.9 7.9 %collective-permute-start.10 = (bf16[128,384]{1,0:T(8,128)(2,1)S(1)}, bf16[128,384]{1,0:T(8,128)(2,1)S(1)}, u32[]{:S(2)}, u32[]{:S(2)}) collective-permute-start(bf16[128,384]{1,0:T(8,128)(2,1)S(1)} %shard_map.103.refs_0_), channel_id=1, source_target_pairs={{0,8},{1,9},{2,10},{3,11},{4,12},{5,13},{6,14},{7,15},{8,0},{9,1},... | collective-permute-start | bytes 294920 | tf_op jit(solution)/shard_map/ppermute | solution.py:149
  50.9 7.9 %collective-permute-start.9 = (bf16[128,384]{1,0:T(8,128)(2,1)S(1)}, bf16[128,384]{1,0:T(8,128)(2,1)S(1)}, u32[]{:S(2)}, u32[]{:S(2)}) collective-permute-start(bf16[128,384]{1,0:T(8,128)(2,1)S(1)} %shard_map.103.refs_0_), channel_id=1, source_target_pairs={{0,4},{1,5},{2,6},{3,7},{4,0},{5,1},{6,2},{7,3},{8,12},{9,13},{10,... | collective-permute-start | bytes 294920 | tf_op jit(solution)/shard_map/ppermute | solution.py:149
  60.0 4.5 %collective-permute-start.15 = (bf16[32,768]{1,0:T(8,128)(2,1)S(1)}, bf16[32,768]{1,0:T(8,128)(2,1)S(1)}, u32[]{:S(2)}, u32[]{:S(2)}) collective-permute-start(bf16[32,768]{1,0:T(8,128)(2,1)S(1)} %get-tuple-element.36), channel_id=1, source_target_pairs={{0,4},{1,5},{2,6},{3,7},{4,0},{5,1},{6,2},{7,3},{8,12},{9,13},{10,... | collective-permute-start | bytes 147464 | tf_op jit(solution)/shard_map/ppermute | solution.py:149
  60.6 5.0 %collective-permute-start.16 = (bf16[32,768]{1,0:T(8,128)(2,1)S(1)}, bf16[32,768]{1,0:T(8,128)(2,1)S(1)}, u32[]{:S(2)}, u32[]{:S(2)}) collective-permute-start(bf16[32,768]{1,0:T(8,128)(2,1)S(1)} %get-tuple-element.37), channel_id=1, source_target_pairs={{0,8},{1,9},{2,10},{3,11},{4,12},{5,13},{6,14},{7,15},{8,0},{9,1},... | collective-permute-start | bytes 147464 | tf_op jit(solution)/shard_map/ppermute | solution.py:149
  62.4 5.9 %collective-permute-start.17 = (bf16[32,768]{1,0:T(8,128)(2,1)S(1)}, bf16[32,768]{1,0:T(8,128)(2,1)S(1)}, u32[]{:S(2)}, u32[]{:S(2)}) collective-permute-start(bf16[32,768]{1,0:T(8,128)(2,1)S(1)} %get-tuple-element.38), channel_id=1, source_target_pairs={{0,12},{1,13},{2,14},{3,15},{4,8},{5,9},{6,10},{7,11},{8,4},{9,5},... | collective-permute-start | bytes 147464 | tf_op jit(solution)/shard_map/ppermute | solution.py:149
where the time goes:
time: 69.2 us; the launch traced here: 69 us
  waiting for transfers between devices  43 us (62%)
  starting transfers between devices  19.3 us (28%)
  Pallas kernels  5.94 us (9%)
  between operations  0.71 us (1%)
    ppermute x18, waiting for transfers between devices, swap(): return lax.ppermute(shard, 'patch', [(i, i ^ by) for i in range(peers)])  43 us
    ppermute x18, starting transfers between devices, swap(): return lax.ppermute(shard, 'patch', [(i, i ^ by) for i in range(peers)])  19.3 us
    pallas_call x1, Pallas kernels, square_body(): kernel(functools.partial(attend_kernel, rows), shaped(count, width), [vme...  1.76 us
  transfers between devices with their start and end apart: 18, of which 11 were waited for; matrix products, arithmetic and copies ran while one was open for 0% of the time, Pallas kernels for 4%

commit v1 on v0

--- a/solution.py
+++ b/solution.py
@@ -149,41 +149,46 @@
     return lax.ppermute(shard, "patch", [(i, i ^ by) for i in range(peers)])
 
 
-def pack_kernel(q_ref, fk_ref, fv_ref, sk_ref, sv_ref, *refs):
-    outs, sem = refs[:-1], refs[-1]
+def line_slices(refs, outs, line):
+    width = refs[0].shape[1] // len(outs)
+    copies = []
+    for k in reversed(range(len(outs))):
+        cols = pl.ds(pl.multiple_of((line ^ k) * width, LANES), width)
+        for t, ref in enumerate(refs):
+            copies.append((ref.at[:, cols], outs[k].at[:, t * width : (t + 1) * width]))
+    return copies
+
+
+def pack_kernel(q_ref, fk_ref, fv_ref, sk_ref, sv_ref, w_ref, *refs):
+    outs, w_out, sem = refs[:-2], refs[-2], refs[-1]
     lines = len(outs) // 2
     line = lax.axis_index("patch") // QUAD
-    width = q_ref.shape[1] // lines
-    copies = []
-    for half, sources in ((0, (sk_ref, sv_ref)), (lines, (q_ref, fk_ref, fv_ref))):
-        for k in reversed(range(lines)):
-            cols = pl.ds(pl.multiple_of((line ^ k) * width, LANES), width)
-            for t, source in enumerate(sources):
-                copy = pltpu.make_async_copy(
-                    source.at[:, cols],
-                    outs[half + k].at[:, t * width : (t + 1) * width],
-                    sem.at[len(copies)],
-                )
-                copy.start()
-                copies.append(copy)
+    copies = line_slices((sk_ref, sv_ref), outs[:lines], line)
+    copies += line_slices((q_ref, fk_ref, fv_ref), outs[lines:], line)
+    copies.append((w_ref.at[: w_out.shape[0], :], w_out))
+    run_copies(copies, sem)
+
+
+def run_copies(pairs, sem):
+    copies = [pltpu.make_async_copy(*pair, sem.at[i]) for i, pair in enumerate(pairs)]
+    for copy in copies:
+        copy.start()
     for copy in copies:
         copy.wait()
 
 
-def fetch_kernel(step_ref, tk_ref, tv_ref, gate_ref, tk_out, tv_out, gate_out, sem):
+def fetch_kernel(step_ref, tk_ref, tv_ref, gate_ref, w_ref, tk_out, tv_out, gate_out, w_out, sem):
     width, out_width = tk_out.shape[1], gate_out.shape[1]
     line = lax.axis_index("patch") // QUAD
     cols = pl.ds(pl.multiple_of(line * width, LANES), width)
     gate_cols = pl.ds(pl.multiple_of(line * out_width, LANES), out_width)
     copies = [
-        pltpu.make_async_copy(tk_ref.at[:, cols], tk_out, sem.at[0]),
-        pltpu.make_async_copy(tv_ref.at[:, cols], tv_out, sem.at[1]),
-        pltpu.make_async_copy(gate_ref.at[pl.ds(step_ref[0], 1), gate_cols], gate_out, sem.at[2]),
+        (tk_ref.at[:, cols], tk_out),
+        (tv_ref.at[:, cols], tv_out),
+        (gate_ref.at[pl.ds(step_ref[0], 1), gate_cols], gate_out),
+        (w_ref.at[w_ref.shape[0] - w_out.shape[0] :, :], w_out),
     ]
-    for copy in copies:
-        copy.start()
-    for copy in copies:
-        copy.wait()
+    run_copies(copies, sem)
 
 
 def join_kernel(*refs):
@@ -193,104 +198,126 @@
         out[k * rows : (k + 1) * rows, :] = part[...]
 
 
-def attend_kernel(rows, tk_ref, tv_ref, *refs):
-    lines = (len(refs) - 4) // 2
-    fresh = refs[:lines]
-    own = refs[lines : 2 * lines]
-    far = refs[2 * lines : 2 * lines + 3]
-    out = refs[-1]
-    width = out.shape[1]
+NT = (((1,), (1,)), ((), ()))
+NN = (((1,), (0,)), ((), ()))
+
+
+def dot(a, b, dims):
+    return lax.dot_general(a, b, dims, preferred_element_type=jnp.float32)
+
+
+def head_rows(q):
+    low = lax.broadcasted_iota(jnp.int32, (1, LANES), 1) < HEAD_DIM
+    q = (q.astype(jnp.float32) * HEAD_DIM**-0.5).astype(q.dtype)
+    zero = jnp.zeros_like(q)
+    return jnp.concatenate([jnp.where(low, q, zero), jnp.where(low, zero, q)], 0)
+
+
+def early_kernel(tk_ref, tv_ref, *refs):
+    lines = (len(refs) - 5) // 2
+    fresh, own, core = refs[:lines], refs[lines : 2 * lines], refs[2 * lines]
+    q_out, acc_out, top_out, sum_out = refs[2 * lines + 1 :]
+    rows, width = fresh[0].shape[0], tk_ref.shape[1]
     count = rows * lines
-    nt = (((1,), (1,)), ((), ()))
-    nn = (((1,), (0,)), ((), ()))
-    lane = lax.broadcasted_iota(jnp.int32, (1, LANES), 1)
-    low = lane < HEAD_DIM
     row_block = (lax.broadcasted_iota(jnp.int32, (2 * count, count), 0) % count) // rows
     col_block = lax.broadcasted_iota(jnp.int32, (2 * count, count), 1) // rows
     same = row_block == col_block
-    scaling = HEAD_DIM**-0.5
-    f32 = jnp.float32
+    for pair in range(width // LANES):
+        first = pair * LANES
+        cols, kcols, vcols = (
+            slice(t * width + first, t * width + first + LANES) for t in range(3)
+        )
+        q = head_rows(jnp.concatenate([ref[:, cols] for ref in fresh], 0))
+        fresh_k = jnp.concatenate([ref[:, kcols] for ref in fresh], 0)
+        fresh_v = jnp.concatenate([ref[:, vcols] for ref in fresh], 0)
+        own_k = jnp.concatenate([ref[:, cols] for ref in own], 0)
+        own_v = jnp.concatenate([ref[:, kcols] for ref in own], 0)
+        s_near = jnp.where(same, dot(q, fresh_k, NT), dot(q, own_k, NT))
+        s_core = dot(q, core[:, cols], NT)
+        s_text = dot(q, tk_ref[:, cols], NT)
+        top = jnp.maximum(
+            jnp.max(jnp.maximum(s_near, s_core), -1, keepdims=True),
+            jnp.max(s_text, -1, keepdims=True),
+        )
+        e_near, e_core, e_text = (jnp.exp(s - top) for s in (s_near, s_core, s_text))
+        total = jnp.sum(e_near + e_core, -1, keepdims=True) + jnp.sum(e_text, -1, keepdims=True)
+        p_near = e_near.astype(jnp.bfloat16)
+        none = jnp.zeros_like(p_near)
+        acc = dot(jnp.where(same, p_near, none), fresh_v, NN)
+        acc += dot(jnp.where(same, none, p_near), own_v, NN)
+        acc += dot(e_core.astype(jnp.bfloat16), core[:, kcols], NN)
+        acc += dot(e_text.astype(jnp.bfloat16), tv_ref[:, cols], NN)
+        span = slice(2 * count * pair, 2 * count * (pair + 1))
+        q_out[span, :] = q
+        acc_out[span, :] = acc
+        top_out[span, :] = jnp.broadcast_to(top, acc.shape)
+        sum_out[span, :] = jnp.broadcast_to(total, acc.shape)
+
+
+def attend_kernel(q_ref, acc_ref, top_ref, sum_ref, y_ref, both_ref, out):
+    count, width = out.shape
+    low = lax.broadcasted_iota(jnp.int32, (1, LANES), 1) < HEAD_DIM
     for pair in range(width // LANES):
         cols = slice(pair * LANES, (pair + 1) * LANES)
-        kcols = slice(width + pair * LANES, width + (pair + 1) * LANES)
-        vcols = slice(2 * width + pair * LANES, 2 * width + (pair + 1) * LANES)
-        q = jnp.concatenate([fresh[k][:, cols] for k in range(lines)], 0)
-        q = (q.astype(f32) * scaling).astype(q.dtype)
-        zero = jnp.zeros_like(q)
-        q2 = jnp.concatenate([jnp.where(low, q, zero), jnp.where(low, zero, q)], 0)
-        fk = jnp.concatenate([fresh[k][:, kcols] for k in range(lines)], 0)
-        fv = jnp.concatenate([fresh[k][:, vcols] for k in range(lines)], 0)
-        sk = jnp.concatenate([own[k][:, cols] for k in range(lines)], 0)
-        sv = jnp.concatenate([own[k][:, kcols] for k in range(lines)], 0)
-        s_fresh = lax.dot_general(q2, fk, nt, preferred_element_type=f32)
-        s_own = lax.dot_general(q2, sk, nt, preferred_element_type=f32)
-        s_near = jnp.where(same, s_fresh, s_own)
-        s_far = [
-            lax.dot_general(q2, ref[:, cols], nt, preferred_element_type=f32) for ref in far
-        ]
-        s_text = lax.dot_general(q2, tk_ref[:, cols], nt, preferred_element_type=f32)
-        top = jnp.max(s_near, -1, keepdims=True)
-        for s in s_far + [s_text]:
-            top = jnp.maximum(top, jnp.max(s, -1, keepdims=True))
-        e_near = jnp.exp(s_near - top)
-        total = jnp.sum(e_near, -1, keepdims=True)
-        p_near = e_near.astype(jnp.bfloat16)
-        none = jnp.zeros_like(p_near)
-        acc = lax.dot_general(jnp.where(same, p_near, none), fv, nn, preferred_element_type=f32)
-        acc += lax.dot_general(jnp.where(same, none, p_near), sv, nn, preferred_element_type=f32)
-        for s, ref in zip(s_far, far):
-            e = jnp.exp(s - top)
-            total += jnp.sum(e, -1, keepdims=True)
-            acc += lax.dot_general(
-                e.astype(jnp.bfloat16), ref[:, kcols], nn, preferred_element_type=f32
-            )
-        e = jnp.exp(s_text - top)
-        total += jnp.sum(e, -1, keepdims=True)
-        acc += lax.dot_general(
-            e.astype(jnp.bfloat16), tv_ref[:, cols], nn, preferred_element_type=f32
-        )
+        vcols = slice(width + pair * LANES, width + (pair + 1) * LANES)
+        span = slice(2 * count * pair, 2 * count * (pair + 1))
+        keys = jnp.concatenate([y_ref[:, cols], both_ref[:, cols]], 0)
+        values = jnp.concatenate([y_ref[:, vcols], both_ref[:, vcols]], 0)
+        s = dot(q_ref[span, :], keys, NT)
+        top = jnp.maximum(top_ref[span, :], jnp.max(s, -1, keepdims=True))
+        shrink = jnp.exp(top_ref[span, :] - top)
+        e = jnp.exp(s - jnp.concatenate([top] * (s.shape[1] // LANES), 1))
+        total = sum_ref[span, :] * shrink + jnp.sum(e, -1, keepdims=True)
+        acc = acc_ref[span, :] * shrink + dot(e.astype(jnp.bfloat16), values, NN)
         acc = acc / total
         out[:, cols] = jnp.where(low, acc[:count], acc[count:]).astype(out.dtype)
 
 
-def project_kernel(rows, gate_ref, *refs):
-    lines = (len(refs) - QUAD) // 2
-    att = refs[:lines]
-    weights = refs[lines : lines + QUAD]
-    outs = refs[lines + QUAD :]
-    width = att[0].shape[1]
-    nt = (((1,), (1,)), ((), ()))
+def project_kernel(ks, last, *refs):
+    weights = refs[: QUAD + 2]
+    weights = [weights[:1], weights[1:2], weights[2:4], weights[4:6]]
+    att, refs = refs[QUAD + 2 : QUAD + 2 + len(ks)], refs[QUAD + 2 + len(ks) :]
     index = lax.axis_index("patch")
     line = index // QUAD
+    width = att[0].shape[1]
+    rows = att[0].shape[0] // QUAD
+    before = refs[0] if last else None
+    acc = [before[j] if last else None for j in range(QUAD)]
+    for k, ref in zip(ks, att):
+        a = jnp.concatenate([ref[(m ^ k) * rows : ((m ^ k) + 1) * rows, :] for m in range(QUAD)], 0)
+        span = pl.ds(pl.multiple_of((line ^ k) * width, LANES), width)
+        for j in range(QUAD):
+            weight = jnp.concatenate([part[:, span] for part in weights[j]], 0)
+            part = dot(a, weight, NT)
+            acc[j] = part if acc[j] is None else acc[j] + part
+    if not last:
+        for j in range(QUAD):
+            refs[0][j] = acc[j]
+        return
+    gate_ref, outs = refs[1], refs[2:]
     odd = (index & 1) == 1
     high = (index & 2) == 2
-    acc = [None] * QUAD
-    for k in range(lines):
-        a = jnp.concatenate(
-            [att[k][(m ^ k) * rows : ((m ^ k) + 1) * rows, :] for m in range(lines)], 0
-        )
-        span = pl.ds(pl.multiple_of((line ^ k) * width, LANES), width)
-        for j in range(QUAD):
-            part = lax.dot_general(a, weights[j][:, span], nt, preferred_element_type=jnp.float32)
-            acc[j] = part if acc[j] is None else acc[j] + part
     pairs = []
     for j in (0, 2):
-        first = jnp.where(odd, acc[j + 1], acc[j])
-        second = jnp.where(odd, acc[j], acc[j + 1])
-        pairs.append(jnp.concatenate([first, second], 1))
+        near = jnp.where(odd, acc[j + 1], acc[j])
+        far = jnp.where(odd, acc[j], acc[j + 1])
+        pairs.append(jnp.concatenate([near, far], 1))
     lower = jnp.where(high, pairs[1], pairs[0])
     upper = jnp.where(high, pairs[0], pairs[1])
     result = (jnp.concatenate([lower, upper], 1) * gate_ref[...]).astype(outs[0].dtype)
-    for m in range(lines):
-        outs[m][...] = result[m * rows : (m + 1) * rows, :]
+    for m, out in enumerate(outs):
+        out[...] = result[m * rows : (m + 1) * rows, :]
 
 
 def place_kernel(*refs):
+    parts, out, sem = refs[:-2], refs[-2], refs[-1]
     line = lax.axis_index("patch") // QUAD
-    parts, out = refs[:-1], refs[-1]
     width = parts[0].shape[1]
+    copies = []
     for m, part in enumerate(parts):
-        out[:, pl.ds(pl.multiple_of((line ^ m) * width, LANES), width)] = part[...]
+        cols = pl.ds(pl.multiple_of((line ^ m) * width, LANES), width)
+        copies.append((part, out.at[:, cols]))
+    run_copies(copies, sem)
 
 
 def square_body(
@@ -332,55 +359,75 @@
             compiler_params=pltpu.CompilerParams(vmem_limit_bytes=grant * GRANT),
         )
 
+    columns = out_weight.T
+    half = columns.shape[0] // 2
     others = list(reversed(range(1, lines)))
-    packed = kernel(
+    *packed, early = kernel(
         pack_kernel,
-        [shaped(rows, 2 * width)] * lines + [shaped(rows, 3 * width)] * lines,
-        [hbm] * 5,
-        [pltpu.SemaphoreType.DMA((5 * lines,))],
-    )(*in_hbm(queries, fresh_keys, fresh_values, stale_keys, stale_values))
-    stale, fresh = list(packed[:lines]), list(packed[lines:])
+        [shaped(rows, 2 * width)] * lines
+        + [shaped(rows, 3 * width)] * lines
+        + [shaped(half, model)],
+        [hbm] * 6,
+        [pltpu.SemaphoreType.DMA((5 * lines + 1,))],
+    )(*in_hbm(queries, fresh_keys, fresh_values, stale_keys, stale_values, columns))
+    stale, fresh = packed[:lines], packed[lines:]
     for k in others:
         stale[k] = swap(stale[k], QUAD * k)
     for k in others:
         fresh[k] = swap(fresh[k], QUAD * k)
-    text_k, text_v, gate = kernel(
+    text_k, text_v, gate, late = kernel(
         fetch_kernel,
-        [shaped(text, width), shaped(text, width), shaped(1, out_width, dtype=jnp.float32)],
-        [smem, hbm, hbm, hbm],
-        [pltpu.SemaphoreType.DMA((3,))],
-    )(timestep, *in_hbm(text_keys, text_values, gate_table))
+        [shaped(text, width)] * 2
+        + [shaped(1, out_width, dtype=jnp.float32), shaped(half, model)],
+        [smem] + [hbm] * 4,
+        [pltpu.SemaphoreType.DMA((4,))],
+    )(timestep, *in_hbm(text_keys, text_values, gate_table, columns))
     line_stale = kernel(join_kernel, shaped(count, 2 * width), [vmem] * lines)(*stale)
     by_y = swap(line_stale, 2)
     by_core = swap(line_stale, 1)
     by_both = swap(by_y, 1)
 
-    columns = out_weight.T
-    late_columns, by_y = lax.optimization_barrier((columns, by_y))
-    weight_y = swap(late_columns, 2)
+    weight_y = [swap(early, 2), swap(late, 2)]
     weight_core = swap(columns, 1)
-    weight_both = swap(weight_y, 1)
-
-    attended = kernel(
-        functools.partial(attend_kernel, rows),
-        shaped(count, width),
-        [vmem] * (2 * lines + 5),
-        grant=2,
-    )(text_k, text_v, *fresh, *stale, by_core, by_y, by_both)
+    weight_both = [swap(weight_y[0], 1), swap(weight_y[1], 1)]
+
+    stacked = 2 * count * (width // LANES)
+    early_part = kernel(
+        early_kernel,
+        [shaped(stacked, LANES)] + [shaped(stacked, LANES, dtype=jnp.float32)] * 3,
+        [vmem] * (2 * lines + 3),
+    )(text_k, text_v, *fresh, *stale, by_core)
+    attended = kernel(attend_kernel, shaped(count, width), [vmem] * 6)(*early_part, by_y, by_both)
 
     gathered = [attended] * lines
     for k in others:
         gathered[k] = swap(attended, QUAD * k)
+    weights = [columns, weight_core, *weight_y, *weight_both]
+    near_lines, far_lines = tuple(range(lines // 2)), tuple(range(lines // 2, lines))
+    sums = kernel(
+        functools.partial(project_kernel, near_lines, False),
+        shaped(QUAD, count, out_weight.shape[1], dtype=jnp.float32),
+        [vmem] * (QUAD + 2 + len(near_lines)),
+        grant=2,
+    )(*weights, *[gathered[k] for k in near_lines])
     parts = kernel(
-        functools.partial(project_kernel, rows),
+        functools.partial(project_kernel, far_lines, True),
         [shaped(rows, out_width)] * lines,
-        [vmem] * (1 + lines + QUAD),
+        [vmem] * (QUAD + 4 + len(far_lines)),
         grant=2,
-    )(gate, *gathered, columns, weight_core, weight_y, weight_both)
+    )(*weights, *[gathered[k] for k in far_lines], sums, gate)
     parts = list(parts)
     for k in others:
         parts[k] = swap(parts[k], QUAD * k)
-    return kernel(place_kernel, shaped(rows, out_width * lines), [vmem] * lines)(*parts)
+    return pl.pallas_call(
+        place_kernel,
+        in_specs=[vmem] * lines,
+        out_specs=hbm,
+        out_shape=shaped(rows, out_width * lines),
+        scratch_shapes=[pltpu.SemaphoreType.DMA((lines,))],
+        compiler_params=pltpu.CompilerParams(vmem_limit_bytes=GRANT),
+        name="place",
+    )(*parts)
 
 
 def solution(mesh):

time: 69.2 us -> 55 us (0.79)
  waiting for transfers between devices: 43 us -> 23.2 us
  starting transfers between devices: 19.3 us -> 24 us
  Pallas kernels: 5.94 us -> 6.9 us
    ppermute x18 -> x20, waiting for transfers between devices: 43 us -> 23.2 us  [swap(): return lax.ppermute(shard, 'patch', [(i, i ^ by) for i in range(peers)])]
    ppermute x18 -> x20, starting transfers between devices: 19.3 us -> 24 us  [swap(): return lax.ppermute(shard, 'patch', [(i, i ^ by) for i in range(peers)])]
    pallas_call x4 -> x6, Pallas kernels: 4.72 us -> 5.5 us  [the longest x1 1.46 us: square_body(): kernel(early_kernel, [shaped(stacked, LANES)] + [shaped(stacked, LANES, d...]
  transfers between devices with their start and end apart: 18 -> 20, of which waited for: 11 -> 9; matrix products, arithmetic and copies ran while one was open for 0% -> 0% of each run, Pallas kernels for 4% -> 7%
where the time goes in v1:
time: 55 us; the launch traced here: 54.8 us
  starting transfers between devices  24 us (44%)
  waiting for transfers between devices  23.2 us (42%)
  Pallas kernels  6.9 us (13%)
  between operations  0.76 us (1%)
    ppermute x20, starting transfers between devices, swap(): return lax.ppermute(shard, 'patch', [(i, i ^ by) for i in range(peers)])  24 us
    ppermute x20, waiting for transfers between devices, swap(): return lax.ppermute(shard, 'patch', [(i, i ^ by) for i in range(peers)])  23.2 us
    pallas_call x1, Pallas kernels, square_body(): kernel(early_kernel, [shaped(stacked, LANES)] + [shaped(stacked, LANES, d...  1.46 us
    pallas_call x1, Pallas kernels, square_body(): kernel(pack_kernel, [shaped(rows, 2 * width)] * lines + [shaped(rows, 3 *...  1.39 us
    pallas_call x1, Pallas kernels, square_body(): kernel(fetch_kernel, [shaped(text, width)] * 2 + [shaped(1, out_width, dt...  1.19 us
  transfers between devices with their start and end apart: 20, of which 9 were waited for; matrix products, arithmetic and copies ran while one was open for 0% of the time, Pallas kernels for 7%

profile of v1, /device:TPU:0, one launch (start us, length us, event | category | flops | bytes accessed | tf_op | source)
XLA Modules:
  0.0 54.8 jit_solution(5231224916828499843)
XLA Ops:
  0.0 1.4 %shard_map.100 = (bf16[32,768]{1,0:T(8,128)(2,1)S(1)}, bf16[32,768]{1,0:T(8,128)(2,1)S(1)}, bf16[32,768]{1,0:T(8,128)(2,1)S(1)}, bf16[32,768]{1,0:T(8,128)(2,1)S...) custom-call(bf16[32,1536]{1,0:T(8,128)(2,1)} %q_ref.1, ...), custom_call_target="tpu_custom_call" | custom-call | tf_op jit(solution)/shard_map/pallas_call | solution.py:365
  1.4 5.1 %collective-permute-start.10 = (bf16[32,768]{1,0:T(8,128)(2,1)S(1)}, bf16[32,768]{1,0:T(8,128)(2,1)S(1)}, u32[]{:S(2)}, u32[]{:S(2)}) collective-permute-start(bf16[32,768]{1,0:T(8,128)(2,1)S(1)} %get-tuple-element.37), channel_id=1, source_target_pairs={{0,12},{1,13},{2,14},{3,15},{4,8},{5,9},{6,10},{7,11},{8,4},{9,5},... | collective-permute-start | bytes 147464 | tf_op jit(solution)/shard_map/ppermute | solution.py:149
  6.5 0.0 collective-permute-start.8
  6.5 0.6 %collective-permute-start.9 = (bf16[32,768]{1,0:T(8,128)(2,1)S(1)}, bf16[32,768]{1,0:T(8,128)(2,1)S(1)}, u32[]{:S(2)}, u32[]{:S(2)}) collective-permute-start(bf16[32,768]{1,0:T(8,128)(2,1)S(1)} %get-tuple-element.36), channel_id=1, source_target_pairs={{0,8},{1,9},{2,10},{3,11},{4,12},{5,13},{6,14},{7,15},{8,0},{9,1},... | collective-permute-start | bytes 147464 | tf_op jit(solution)/shard_map/ppermute | solution.py:149
  7.2 1.4 %collective-permute-start.5 = (bf16[32,1152]{1,0:T(8,128)(2,1)S(1)}, bf16[32,1152]{1,0:T(8,128)(2,1)S(1)}, u32[]{:S(2)}, u32[]{:S(2)}) collective-permute-start(bf16[32,1152]{1,0:T(8,128)(2,1)S(1)} %get-tuple-element.31), channel_id=1, source_target_pairs={{0,4},{1,5},{2,6},{3,7},{4,0},{5,1},{6,2},{7,3},{8,12},{9,13},{10,... | collective-permute-start | bytes 221192 | tf_op jit(solution)/shard_map/ppermute | solution.py:149
  8.6 1.5 %collective-permute-start.1 = (bf16[96,1536]{1,0:T(8,128)(2,1)S(1)}, bf16[96,1536]{1,0:T(8,128)(2,1)S(1)}, u32[]{:S(2)}, u32[]{:S(2)}) collective-permute-start(bf16[96,1536]{1,0:T(8,128)(2,1)S(1)} %get-tuple-element.26), channel_id=1, source_target_pairs={{0,2},{1,3},{2,0},{3,1},{4,6},{5,7},{6,4},{7,5},{8,10},{9,11},{10,... | collective-permute-start | bytes 884744 | tf_op jit(solution)/shard_map/ppermute | solution.py:149
  10.7 0.0 collective-permute-done.10.refs_3_.refs_7_
  10.8 0.4 collective-permute-done.8.refs_1_.refs_5_
  11.2 0.7 %collective-permute-done.9.refs_2_.refs_6_ = bf16[32,768]{1,0:T(8,128)(2,1)S(1)} collective-permute-done((bf16[32,768]{1,0:T(8,128)(2,1)S(1)}, bf16[32,768]{1,0:T(8,128)(2,1)S(1)}, u32[]{:S(2)}, u32[]{:S(2)}) %collective-permute-start.9) | collective-permute-done | bytes 49184 | tf_op jit(solution)/shard_map/ppermute | solution.py:149
  11.9 0.0 copy-start
  12.0 1.6 %collective-permute-start.12 = (bf16[128,768]{1,0:T(8,128)(2,1)S(1)}, bf16[128,768]{1,0:T(8,128)(2,1)S(1)}, u32[]{:S(2)}, u32[]{:S(2)}) collective-permute-start(bf16[128,768]{1,0:T(8,128)(2,1)S(1)} %shard_map.102), channel_id=1, source_target_pairs={{0,2},{1,3},{2,0},{3,1},{4,6},{5,7},{6,4},{7,5},{8,10},{9,11},{10,... | collective-permute-start | bytes 589832 | tf_op jit(solution)/shard_map/ppermute | solution.py:149
  13.5 1.2 %shard_map.101 = (bf16[226,384]{1,0:T(8,128)(2,1)S(1)}, bf16[226,384]{1,0:T(8,128)(2,1)S(1)}, f32[1,768]{1,0:T(1,128)S(1)}, bf16[96,1536]{1,0:T(8,128)(2,1)S(1)}) custom-call(s32[1]{0:T(128)S(6)} %copy.11.step_ref, bf16[226,1536]{1,0:T(8,128)(2,1)} %tk_ref.1, bf16[226,1536]{1,0:T(8,128)(2,1)} %tv_ref.1, f32[50,3072]{1,0:T(8,128)} %gate_ref.1, ...), custom_call_target="tpu_custom_call" | custom-call | tf_op jit(solution)/shard_map/pallas_call | solution.py:378
  14.7 0.6 %collective-permute-start.2 = (bf16[96,1536]{1,0:T(8,128)(2,1)S(1)}, bf16[96,1536]{1,0:T(8,128)(2,1)S(1)}, u32[]{:S(2)}, u32[]{:S(2)}) collective-permute-start(bf16[96,1536]{1,0:T(8,128)(2,1)S(1)} %get-tuple-element.27), channel_id=1, source_target_pairs={{0,2},{1,3},{2,0},{3,1},{4,6},{5,7},{6,4},{7,5},{8,10},{9,11},{10,... | collective-permute-start | bytes 884744 | tf_op jit(solution)/shard_map/ppermute | solution.py:149
  15.3 0.0 copy-done
  15.3 0.0 collective-permute-start
  15.3 0.0 collective-permute-done.5.refs_1_
  15.3 2.0 %collective-permute-start.6 = (bf16[32,1152]{1,0:T(8,128)(2,1)S(1)}, bf16[32,1152]{1,0:T(8,128)(2,1)S(1)}, u32[]{:S(2)}, u32[]{:S(2)}) collective-permute-start(bf16[32,1152]{1,0:T(8,128)(2,1)S(1)} %get-tuple-element.32), channel_id=1, source_target_pairs={{0,8},{1,9},{2,10},{3,11},{4,12},{5,13},{6,14},{7,15},{8,0},{9,1},... | collective-permute-start | bytes 221192 | tf_op jit(solution)/shard_map/ppermute | solution.py:149
  17.3 5.2 %collective-permute-done.6.refs_2_ = bf16[32,1152]{1,0:T(8,128)(2,1)S(1)} collective-permute-done((bf16[32,1152]{1,0:T(8,128)(2,1)S(1)}, bf16[32,1152]{1,0:T(8,128)(2,1)S(1)}, u32[]{:S(2)}, u32[]{:S(2)}) %collective-permute-start.6) | collective-permute-done | bytes 73760 | tf_op jit(solution)/shard_map/ppermute | solution.py:149
  22.5 1.5 %collective-permute-start.7 = (bf16[32,1152]{1,0:T(8,128)(2,1)S(1)}, bf16[32,1152]{1,0:T(8,128)(2,1)S(1)}, u32[]{:S(2)}, u32[]{:S(2)}) collective-permute-start(bf16[32,1152]{1,0:T(8,128)(2,1)S(1)} %get-tuple-element.33), channel_id=1, source_target_pairs={{0,12},{1,13},{2,14},{3,15},{4,8},{5,9},{6,10},{7,11},{8,4},{9,5},... | collective-permute-start | bytes 221192 | tf_op jit(solution)/shard_map/ppermute | solution.py:149
  24.0 4.7 %collective-permute-done.7.refs_3_ = bf16[32,1152]{1,0:T(8,128)(2,1)S(1)} collective-permute-done((bf16[32,1152]{1,0:T(8,128)(2,1)S(1)}, bf16[32,1152]{1,0:T(8,128)(2,1)S(1)}, u32[]{:S(2)}, u32[]{:S(2)}) %collective-permute-start.7) | collective-permute-done | bytes 73760 | tf_op jit(solution)/shard_map/ppermute | solution.py:149
  28.6 0.0 collective-permute-start.11
  28.6 0.0 collective-permute-done.12.y_ref
  28.6 0.5 collective-permute-start.13
  29.1 0.0 collective-permute-done.1.refs_2_
  29.2 0.1 collective-permute-start.3
  29.2 0.0 collective-permute-done.2.refs_3_
  29.2 0.4 collective-permute-start.4
  29.7 0.4 collective-permute-done.11.refs_8_
  30.1 1.5 %shard_map.103 = (bf16[768,128]{1,0:T(8,128)(2,1)S(1)}, f32[768,128]{1,0:T(8,128)S(1)}, f32[768,128]{1,0:T(8,128)S(1)}, f32[768,128]{1,0:T(8,128)S(1)}) custom-call(bf16[226,384]{1,0:T(8,128)(2,1)S(1)} %get-tuple-element.28.tk_ref, bf16[226,384]{1,0:T(8,128)(2,1)S(1)} %get-tuple-element.29.tv_ref, bf16[32,1152]{1,0:T(8,128)(2,1)S(1)} %get-tuple-element.30.refs_0_, ...), custom_call_target="tpu_custom_call" | custom-call | tf_op jit(solution)/shard_map/pallas_call | solution.py:395
  31.5 0.0 collective-permute-done.13.both_ref
  31.5 0.8 %shard_map.104.refs_6_ = bf16[128,384]{1,0:T(8,128)(2,1)S(1)} custom-call(bf16[768,128]{1,0:T(8,128)(2,1)S(1)} %get-tuple-element.38.q_ref, f32[768,128]{1,0:T(8,128)S(1)} %get-tuple-element.39.acc_ref, f32[768,128]{1,0:T(8,128)S(1)} %get-tuple-element.40.top_ref, f32[768,128]{1,0:T(8,128)S(1)} %get-tuple-element.41.sum_ref, ...), custom_call_target="tpu_custom_call" | custom-call | tf_op jit(solution)/shard_map/pallas_call | solution.py:400
  32.3 0.1 collective-permute-start.16
  32.4 2.0 %collective-permute-start.14 = (bf16[128,384]{1,0:T(8,128)(2,1)S(1)}, bf16[128,384]{1,0:T(8,128)(2,1)S(1)}, u32[]{:S(2)}, u32[]{:S(2)}) collective-permute-start(bf16[128,384]{1,0:T(8,128)(2,1)S(1)} %shard_map.104.refs_6_), channel_id=1, source_target_pairs={{0,8},{1,9},{2,10},{3,11},{4,12},{5,13},{6,14},{7,15},{8,0},{9,1},... | collective-permute-start | bytes 294920 | tf_op jit(solution)/shard_map/ppermute | solution.py:149
  34.4 4.0 %collective-permute-done.16.refs_7_ = bf16[128,384]{1,0:T(8,128)(2,1)S(1)} collective-permute-done((bf16[128,384]{1,0:T(8,128)(2,1)S(1)}, bf16[128,384]{1,0:T(8,128)(2,1)S(1)}, u32[]{:S(2)}, u32[]{:S(2)}) %collective-permute-start.16) | collective-permute-done | bytes 98336 | tf_op jit(solution)/shard_map/ppermute | solution.py:149
  38.4 2.1 %collective-permute-start.15 = (bf16[128,384]{1,0:T(8,128)(2,1)S(1)}, bf16[128,384]{1,0:T(8,128)(2,1)S(1)}, u32[]{:S(2)}, u32[]{:S(2)}) collective-permute-start(bf16[128,384]{1,0:T(8,128)(2,1)S(1)} %shard_map.104.refs_6_), channel_id=1, source_target_pairs={{0,12},{1,13},{2,14},{3,15},{4,8},{5,9},{6,10},{7,11},{8,4},{9,5},... | collective-permute-start | bytes 294920 | tf_op jit(solution)/shard_map/ppermute | solution.py:149
  40.5 0.0 collective-permute-done.3.refs_4_
  40.5 0.0 collective-permute-done.4.refs_5_
  40.5 0.0 collective-permute-done.refs_1_
  40.5 0.7 %shard_map.105.refs_8_ = f32[4,128,192]{2,1,0:T(8,128)S(1)} custom-call(bf16[192,1536]{1,0:T(8,128)(2,1)S(1)} %bitcast.4, bf16[192,1536]{1,0:T(8,128)(2,1)S(1)} %collective-permute-done.refs_1_, bf16[96,1536]{1,0:T(8,128)(2,1)S(1)} %collective-permute-done.1.refs_2_, bf16[96,1536]{1,0:T(8,128)(2,1)S(1)} %collective-permute-done.2.refs_3_, ...), custom_call_target="tpu_custom_call" | custom-call | tf_op jit(solution)/shard_map/pallas_call | solution.py:407
  41.2 0.0 collective-permute-done.14.refs_6_
  41.2 3.6 %collective-permute-done.15.refs_7_ = bf16[128,384]{1,0:T(8,128)(2,1)S(1)} collective-permute-done((bf16[128,384]{1,0:T(8,128)(2,1)S(1)}, bf16[128,384]{1,0:T(8,128)(2,1)S(1)}, u32[]{:S(2)}, u32[]{:S(2)}) %collective-permute-start.15) | collective-permute-done | bytes 98336 | tf_op jit(solution)/shard_map/ppermute | solution.py:149
  44.8 0.7 %shard_map.106 = (bf16[32,768]{1,0:T(8,128)(2,1)S(1)}, bf16[32,768]{1,0:T(8,128)(2,1)S(1)}, bf16[32,768]{1,0:T(8,128)(2,1)S(1)}, bf16[32,768]{1,0:T(8,128)(2,1)S(1)}) custom-call(bf16[192,1536]{1,0:T(8,128)(2,1)S(1)} %bitcast.5, bf16[192,1536]{1,0:T(8,128)(2,1)S(1)} %collective-permute-done.refs_1_, bf16[96,1536]{1,0:T(8,128)(2,1)S(1)} %collective-permute-done.1.refs_2_, ...), custom_call_target="tpu_custom_call" | custom-call | tf_op jit(solution)/shard_map/pallas_call | solution.py:413
  45.5 0.1 collective-permute-start.17
  45.6 2.7 %collective-permute-start.18 = (bf16[32,768]{1,0:T(8,128)(2,1)S(1)}, bf16[32,768]{1,0:T(8,128)(2,1)S(1)}, u32[]{:S(2)}, u32[]{:S(2)}) collective-permute-start(bf16[32,768]{1,0:T(8,128)(2,1)S(1)} %get-tuple-element.45), channel_id=1, source_target_pairs={{0,8},{1,9},{2,10},{3,11},{4,12},{5,13},{6,14},{7,15},{8,0},{9,1},... | collective-permute-start | bytes 147464 | tf_op jit(solution)/shard_map/ppermute | solution.py:149
  48.3 1.7 %collective-permute-start.19 = (bf16[32,768]{1,0:T(8,128)(2,1)S(1)}, bf16[32,768]{1,0:T(8,128)(2,1)S(1)}, u32[]{:S(2)}, u32[]{:S(2)}) collective-permute-start(bf16[32,768]{1,0:T(8,128)(2,1)S(1)} %get-tuple-element.46), channel_id=1, source_target_pairs={{0,12},{1,13},{2,14},{3,15},{4,8},{5,9},{6,10},{7,11},{8,4},{9,5},... | collective-permute-start | bytes 147464 | tf_op jit(solution)/shard_map/ppermute | solution.py:149
  50.0 0.0 collective-permute-done.17.refs_1_
  50.0 1.0 %collective-permute-done.18.refs_2_ = bf16[32,768]{1,0:T(8,128)(2,1)S(1)} collective-permute-done((bf16[32,768]{1,0:T(8,128)(2,1)S(1)}, bf16[32,768]{1,0:T(8,128)(2,1)S(1)}, u32[]{:S(2)}, u32[]{:S(2)}) %collective-permute-start.18) | collective-permute-done | bytes 49184 | tf_op jit(solution)/shard_map/ppermute | solution.py:149
  51.0 3.2 %collective-permute-done.19.refs_3_ = bf16[32,768]{1,0:T(8,128)(2,1)S(1)} collective-permute-done((bf16[32,768]{1,0:T(8,128)(2,1)S(1)}, bf16[32,768]{1,0:T(8,128)(2,1)S(1)}, u32[]{:S(2)}, u32[]{:S(2)}) %collective-permute-start.19) | collective-permute-done | bytes 49184 | tf_op jit(solution)/shard_map/ppermute | solution.py:149
  54.1 0.7 %place.1 = bf16[32,3072]{1,0:T(8,128)(2,1)} custom-call(bf16[32,768]{1,0:T(8,128)(2,1)S(1)} %get-tuple-element.43.refs_0_, bf16[32,768]{1,0:T(8,128)(2,1)S(1)} %collective-permute-done.17.refs_1_, bf16[32,768]{1,0:T(8,128)(2,1)S(1)} %collective-permute-done.18.refs_2_, bf16[32,768]{1,0:T(8,128)(2,1)S(1)} %collective-permute-done.19.refs_3_), custom_call_target="tpu_custom_call" | custom-call | tf_op jit(solution)/shard_map/place/pallas_call | solution.py:422
  (1 shorter events, 0.0 us)
Async XLA Ops:
  1.4 9.3 %collective-permute-start.10 = (bf16[32,768]{1,0:T(8,128)(2,1)S(1)}, bf16[32,768]{1,0:T(8,128)(2,1)S(1)}, u32[]{:S(2)}, u32[]{:S(2)}) collective-permute-start(bf16[32,768]{1,0:T(8,128)(2,1)S(1)} %get-tuple-element.37), channel_id=1, source_target_pairs={{0,12},{1,13},{2,14},{3,15},{4,8},{5,9},{6,10},{7,11},{8,4},{9,5},... | collective-permute-start | bytes 147464 | tf_op jit(solution)/shard_map/ppermute | solution.py:149
  6.5 4.7 %collective-permute-start.8 = (bf16[32,768]{1,0:T(8,128)(2,1)S(1)}, bf16[32,768]{1,0:T(8,128)(2,1)S(1)}, u32[]{:S(2)}, u32[]{:S(2)}) collective-permute-start(bf16[32,768]{1,0:T(8,128)(2,1)S(1)} %get-tuple-element.35), channel_id=1, source_target_pairs={{0,4},{1,5},{2,6},{3,7},{4,0},{5,1},{6,2},{7,3},{8,12},{9,13},{10,... | collective-permute-start | bytes 147464 | tf_op jit(solution)/shard_map/ppermute | solution.py:149
  6.5 5.4 %collective-permute-start.9 = (bf16[32,768]{1,0:T(8,128)(2,1)S(1)}, bf16[32,768]{1,0:T(8,128)(2,1)S(1)}, u32[]{:S(2)}, u32[]{:S(2)}) collective-permute-start(bf16[32,768]{1,0:T(8,128)(2,1)S(1)} %get-tuple-element.36), channel_id=1, source_target_pairs={{0,8},{1,9},{2,10},{3,11},{4,12},{5,13},{6,14},{7,15},{8,0},{9,1},... | collective-permute-start | bytes 147464 | tf_op jit(solution)/shard_map/ppermute | solution.py:149
  7.2 8.1 %collective-permute-start.5 = (bf16[32,1152]{1,0:T(8,128)(2,1)S(1)}, bf16[32,1152]{1,0:T(8,128)(2,1)S(1)}, u32[]{:S(2)}, u32[]{:S(2)}) collective-permute-start(bf16[32,1152]{1,0:T(8,128)(2,1)S(1)} %get-tuple-element.31), channel_id=1, source_target_pairs={{0,4},{1,5},{2,6},{3,7},{4,0},{5,1},{6,2},{7,3},{8,12},{9,13},{10,... | collective-permute-start | bytes 221192 | tf_op jit(solution)/shard_map/ppermute | solution.py:149
  8.6 20.6 %collective-permute-start.1 = (bf16[96,1536]{1,0:T(8,128)(2,1)S(1)}, bf16[96,1536]{1,0:T(8,128)(2,1)S(1)}, u32[]{:S(2)}, u32[]{:S(2)}) collective-permute-start(bf16[96,1536]{1,0:T(8,128)(2,1)S(1)} %get-tuple-element.26), channel_id=1, source_target_pairs={{0,2},{1,3},{2,0},{3,1},{4,6},{5,7},{6,4},{7,5},{8,10},{9,11},{10,... | collective-permute-start | bytes 884744 | tf_op jit(solution)/shard_map/ppermute | solution.py:149
  11.9 3.4 %copy-start = (bf16[1536,192]{0,1:T(8,128)(2,1)S(1)}, bf16[1536,192]{0,1:T(8,128)(2,1)}, u32[]{:S(2)}) copy-start(bf16[1536,192]{0,1:T(8,128)(2,1)} %param.17) | copy-start | bytes 1769476
  12.0 16.7 %collective-permute-start.12 = (bf16[128,768]{1,0:T(8,128)(2,1)S(1)}, bf16[128,768]{1,0:T(8,128)(2,1)S(1)}, u32[]{:S(2)}, u32[]{:S(2)}) collective-permute-start(bf16[128,768]{1,0:T(8,128)(2,1)S(1)} %shard_map.102), channel_id=1, source_target_pairs={{0,2},{1,3},{2,0},{3,1},{4,6},{5,7},{6,4},{7,5},{8,10},{9,11},{10,... | collective-permute-start | bytes 589832 | tf_op jit(solution)/shard_map/ppermute | solution.py:149
  14.7 14.5 %collective-permute-start.2 = (bf16[96,1536]{1,0:T(8,128)(2,1)S(1)}, bf16[96,1536]{1,0:T(8,128)(2,1)S(1)}, u32[]{:S(2)}, u32[]{:S(2)}) collective-permute-start(bf16[96,1536]{1,0:T(8,128)(2,1)S(1)} %get-tuple-element.27), channel_id=1, source_target_pairs={{0,2},{1,3},{2,0},{3,1},{4,6},{5,7},{6,4},{7,5},{8,10},{9,11},{10,... | collective-permute-start | bytes 884744 | tf_op jit(solution)/shard_map/ppermute | solution.py:149
  15.3 25.2 %collective-permute-start = (bf16[192,1536]{1,0:T(8,128)(2,1)S(1)}, bf16[192,1536]{1,0:T(8,128)(2,1)S(1)}, u32[]{:S(2)}, u32[]{:S(2)}) collective-permute-start(bf16[192,1536]{1,0:T(8,128)(2,1)S(1)} %bitcast.3), channel_id=1, source_target_pairs={{0,1},{1,0},{2,3},{3,2},{4,5},{5,4},{6,7},{7,6},{8,9},{9,8},{10,11... | collective-permute-start | bytes 1769480 | tf_op jit(solution)/shard_map/ppermute | solution.py:149
  15.3 7.2 %collective-permute-start.6 = (bf16[32,1152]{1,0:T(8,128)(2,1)S(1)}, bf16[32,1152]{1,0:T(8,128)(2,1)S(1)}, u32[]{:S(2)}, u32[]{:S(2)}) collective-permute-start(bf16[32,1152]{1,0:T(8,128)(2,1)S(1)} %get-tuple-element.32), channel_id=1, source_target_pairs={{0,8},{1,9},{2,10},{3,11},{4,12},{5,13},{6,14},{7,15},{8,0},{9,1},... | collective-permute-start | bytes 221192 | tf_op jit(solution)/shard_map/ppermute | solution.py:149
  22.5 6.2 %collective-permute-start.7 = (bf16[32,1152]{1,0:T(8,128)(2,1)S(1)}, bf16[32,1152]{1,0:T(8,128)(2,1)S(1)}, u32[]{:S(2)}, u32[]{:S(2)}) collective-permute-start(bf16[32,1152]{1,0:T(8,128)(2,1)S(1)} %get-tuple-element.33), channel_id=1, source_target_pairs={{0,12},{1,13},{2,14},{3,15},{4,8},{5,9},{6,10},{7,11},{8,4},{9,5},... | collective-permute-start | bytes 221192 | tf_op jit(solution)/shard_map/ppermute | solution.py:149
  28.6 1.4 %collective-permute-start.11 = (bf16[128,768]{1,0:T(8,128)(2,1)S(1)}, bf16[128,768]{1,0:T(8,128)(2,1)S(1)}, u32[]{:S(2)}, u32[]{:S(2)}) collective-permute-start(bf16[128,768]{1,0:T(8,128)(2,1)S(1)} %shard_map.102), channel_id=1, source_target_pairs={{0,1},{1,0},{2,3},{3,2},{4,5},{5,4},{6,7},{7,6},{8,9},{9,8},{10,11... | collective-permute-start | bytes 589832 | tf_op jit(solution)/shard_map/ppermute | solution.py:149
  28.6 2.9 %collective-permute-start.13 = (bf16[128,768]{1,0:T(8,128)(2,1)S(1)}, bf16[128,768]{1,0:T(8,128)(2,1)S(1)}, u32[]{:S(2)}, u32[]{:S(2)}) collective-permute-start(bf16[128,768]{1,0:T(8,128)(2,1)S(1)} %collective-permute-done.12.y_ref), channel_id=1, source_target_pairs={{0,1},{1,0},{2,3},{3,2},{4,5},{5,4},{6,7},{7,6},{8,9},{9,8},{10,11... | collective-permute-start | bytes 589832 | tf_op jit(solution)/shard_map/ppermute | solution.py:149
  29.2 11.3 %collective-permute-start.3 = (bf16[96,1536]{1,0:T(8,128)(2,1)S(1)}, bf16[96,1536]{1,0:T(8,128)(2,1)S(1)}, u32[]{:S(2)}, u32[]{:S(2)}) collective-permute-start(bf16[96,1536]{1,0:T(8,128)(2,1)S(1)} %collective-permute-done.1.refs_2_), channel_id=1, source_target_pairs={{0,1},{1,0},{2,3},{3,2},{4,5},{5,4},{6,7},{7,6},{8,9},{9,8},{10,11... | collective-permute-start | bytes 884744 | tf_op jit(solution)/shard_map/ppermute | solution.py:149
  29.2 11.3 %collective-permute-start.4 = (bf16[96,1536]{1,0:T(8,128)(2,1)S(1)}, bf16[96,1536]{1,0:T(8,128)(2,1)S(1)}, u32[]{:S(2)}, u32[]{:S(2)}) collective-permute-start(bf16[96,1536]{1,0:T(8,128)(2,1)S(1)} %collective-permute-done.2.refs_3_), channel_id=1, source_target_pairs={{0,1},{1,0},{2,3},{3,2},{4,5},{5,4},{6,7},{7,6},{8,9},{9,8},{10,11... | collective-permute-start | bytes 884744 | tf_op jit(solution)/shard_map/ppermute | solution.py:149
  32.3 6.1 %collective-permute-start.16 = (bf16[128,384]{1,0:T(8,128)(2,1)S(1)}, bf16[128,384]{1,0:T(8,128)(2,1)S(1)}, u32[]{:S(2)}, u32[]{:S(2)}) collective-permute-start(bf16[128,384]{1,0:T(8,128)(2,1)S(1)} %shard_map.104.refs_6_), channel_id=1, source_target_pairs={{0,4},{1,5},{2,6},{3,7},{4,0},{5,1},{6,2},{7,3},{8,12},{9,13},{10,... | collective-permute-start | bytes 294920 | tf_op jit(solution)/shard_map/ppermute | solution.py:149
  32.4 8.8 %collective-permute-start.14 = (bf16[128,384]{1,0:T(8,128)(2,1)S(1)}, bf16[128,384]{1,0:T(8,128)(2,1)S(1)}, u32[]{:S(2)}, u32[]{:S(2)}) collective-permute-start(bf16[128,384]{1,0:T(8,128)(2,1)S(1)} %shard_map.104.refs_6_), channel_id=1, source_target_pairs={{0,8},{1,9},{2,10},{3,11},{4,12},{5,13},{6,14},{7,15},{8,0},{9,1},... | collective-permute-start | bytes 294920 | tf_op jit(solution)/shard_map/ppermute | solution.py:149
  38.4 6.4 %collective-permute-start.15 = (bf16[128,384]{1,0:T(8,128)(2,1)S(1)}, bf16[128,384]{1,0:T(8,128)(2,1)S(1)}, u32[]{:S(2)}, u32[]{:S(2)}) collective-permute-start(bf16[128,384]{1,0:T(8,128)(2,1)S(1)} %shard_map.104.refs_6_), channel_id=1, source_target_pairs={{0,12},{1,13},{2,14},{3,15},{4,8},{5,9},{6,10},{7,11},{8,4},{9,5},... | collective-permute-start | bytes 294920 | tf_op jit(solution)/shard_map/ppermute | solution.py:149
  45.5 4.5 %collective-permute-start.17 = (bf16[32,768]{1,0:T(8,128)(2,1)S(1)}, bf16[32,768]{1,0:T(8,128)(2,1)S(1)}, u32[]{:S(2)}, u32[]{:S(2)}) collective-permute-start(bf16[32,768]{1,0:T(8,128)(2,1)S(1)} %get-tuple-element.44), channel_id=1, source_target_pairs={{0,4},{1,5},{2,6},{3,7},{4,0},{5,1},{6,2},{7,3},{8,12},{9,13},{10,... | collective-permute-start | bytes 147464 | tf_op jit(solution)/shard_map/ppermute | solution.py:149
  45.6 5.4 %collective-permute-start.18 = (bf16[32,768]{1,0:T(8,128)(2,1)S(1)}, bf16[32,768]{1,0:T(8,128)(2,1)S(1)}, u32[]{:S(2)}, u32[]{:S(2)}) collective-permute-start(bf16[32,768]{1,0:T(8,128)(2,1)S(1)} %get-tuple-element.45), channel_id=1, source_target_pairs={{0,8},{1,9},{2,10},{3,11},{4,12},{5,13},{6,14},{7,15},{8,0},{9,1},... | collective-permute-start | bytes 147464 | tf_op jit(solution)/shard_map/ppermute | solution.py:149
  48.3 5.9 %collective-permute-start.19 = (bf16[32,768]{1,0:T(8,128)(2,1)S(1)}, bf16[32,768]{1,0:T(8,128)(2,1)S(1)}, u32[]{:S(2)}, u32[]{:S(2)}) collective-permute-start(bf16[32,768]{1,0:T(8,128)(2,1)S(1)} %get-tuple-element.46), channel_id=1, source_target_pairs={{0,12},{1,13},{2,14},{3,15},{4,8},{5,9},{6,10},{7,11},{8,4},{9,5},... | collective-permute-start | bytes 147464 | tf_op jit(solution)/shard_map/ppermute | solution.py:149

commit v2 on v1

--- a/solution.py
+++ b/solution.py
@@ -254,8 +254,10 @@
         sum_out[span, :] = jnp.broadcast_to(total, acc.shape)
 
 
-def attend_kernel(q_ref, acc_ref, top_ref, sum_ref, y_ref, both_ref, out):
-    count, width = out.shape
+def attend_kernel(q_ref, acc_ref, top_ref, sum_ref, y_ref, both_ref, *outs):
+    count, width = outs[0].shape
+    lines = (len(outs) + 1) // 2
+    rows = count // lines
     low = lax.broadcasted_iota(jnp.int32, (1, LANES), 1) < HEAD_DIM
     for pair in range(width // LANES):
         cols = slice(pair * LANES, (pair + 1) * LANES)
@@ -270,21 +272,37 @@
         total = sum_ref[span, :] * shrink + jnp.sum(e, -1, keepdims=True)
         acc = acc_ref[span, :] * shrink + dot(e.astype(jnp.bfloat16), values, NN)
         acc = acc / total
-        out[:, cols] = jnp.where(low, acc[:count], acc[count:]).astype(out.dtype)
-
-
-def project_kernel(ks, last, *refs):
-    weights = refs[: QUAD + 2]
+        both = jnp.where(low, acc[:count], acc[count:]).astype(outs[0].dtype)
+        outs[0][:, cols] = both
+        for k in range(1, lines):
+            outs[k][: k * rows, cols] = both[: k * rows]
+            if k < lines - 1:
+                outs[k][k * rows :, cols] = both[(k + 1) * rows :]
+            outs[lines + k - 1][:, cols] = both[k * rows : (k + 1) * rows]
+
+
+def project_kernel(ks, own_rows, first, last, *refs):
+    weights, refs = refs[: QUAD + 2], refs[QUAD + 2 :]
     weights = [weights[:1], weights[1:2], weights[2:4], weights[4:6]]
-    att, refs = refs[QUAD + 2 : QUAD + 2 + len(ks)], refs[QUAD + 2 + len(ks) :]
+    att, refs = refs[: len(ks)], refs[len(ks) :]
     index = lax.axis_index("patch")
     line = index // QUAD
+    acc = [None] * QUAD
+    if not first:
+        acc, refs = [refs[0][j] for j in range(QUAD)], refs[1:]
     width = att[0].shape[1]
-    rows = att[0].shape[0] // QUAD
-    before = refs[0] if last else None
-    acc = [before[j] if last else None for j in range(QUAD)]
+
+    def block(ref, i, rows):
+        return ref[i * rows : (i + 1) * rows, :]
+
     for k, ref in zip(ks, att):
-        a = jnp.concatenate([ref[(m ^ k) * rows : ((m ^ k) + 1) * rows, :] for m in range(QUAD)], 0)
+        if own_rows:
+            a = block(ref, 0, ref.shape[0] // QUAD) if k == 0 else ref[...]
+        elif k == 0:
+            a = ref[ref.shape[0] // QUAD :, :]
+        else:
+            spots = [(m ^ k) - ((m ^ k) > k) for m in range(1, QUAD)]
+            a = jnp.concatenate([block(ref, i, ref.shape[0] // len(spots)) for i in spots], 0)
         span = pl.ds(pl.multiple_of((line ^ k) * width, LANES), width)
         for j in range(QUAD):
             weight = jnp.concatenate([part[:, span] for part in weights[j]], 0)
@@ -294,7 +312,7 @@
         for j in range(QUAD):
             refs[0][j] = acc[j]
         return
-    gate_ref, outs = refs[1], refs[2:]
+    gate_ref, outs = refs[0], refs[1:]
     odd = (index & 1) == 1
     high = (index & 2) == 2
     pairs = []
@@ -306,7 +324,7 @@
     upper = jnp.where(high, pairs[0], pairs[1])
     result = (jnp.concatenate([lower, upper], 1) * gate_ref[...]).astype(outs[0].dtype)
     for m, out in enumerate(outs):
-        out[...] = result[m * rows : (m + 1) * rows, :]
+        out[...] = block(result, m, out.shape[0])
 
 
 def place_kernel(*refs):
@@ -397,28 +415,38 @@
         [shaped(stacked, LANES)] + [shaped(stacked, LANES, dtype=jnp.float32)] * 3,
         [vmem] * (2 * lines + 3),
     )(text_k, text_v, *fresh, *stale, by_core)
-    attended = kernel(attend_kernel, shaped(count, width), [vmem] * 6)(*early_part, by_y, by_both)
-
-    gathered = [attended] * lines
+    attended, *blocks = kernel(
+        attend_kernel,
+        [shaped(count, width)]
+        + [shaped(count - rows, width)] * (lines - 1)
+        + [shaped(rows, width)] * (lines - 1),
+        [vmem] * 6,
+    )(*early_part, by_y, by_both)
+    theirs, mine = [attended, *blocks[: lines - 1]], [attended, *blocks[lines - 1 :]]
     for k in others:
-        gathered[k] = swap(attended, QUAD * k)
+        theirs[k] = swap(theirs[k], QUAD * k)
+    for k in others:
+        mine[k] = swap(mine[k], QUAD * k)
     weights = [columns, weight_core, *weight_y, *weight_both]
-    near_lines, far_lines = tuple(range(lines // 2)), tuple(range(lines // 2, lines))
-    sums = kernel(
-        functools.partial(project_kernel, near_lines, False),
-        shaped(QUAD, count, out_weight.shape[1], dtype=jnp.float32),
-        [vmem] * (QUAD + 2 + len(near_lines)),
-        grant=2,
-    )(*weights, *[gathered[k] for k in near_lines])
-    parts = kernel(
-        functools.partial(project_kernel, far_lines, True),
-        [shaped(rows, out_width)] * lines,
-        [vmem] * (QUAD + 4 + len(far_lines)),
-        grant=2,
-    )(*weights, *[gathered[k] for k in far_lines], sums, gate)
-    parts = list(parts)
+
+    def project(ks, own_rows, attended, before, outs):
+        first, last = before is None, isinstance(outs, list)
+        more = ([] if first else [before]) + ([gate] if last else [])
+        return kernel(
+            functools.partial(project_kernel, ks, own_rows, first, last),
+            outs,
+            [vmem] * (len(weights) + len(ks) + len(more)),
+            grant=2,
+        )(*weights, *[attended[k] for k in ks], *more)
+
+    near, far, every = (0, 1), tuple(range(2, lines)), tuple(range(lines))
+    sums = shaped(QUAD, count - rows, out_weight.shape[1], dtype=jnp.float32)
+    made = shaped(rows, out_width)
+    sums = project(near, False, theirs, None, sums)
+    parts = [None, *project(far, False, theirs, sums, [made] * (lines - 1))]
     for k in others:
         parts[k] = swap(parts[k], QUAD * k)
+    parts[0] = project(every, True, mine, None, [made])[0]
     return pl.pallas_call(
         place_kernel,
         in_specs=[vmem] * lines,

time: 55 us -> 58 us (1.055)
  starting transfers between devices: 24 us -> 34.9 us
  waiting for transfers between devices: 23.2 us -> 14.1 us
  Pallas kernels: 6.9 us -> 8.09 us
    ppermute x20 -> x23, starting transfers between devices: 24 us -> 34.9 us  [swap(): return lax.ppermute(shard, 'patch', [(i, i ^ by) for i in range(peers)])]
    ppermute x20 -> x23, waiting for transfers between devices: 23.2 us -> 14.1 us  [swap(): return lax.ppermute(shard, 'patch', [(i, i ^ by) for i in range(peers)])]
    pallas_call x3 -> x4, Pallas kernels: 2.14 us -> 3.26 us  [the longest x3 2.47 us: project(): kernel(functools.partial(project_kernel, ks, own_rows, first, last), outs...]
  transfers between devices with their start and end apart: 20 -> 23, of which waited for: 9 -> 8; matrix products, arithmetic and copies ran while one was open for 0% -> 0% of each run, Pallas kernels for 7% -> 10%
where the time goes in v2:
time: 58 us; the launch traced here: 57.9 us
  starting transfers between devices  34.9 us (60%)
  waiting for transfers between devices  14.1 us (24%)
  Pallas kernels  8.09 us (14%)
  between operations  0.8 us (1%)
    ppermute x23, starting transfers between devices, swap(): return lax.ppermute(shard, 'patch', [(i, i ^ by) for i in range(peers)])  34.9 us
    ppermute x23, waiting for transfers between devices, swap(): return lax.ppermute(shard, 'patch', [(i, i ^ by) for i in range(peers)])  14.1 us
    pallas_call x3, Pallas kernels, project(): kernel(functools.partial(project_kernel, ks, own_rows, first, last), outs...  2.47 us
    pallas_call x1, Pallas kernels, square_body(): kernel(early_kernel, [shaped(stacked, LANES)] + [shaped(stacked, LANES, d...  1.45 us
    pallas_call x1, Pallas kernels, square_body(): kernel(pack_kernel, [shaped(rows, 2 * width)] * lines + [shaped(rows, 3 *...  1.39 us
    pallas_call x1, Pallas kernels, square_body(): kernel(fetch_kernel, [shaped(text, width)] * 2 + [shaped(1, out_width, dt...  1.26 us
  transfers between devices with their start and end apart: 23, of which 8 were waited for; matrix products, arithmetic and copies ran while one was open for 0% of the time, Pallas kernels for 10%

profile of v2, /device:TPU:0, one launch (start us, length us, event | category | flops | bytes accessed | tf_op | source)
XLA Modules:
  0.0 57.9 jit_solution(13296864265962540907)
XLA Ops:
  0.0 1.4 %shard_map.100 = (bf16[32,768]{1,0:T(8,128)(2,1)S(1)}, bf16[32,768]{1,0:T(8,128)(2,1)S(1)}, bf16[32,768]{1,0:T(8,128)(2,1)S(1)}, bf16[32,768]{1,0:T(8,128)(2,1)S...) custom-call(bf16[32,1536]{1,0:T(8,128)(2,1)} %q_ref.1, ...), custom_call_target="tpu_custom_call" | custom-call | tf_op jit(solution)/shard_map/pallas_call | solution.py:383
  1.4 5.1 %collective-permute-start.10 = (bf16[32,768]{1,0:T(8,128)(2,1)S(1)}, bf16[32,768]{1,0:T(8,128)(2,1)S(1)}, u32[]{:S(2)}, u32[]{:S(2)}) collective-permute-start(bf16[32,768]{1,0:T(8,128)(2,1)S(1)} %get-tuple-element.43), channel_id=1, source_target_pairs={{0,12},{1,13},{2,14},{3,15},{4,8},{5,9},{6,10},{7,11},{8,4},{9,5},... | collective-permute-start | bytes 147464 | tf_op jit(solution)/shard_map/ppermute | solution.py:149
  6.5 0.0 collective-permute-start.8
  6.5 0.6 %collective-permute-start.9 = (bf16[32,768]{1,0:T(8,128)(2,1)S(1)}, bf16[32,768]{1,0:T(8,128)(2,1)S(1)}, u32[]{:S(2)}, u32[]{:S(2)}) collective-permute-start(bf16[32,768]{1,0:T(8,128)(2,1)S(1)} %get-tuple-element.42), channel_id=1, source_target_pairs={{0,8},{1,9},{2,10},{3,11},{4,12},{5,13},{6,14},{7,15},{8,0},{9,1},... | collective-permute-start | bytes 147464 | tf_op jit(solution)/shard_map/ppermute | solution.py:149
  7.2 1.7 %collective-permute-start.1 = (bf16[96,1536]{1,0:T(8,128)(2,1)S(1)}, bf16[96,1536]{1,0:T(8,128)(2,1)S(1)}, u32[]{:S(2)}, u32[]{:S(2)}) collective-permute-start(bf16[96,1536]{1,0:T(8,128)(2,1)S(1)} %get-tuple-element.32), channel_id=1, source_target_pairs={{0,2},{1,3},{2,0},{3,1},{4,6},{5,7},{6,4},{7,5},{8,10},{9,11},{10,... | collective-permute-start | bytes 884744 | tf_op jit(solution)/shard_map/ppermute | solution.py:149
  9.5 0.0 copy-start
  9.5 1.3 %shard_map.101 = (bf16[226,384]{1,0:T(8,128)(2,1)S(1)}, bf16[226,384]{1,0:T(8,128)(2,1)S(1)}, f32[1,768]{1,0:T(1,128)S(1)}, bf16[96,1536]{1,0:T(8,128)(2,1)S(1)}) custom-call(s32[1]{0:T(128)S(6)} %copy.11.step_ref, bf16[226,1536]{1,0:T(8,128)(2,1)} %tk_ref.1, bf16[226,1536]{1,0:T(8,128)(2,1)} %tv_ref.1, f32[50,3072]{1,0:T(8,128)} %gate_ref.1, ...), custom_call_target="tpu_custom_call" | custom-call | tf_op jit(solution)/shard_map/pallas_call | solution.py:396
  10.8 0.4 collective-permute-start.2
  11.2 0.0 collective-permute-done.10.refs_3_.refs_7_
  11.2 0.0 copy-done
  11.2 0.0 collective-permute-start
  11.2 0.0 collective-permute-done.8.refs_1_.refs_5_
  11.2 1.5 %collective-permute-start.5 = (bf16[32,1152]{1,0:T(8,128)(2,1)S(1)}, bf16[32,1152]{1,0:T(8,128)(2,1)S(1)}, u32[]{:S(2)}, u32[]{:S(2)}) collective-permute-start(bf16[32,1152]{1,0:T(8,128)(2,1)S(1)} %get-tuple-element.37), channel_id=1, source_target_pairs={{0,4},{1,5},{2,6},{3,7},{4,0},{5,1},{6,2},{7,3},{8,12},{9,13},{10,... | collective-permute-start | bytes 221192 | tf_op jit(solution)/shard_map/ppermute | solution.py:149
  12.7 0.0 collective-permute-done.9.refs_2_.refs_6_
  12.7 1.6 %collective-permute-start.12 = (bf16[128,768]{1,0:T(8,128)(2,1)S(1)}, bf16[128,768]{1,0:T(8,128)(2,1)S(1)}, u32[]{:S(2)}, u32[]{:S(2)}) collective-permute-start(bf16[128,768]{1,0:T(8,128)(2,1)S(1)} %shard_map.102), channel_id=1, source_target_pairs={{0,2},{1,3},{2,0},{3,1},{4,6},{5,7},{6,4},{7,5},{8,10},{9,11},{10,... | collective-permute-start | bytes 589832 | tf_op jit(solution)/shard_map/ppermute | solution.py:149
  14.3 1.6 %collective-permute-done.5.refs_1_ = bf16[32,1152]{1,0:T(8,128)(2,1)S(1)} collective-permute-done((bf16[32,1152]{1,0:T(8,128)(2,1)S(1)}, bf16[32,1152]{1,0:T(8,128)(2,1)S(1)}, u32[]{:S(2)}, u32[]{:S(2)}) %collective-permute-start.5) | collective-permute-done | bytes 73760 | tf_op jit(solution)/shard_map/ppermute | solution.py:149
  15.9 2.6 %collective-permute-start.6 = (bf16[32,1152]{1,0:T(8,128)(2,1)S(1)}, bf16[32,1152]{1,0:T(8,128)(2,1)S(1)}, u32[]{:S(2)}, u32[]{:S(2)}) collective-permute-start(bf16[32,1152]{1,0:T(8,128)(2,1)S(1)} %get-tuple-element.38), channel_id=1, source_target_pairs={{0,8},{1,9},{2,10},{3,11},{4,12},{5,13},{6,14},{7,15},{8,0},{9,1},... | collective-permute-start | bytes 221192 | tf_op jit(solution)/shard_map/ppermute | solution.py:149
  18.5 4.0 %collective-permute-done.6.refs_2_ = bf16[32,1152]{1,0:T(8,128)(2,1)S(1)} collective-permute-done((bf16[32,1152]{1,0:T(8,128)(2,1)S(1)}, bf16[32,1152]{1,0:T(8,128)(2,1)S(1)}, u32[]{:S(2)}, u32[]{:S(2)}) %collective-permute-start.6) | collective-permute-done | bytes 73760 | tf_op jit(solution)/shard_map/ppermute | solution.py:149
  22.4 3.4 %collective-permute-start.7 = (bf16[32,1152]{1,0:T(8,128)(2,1)S(1)}, bf16[32,1152]{1,0:T(8,128)(2,1)S(1)}, u32[]{:S(2)}, u32[]{:S(2)}) collective-permute-start(bf16[32,1152]{1,0:T(8,128)(2,1)S(1)} %get-tuple-element.39), channel_id=1, source_target_pairs={{0,12},{1,13},{2,14},{3,15},{4,8},{5,9},{6,10},{7,11},{8,4},{9,5},... | collective-permute-start | bytes 221192 | tf_op jit(solution)/shard_map/ppermute | solution.py:149
  25.9 2.7 %collective-permute-done.7.refs_3_ = bf16[32,1152]{1,0:T(8,128)(2,1)S(1)} collective-permute-done((bf16[32,1152]{1,0:T(8,128)(2,1)S(1)}, bf16[32,1152]{1,0:T(8,128)(2,1)S(1)}, u32[]{:S(2)}, u32[]{:S(2)}) %collective-permute-start.7) | collective-permute-done | bytes 73760 | tf_op jit(solution)/shard_map/ppermute | solution.py:149
  28.6 0.0 collective-permute-start.11
  28.6 0.0 collective-permute-done.12.y_ref
  28.6 0.5 collective-permute-start.13
  29.1 0.0 collective-permute-done.1.refs_2_
  29.1 0.1 collective-permute-start.3
  29.2 0.0 collective-permute-done.2.refs_3_
  29.2 0.4 collective-permute-start.4
  29.6 0.4 collective-permute-done.11.refs_8_
  30.0 1.5 %shard_map.103 = (bf16[768,128]{1,0:T(8,128)(2,1)S(1)}, f32[768,128]{1,0:T(8,128)S(1)}, f32[768,128]{1,0:T(8,128)S(1)}, f32[768,128]{1,0:T(8,128)S(1)}) custom-call(bf16[226,384]{1,0:T(8,128)(2,1)S(1)} %get-tuple-element.34.tk_ref, bf16[226,384]{1,0:T(8,128)(2,1)S(1)} %get-tuple-element.35.tv_ref, bf16[32,1152]{1,0:T(8,128)(2,1)S(1)} %get-tuple-element.36.refs_0_, ...), custom_call_target="tpu_custom_call" | custom-call | tf_op jit(solution)/shard_map/pallas_call | solution.py:413
  31.5 0.0 collective-permute-done.13.both_ref
  31.5 0.8 %shard_map.104 = (bf16[128,384]{1,0:T(8,128)(2,1)S(1)}, bf16[96,384]{1,0:T(8,128)(2,1)S(1)}, bf16[96,384]{1,0:T(8,128)(2,1)S(1)}, bf16[96,384]{1,0:T(8,128)(2,1)...) custom-call(bf16[768,128]{1,0:T(8,128)(2,1)S(1)} %get-tuple-element.44.q_ref, ...), custom_call_target="tpu_custom_call" | custom-call | tf_op jit(solution)/shard_map/pallas_call | solution.py:418
  32.3 0.1 collective-permute-start.19
  32.4 4.0 %collective-permute-start.17 = (bf16[96,384]{1,0:T(8,128)(2,1)S(1)}, bf16[96,384]{1,0:T(8,128)(2,1)S(1)}, u32[]{:S(2)}, u32[]{:S(2)}) collective-permute-start(bf16[96,384]{1,0:T(8,128)(2,1)S(1)} %get-tuple-element.53), channel_id=1, source_target_pairs={{0,8},{1,9},{2,10},{3,11},{4,12},{5,13},{6,14},{7,15},{8,0},{9,1},... | collective-permute-start | bytes 221192 | tf_op jit(solution)/shard_map/ppermute | solution.py:149
  36.4 0.4 collective-permute-done.19.refs_7_
  36.7 4.6 %collective-permute-start.18 = (bf16[96,384]{1,0:T(8,128)(2,1)S(1)}, bf16[96,384]{1,0:T(8,128)(2,1)S(1)}, u32[]{:S(2)}, u32[]{:S(2)}) collective-permute-start(bf16[96,384]{1,0:T(8,128)(2,1)S(1)} %get-tuple-element.54), channel_id=1, source_target_pairs={{0,12},{1,13},{2,14},{3,15},{4,8},{5,9},{6,10},{7,11},{8,4},{9,5},... | collective-permute-start | bytes 221192 | tf_op jit(solution)/shard_map/ppermute | solution.py:149
  41.3 0.0 collective-permute-done.3.refs_4_
  41.3 0.0 collective-permute-start.14
  41.3 0.0 collective-permute-done.4.refs_5_
  41.3 0.0 collective-permute-done.refs_1_
  41.3 0.6 %shard_map.106.refs_8_ = f32[4,96,192]{2,1,0:T(8,128)S(1)} custom-call(bf16[192,1536]{1,0:T(8,128)(2,1)S(1)} %bitcast.4, bf16[192,1536]{1,0:T(8,128)(2,1)S(1)} %collective-permute-done.refs_1_, bf16[96,1536]{1,0:T(8,128)(2,1)S(1)} %collective-permute-done.1.refs_2_, bf16[96,1536]{1,0:T(8,128)(2,1)S(1)} %collective-permute-done.2.refs_3_, ...), custom_call_target="tpu_custom_call" | custom-call | tf_op jit(solution)/shard_map/pallas_call | solution.py:435
  42.0 0.0 collective-permute-done.17.refs_6_
  42.0 1.7 %collective-permute-done.18.refs_7_ = bf16[96,384]{1,0:T(8,128)(2,1)S(1)} collective-permute-done((bf16[96,384]{1,0:T(8,128)(2,1)S(1)}, bf16[96,384]{1,0:T(8,128)(2,1)S(1)}, u32[]{:S(2)}, u32[]{:S(2)}) %collective-permute-start.18) | collective-permute-done | bytes 73760 | tf_op jit(solution)/shard_map/ppermute | solution.py:149
  43.6 0.7 %shard_map.107 = (bf16[32,768]{1,0:T(8,128)(2,1)S(1)}, bf16[32,768]{1,0:T(8,128)(2,1)S(1)}, bf16[32,768]{1,0:T(8,128)(2,1)S(1)}) custom-call(bf16[192,1536]{1,0:T(8,128)(2,1)S(1)} %bitcast.5, bf16[192,1536]{1,0:T(8,128)(2,1)S(1)} %collective-permute-done.refs_1_, bf16[96,1536]{1,0:T(8,128)(2,1)S(1)} %collective-permute-done.1.refs_2_, ...), custom_call_target="tpu_custom_call" | custom-call | tf_op jit(solution)/shard_map/pallas_call | solution.py:435
  44.4 0.4 collective-permute-start.20
  44.8 4.0 %collective-permute-start.21 = (bf16[32,768]{1,0:T(8,128)(2,1)S(1)}, bf16[32,768]{1,0:T(8,128)(2,1)S(1)}, u32[]{:S(2)}, u32[]{:S(2)}) collective-permute-start(bf16[32,768]{1,0:T(8,128)(2,1)S(1)} %get-tuple-element.57), channel_id=1, source_target_pairs={{0,8},{1,9},{2,10},{3,11},{4,12},{5,13},{6,14},{7,15},{8,0},{9,1},... | collective-permute-start | bytes 147464 | tf_op jit(solution)/shard_map/ppermute | solution.py:149
  48.8 0.0 collective-permute-start.22
  48.8 1.5 %collective-permute-start.15 = (bf16[32,384]{1,0:T(8,128)(2,1)S(1)}, bf16[32,384]{1,0:T(8,128)(2,1)S(1)}, u32[]{:S(2)}, u32[]{:S(2)}) collective-permute-start(bf16[32,384]{1,0:T(8,128)(2,1)S(1)} %get-tuple-element.50), channel_id=1, source_target_pairs={{0,8},{1,9},{2,10},{3,11},{4,12},{5,13},{6,14},{7,15},{8,0},{9,1},... | collective-permute-start | bytes 73736 | tf_op jit(solution)/shard_map/ppermute | solution.py:149
  50.4 0.0 collective-permute-done.14.refs_7_
  50.4 2.3 %collective-permute-start.16 = (bf16[32,384]{1,0:T(8,128)(2,1)S(1)}, bf16[32,384]{1,0:T(8,128)(2,1)S(1)}, u32[]{:S(2)}, u32[]{:S(2)}) collective-permute-start(bf16[32,384]{1,0:T(8,128)(2,1)S(1)} %get-tuple-element.51), channel_id=1, source_target_pairs={{0,12},{1,13},{2,14},{3,15},{4,8},{5,9},{6,10},{7,11},{8,4},{9,5},... | collective-permute-start | bytes 73736 | tf_op jit(solution)/shard_map/ppermute | solution.py:149
  52.6 0.9 %collective-permute-done.15.refs_8_ = bf16[32,384]{1,0:T(8,128)(2,1)S(1)} collective-permute-done((bf16[32,384]{1,0:T(8,128)(2,1)S(1)}, bf16[32,384]{1,0:T(8,128)(2,1)S(1)}, u32[]{:S(2)}, u32[]{:S(2)}) %collective-permute-start.15) | collective-permute-done | bytes 24608 | tf_op jit(solution)/shard_map/ppermute | solution.py:149
  53.5 2.4 %collective-permute-done.16.refs_9_ = bf16[32,384]{1,0:T(8,128)(2,1)S(1)} collective-permute-done((bf16[32,384]{1,0:T(8,128)(2,1)S(1)}, bf16[32,384]{1,0:T(8,128)(2,1)S(1)}, u32[]{:S(2)}, u32[]{:S(2)}) %collective-permute-start.16) | collective-permute-done | bytes 24608 | tf_op jit(solution)/shard_map/ppermute | solution.py:149
  56.0 1.1 %shard_map.105.refs_0_ = bf16[32,768]{1,0:T(8,128)(2,1)S(1)} custom-call(bf16[192,1536]{1,0:T(8,128)(2,1)S(1)} %bitcast.6, bf16[192,1536]{1,0:T(8,128)(2,1)S(1)} %collective-permute-done.refs_1_, bf16[96,1536]{1,0:T(8,128)(2,1)S(1)} %collective-permute-done.1.refs_2_, bf16[96,1536]{1,0:T(8,128)(2,1)S(1)} %collective-permute-done.2.refs_3_, ...), custom_call_target="tpu_custom_call" | custom-call | tf_op jit(solution)/shard_map/pallas_call | solution.py:435
  57.1 0.0 collective-permute-done.20.refs_1_
  57.1 0.0 collective-permute-done.21.refs_2_
  57.1 0.0 collective-permute-done.22.refs_3_
  57.1 0.7 %place.1 = bf16[32,3072]{1,0:T(8,128)(2,1)} custom-call(bf16[32,768]{1,0:T(8,128)(2,1)S(1)} %shard_map.105.refs_0_, bf16[32,768]{1,0:T(8,128)(2,1)S(1)} %collective-permute-done.20.refs_1_, bf16[32,768]{1,0:T(8,128)(2,1)S(1)} %collective-permute-done.21.refs_2_, bf16[32,768]{1,0:T(8,128)(2,1)S(1)} %collective-permute-done.22.refs_3_), custom_call_target="tpu_custom_call" | custom-call | tf_op jit(solution)/shard_map/place/pallas_call | solution.py:450
  (1 shorter events, 0.0 us)
Async XLA Ops:
  1.4 9.8 %collective-permute-start.10 = (bf16[32,768]{1,0:T(8,128)(2,1)S(1)}, bf16[32,768]{1,0:T(8,128)(2,1)S(1)}, u32[]{:S(2)}, u32[]{:S(2)}) collective-permute-start(bf16[32,768]{1,0:T(8,128)(2,1)S(1)} %get-tuple-element.43), channel_id=1, source_target_pairs={{0,12},{1,13},{2,14},{3,15},{4,8},{5,9},{6,10},{7,11},{8,4},{9,5},... | collective-permute-start | bytes 147464 | tf_op jit(solution)/shard_map/ppermute | solution.py:149
  6.5 4.7 %collective-permute-start.8 = (bf16[32,768]{1,0:T(8,128)(2,1)S(1)}, bf16[32,768]{1,0:T(8,128)(2,1)S(1)}, u32[]{:S(2)}, u32[]{:S(2)}) collective-permute-start(bf16[32,768]{1,0:T(8,128)(2,1)S(1)} %get-tuple-element.41), channel_id=1, source_target_pairs={{0,4},{1,5},{2,6},{3,7},{4,0},{5,1},{6,2},{7,3},{8,12},{9,13},{10,... | collective-permute-start | bytes 147464 | tf_op jit(solution)/shard_map/ppermute | solution.py:149
  6.5 6.1 %collective-permute-start.9 = (bf16[32,768]{1,0:T(8,128)(2,1)S(1)}, bf16[32,768]{1,0:T(8,128)(2,1)S(1)}, u32[]{:S(2)}, u32[]{:S(2)}) collective-permute-start(bf16[32,768]{1,0:T(8,128)(2,1)S(1)} %get-tuple-element.42), channel_id=1, source_target_pairs={{0,8},{1,9},{2,10},{3,11},{4,12},{5,13},{6,14},{7,15},{8,0},{9,1},... | collective-permute-start | bytes 147464 | tf_op jit(solution)/shard_map/ppermute | solution.py:149
  7.2 21.9 %collective-permute-start.1 = (bf16[96,1536]{1,0:T(8,128)(2,1)S(1)}, bf16[96,1536]{1,0:T(8,128)(2,1)S(1)}, u32[]{:S(2)}, u32[]{:S(2)}) collective-permute-start(bf16[96,1536]{1,0:T(8,128)(2,1)S(1)} %get-tuple-element.32), channel_id=1, source_target_pairs={{0,2},{1,3},{2,0},{3,1},{4,6},{5,7},{6,4},{7,5},{8,10},{9,11},{10,... | collective-permute-start | bytes 884744 | tf_op jit(solution)/shard_map/ppermute | solution.py:149
  9.5 1.7 %copy-start = (bf16[1536,192]{0,1:T(8,128)(2,1)S(1)}, bf16[1536,192]{0,1:T(8,128)(2,1)}, u32[]{:S(2)}) copy-start(bf16[1536,192]{0,1:T(8,128)(2,1)} %param.17) | copy-start | bytes 1769476
  10.8 18.4 %collective-permute-start.2 = (bf16[96,1536]{1,0:T(8,128)(2,1)S(1)}, bf16[96,1536]{1,0:T(8,128)(2,1)S(1)}, u32[]{:S(2)}, u32[]{:S(2)}) collective-permute-start(bf16[96,1536]{1,0:T(8,128)(2,1)S(1)} %get-tuple-element.33), channel_id=1, source_target_pairs={{0,2},{1,3},{2,0},{3,1},{4,6},{5,7},{6,4},{7,5},{8,10},{9,11},{10,... | collective-permute-start | bytes 884744 | tf_op jit(solution)/shard_map/ppermute | solution.py:149
  11.2 30.1 %collective-permute-start = (bf16[192,1536]{1,0:T(8,128)(2,1)S(1)}, bf16[192,1536]{1,0:T(8,128)(2,1)S(1)}, u32[]{:S(2)}, u32[]{:S(2)}) collective-permute-start(bf16[192,1536]{1,0:T(8,128)(2,1)S(1)} %bitcast.3), channel_id=1, source_target_pairs={{0,1},{1,0},{2,3},{3,2},{4,5},{5,4},{6,7},{7,6},{8,9},{9,8},{10,11... | collective-permute-start | bytes 1769480 | tf_op jit(solution)/shard_map/ppermute | solution.py:149
  11.2 4.7 %collective-permute-start.5 = (bf16[32,1152]{1,0:T(8,128)(2,1)S(1)}, bf16[32,1152]{1,0:T(8,128)(2,1)S(1)}, u32[]{:S(2)}, u32[]{:S(2)}) collective-permute-start(bf16[32,1152]{1,0:T(8,128)(2,1)S(1)} %get-tuple-element.37), channel_id=1, source_target_pairs={{0,4},{1,5},{2,6},{3,7},{4,0},{5,1},{6,2},{7,3},{8,12},{9,13},{10,... | collective-permute-start | bytes 221192 | tf_op jit(solution)/shard_map/ppermute | solution.py:149
  12.7 15.9 %collective-permute-start.12 = (bf16[128,768]{1,0:T(8,128)(2,1)S(1)}, bf16[128,768]{1,0:T(8,128)(2,1)S(1)}, u32[]{:S(2)}, u32[]{:S(2)}) collective-permute-start(bf16[128,768]{1,0:T(8,128)(2,1)S(1)} %shard_map.102), channel_id=1, source_target_pairs={{0,2},{1,3},{2,0},{3,1},{4,6},{5,7},{6,4},{7,5},{8,10},{9,11},{10,... | collective-permute-start | bytes 589832 | tf_op jit(solution)/shard_map/ppermute | solution.py:149
  15.9 6.5 %collective-permute-start.6 = (bf16[32,1152]{1,0:T(8,128)(2,1)S(1)}, bf16[32,1152]{1,0:T(8,128)(2,1)S(1)}, u32[]{:S(2)}, u32[]{:S(2)}) collective-permute-start(bf16[32,1152]{1,0:T(8,128)(2,1)S(1)} %get-tuple-element.38), channel_id=1, source_target_pairs={{0,8},{1,9},{2,10},{3,11},{4,12},{5,13},{6,14},{7,15},{8,0},{9,1},... | collective-permute-start | bytes 221192 | tf_op jit(solution)/shard_map/ppermute | solution.py:149
  22.4 6.2 %collective-permute-start.7 = (bf16[32,1152]{1,0:T(8,128)(2,1)S(1)}, bf16[32,1152]{1,0:T(8,128)(2,1)S(1)}, u32[]{:S(2)}, u32[]{:S(2)}) collective-permute-start(bf16[32,1152]{1,0:T(8,128)(2,1)S(1)} %get-tuple-element.39), channel_id=1, source_target_pairs={{0,12},{1,13},{2,14},{3,15},{4,8},{5,9},{6,10},{7,11},{8,4},{9,5},... | collective-permute-start | bytes 221192 | tf_op jit(solution)/shard_map/ppermute | solution.py:149
  28.6 1.4 %collective-permute-start.11 = (bf16[128,768]{1,0:T(8,128)(2,1)S(1)}, bf16[128,768]{1,0:T(8,128)(2,1)S(1)}, u32[]{:S(2)}, u32[]{:S(2)}) collective-permute-start(bf16[128,768]{1,0:T(8,128)(2,1)S(1)} %shard_map.102), channel_id=1, source_target_pairs={{0,1},{1,0},{2,3},{3,2},{4,5},{5,4},{6,7},{7,6},{8,9},{9,8},{10,11... | collective-permute-start | bytes 589832 | tf_op jit(solution)/shard_map/ppermute | solution.py:149
  28.6 2.9 %collective-permute-start.13 = (bf16[128,768]{1,0:T(8,128)(2,1)S(1)}, bf16[128,768]{1,0:T(8,128)(2,1)S(1)}, u32[]{:S(2)}, u32[]{:S(2)}) collective-permute-start(bf16[128,768]{1,0:T(8,128)(2,1)S(1)} %collective-permute-done.12.y_ref), channel_id=1, source_target_pairs={{0,1},{1,0},{2,3},{3,2},{4,5},{5,4},{6,7},{7,6},{8,9},{9,8},{10,11... | collective-permute-start | bytes 589832 | tf_op jit(solution)/shard_map/ppermute | solution.py:149
  29.1 12.2 %collective-permute-start.3 = (bf16[96,1536]{1,0:T(8,128)(2,1)S(1)}, bf16[96,1536]{1,0:T(8,128)(2,1)S(1)}, u32[]{:S(2)}, u32[]{:S(2)}) collective-permute-start(bf16[96,1536]{1,0:T(8,128)(2,1)S(1)} %collective-permute-done.1.refs_2_), channel_id=1, source_target_pairs={{0,1},{1,0},{2,3},{3,2},{4,5},{5,4},{6,7},{7,6},{8,9},{9,8},{10,11... | collective-permute-start | bytes 884744 | tf_op jit(solution)/shard_map/ppermute | solution.py:149
  29.2 12.1 %collective-permute-start.4 = (bf16[96,1536]{1,0:T(8,128)(2,1)S(1)}, bf16[96,1536]{1,0:T(8,128)(2,1)S(1)}, u32[]{:S(2)}, u32[]{:S(2)}) collective-permute-start(bf16[96,1536]{1,0:T(8,128)(2,1)S(1)} %collective-permute-done.2.refs_3_), channel_id=1, source_target_pairs={{0,1},{1,0},{2,3},{3,2},{4,5},{5,4},{6,7},{7,6},{8,9},{9,8},{10,11... | collective-permute-start | bytes 884744 | tf_op jit(solution)/shard_map/ppermute | solution.py:149
  32.3 4.4 %collective-permute-start.19 = (bf16[96,384]{1,0:T(8,128)(2,1)S(1)}, bf16[96,384]{1,0:T(8,128)(2,1)S(1)}, u32[]{:S(2)}, u32[]{:S(2)}) collective-permute-start(bf16[96,384]{1,0:T(8,128)(2,1)S(1)} %get-tuple-element.55), channel_id=1, source_target_pairs={{0,4},{1,5},{2,6},{3,7},{4,0},{5,1},{6,2},{7,3},{8,12},{9,13},{10,... | collective-permute-start | bytes 221192 | tf_op jit(solution)/shard_map/ppermute | solution.py:149
  32.4 9.6 %collective-permute-start.17 = (bf16[96,384]{1,0:T(8,128)(2,1)S(1)}, bf16[96,384]{1,0:T(8,128)(2,1)S(1)}, u32[]{:S(2)}, u32[]{:S(2)}) collective-permute-start(bf16[96,384]{1,0:T(8,128)(2,1)S(1)} %get-tuple-element.53), channel_id=1, source_target_pairs={{0,8},{1,9},{2,10},{3,11},{4,12},{5,13},{6,14},{7,15},{8,0},{9,1},... | collective-permute-start | bytes 221192 | tf_op jit(solution)/shard_map/ppermute | solution.py:149
  36.7 6.9 %collective-permute-start.18 = (bf16[96,384]{1,0:T(8,128)(2,1)S(1)}, bf16[96,384]{1,0:T(8,128)(2,1)S(1)}, u32[]{:S(2)}, u32[]{:S(2)}) collective-permute-start(bf16[96,384]{1,0:T(8,128)(2,1)S(1)} %get-tuple-element.54), channel_id=1, source_target_pairs={{0,12},{1,13},{2,14},{3,15},{4,8},{5,9},{6,10},{7,11},{8,4},{9,5},... | collective-permute-start | bytes 221192 | tf_op jit(solution)/shard_map/ppermute | solution.py:149
  41.3 9.0 %collective-permute-start.14 = (bf16[32,384]{1,0:T(8,128)(2,1)S(1)}, bf16[32,384]{1,0:T(8,128)(2,1)S(1)}, u32[]{:S(2)}, u32[]{:S(2)}) collective-permute-start(bf16[32,384]{1,0:T(8,128)(2,1)S(1)} %get-tuple-element.49), channel_id=1, source_target_pairs={{0,4},{1,5},{2,6},{3,7},{4,0},{5,1},{6,2},{7,3},{8,12},{9,13},{10,... | collective-permute-start | bytes 73736 | tf_op jit(solution)/shard_map/ppermute | solution.py:149
  44.4 12.8 %collective-permute-start.20 = (bf16[32,768]{1,0:T(8,128)(2,1)S(1)}, bf16[32,768]{1,0:T(8,128)(2,1)S(1)}, u32[]{:S(2)}, u32[]{:S(2)}) collective-permute-start(bf16[32,768]{1,0:T(8,128)(2,1)S(1)} %get-tuple-element.56), channel_id=1, source_target_pairs={{0,4},{1,5},{2,6},{3,7},{4,0},{5,1},{6,2},{7,3},{8,12},{9,13},{10,... | collective-permute-start | bytes 147464 | tf_op jit(solution)/shard_map/ppermute | solution.py:149
  44.8 12.3 %collective-permute-start.21 = (bf16[32,768]{1,0:T(8,128)(2,1)S(1)}, bf16[32,768]{1,0:T(8,128)(2,1)S(1)}, u32[]{:S(2)}, u32[]{:S(2)}) collective-permute-start(bf16[32,768]{1,0:T(8,128)(2,1)S(1)} %get-tuple-element.57), channel_id=1, source_target_pairs={{0,8},{1,9},{2,10},{3,11},{4,12},{5,13},{6,14},{7,15},{8,0},{9,1},... | collective-permute-start | bytes 147464 | tf_op jit(solution)/shard_map/ppermute | solution.py:149
  48.8 8.3 %collective-permute-start.22 = (bf16[32,768]{1,0:T(8,128)(2,1)S(1)}, bf16[32,768]{1,0:T(8,128)(2,1)S(1)}, u32[]{:S(2)}, u32[]{:S(2)}) collective-permute-start(bf16[32,768]{1,0:T(8,128)(2,1)S(1)} %get-tuple-element.58), channel_id=1, source_target_pairs={{0,12},{1,13},{2,14},{3,15},{4,8},{5,9},{6,10},{7,11},{8,4},{9,5},... | collective-permute-start | bytes 147464 | tf_op jit(solution)/shard_map/ppermute | solution.py:149
  48.8 4.7 %collective-permute-start.15 = (bf16[32,384]{1,0:T(8,128)(2,1)S(1)}, bf16[32,384]{1,0:T(8,128)(2,1)S(1)}, u32[]{:S(2)}, u32[]{:S(2)}) collective-permute-start(bf16[32,384]{1,0:T(8,128)(2,1)S(1)} %get-tuple-element.50), channel_id=1, source_target_pairs={{0,8},{1,9},{2,10},{3,11},{4,12},{5,13},{6,14},{7,15},{8,0},{9,1},... | collective-permute-start | bytes 73736 | tf_op jit(solution)/shard_map/ppermute | solution.py:149
  50.4 5.6 %collective-permute-start.16 = (bf16[32,384]{1,0:T(8,128)(2,1)S(1)}, bf16[32,384]{1,0:T(8,128)(2,1)S(1)}, u32[]{:S(2)}, u32[]{:S(2)}) collective-permute-start(bf16[32,384]{1,0:T(8,128)(2,1)S(1)} %get-tuple-element.51), channel_id=1, source_target_pairs={{0,12},{1,13},{2,14},{3,15},{4,8},{5,9},{6,10},{7,11},{8,4},{9,5},... | collective-permute-start | bytes 73736 | tf_op jit(solution)/shard_map/ppermute | solution.py:149

commit v3 on v2

--- a/solution.py
+++ b/solution.py
@@ -142,6 +142,10 @@
 
 QUAD = 4
 GRANT = 8 * 2**20
+
+
+def step_to(k):
+    return QUAD * k ^ (k in (1, 2))
 
 
 def swap(shard, by):
@@ -390,9 +394,9 @@
     )(*in_hbm(queries, fresh_keys, fresh_values, stale_keys, stale_values, columns))
     stale, fresh = packed[:lines], packed[lines:]
     for k in others:
-        stale[k] = swap(stale[k], QUAD * k)
+        stale[k] = swap(stale[k], step_to(k))
     for k in others:
-        fresh[k] = swap(fresh[k], QUAD * k)
+        fresh[k] = swap(fresh[k], step_to(k))
     text_k, text_v, gate, late = kernel(
         fetch_kernel,
         [shaped(text, width)] * 2
@@ -424,9 +428,9 @@
     )(*early_part, by_y, by_both)
     theirs, mine = [attended, *blocks[: lines - 1]], [attended, *blocks[lines - 1 :]]
     for k in others:
-        theirs[k] = swap(theirs[k], QUAD * k)
+        theirs[k] = swap(theirs[k], step_to(k))
     for k in others:
-        mine[k] = swap(mine[k], QUAD * k)
+        mine[k] = swap(mine[k], step_to(k))
     weights = [columns, weight_core, *weight_y, *weight_both]
 
     def project(ks, own_rows, attended, before, outs):
@@ -445,7 +449,7 @@
     sums = project(near, False, theirs, None, sums)
     parts = [None, *project(far, False, theirs, sums, [made] * (lines - 1))]
     for k in others:
-        parts[k] = swap(parts[k], QUAD * k)
+        parts[k] = swap(parts[k], step_to(k))
     parts[0] = project(every, True, mine, None, [made])[0]
     return pl.pallas_call(
         place_kernel,

time: 58 us -> 57.6 us (level)
  waiting for transfers between devices: 14.1 us -> 12.8 us
  starting transfers between devices: 34.9 us -> 35.7 us
    ppermute x23, waiting for transfers between devices: 14.1 us -> 12.8 us  [swap(): return lax.ppermute(shard, 'patch', [(i, i ^ by) for i in range(peers)])]
    ppermute x23, starting transfers between devices: 34.9 us -> 35.7 us  [swap(): return lax.ppermute(shard, 'patch', [(i, i ^ by) for i in range(peers)])]
where the time goes in v3:
time: 57.6 us; the launch traced here: 57.4 us
  starting transfers between devices  35.7 us (62%)
  waiting for transfers between devices  12.8 us (22%)
  Pallas kernels  8.1 us (14%)
  between operations  0.8 us (1%)
    ppermute x23, starting transfers between devices, swap(): return lax.ppermute(shard, 'patch', [(i, i ^ by) for i in range(peers)])  35.7 us
    ppermute x23, waiting for transfers between devices, swap(): return lax.ppermute(shard, 'patch', [(i, i ^ by) for i in range(peers)])  12.8 us
    pallas_call x3, Pallas kernels, project(): kernel(functools.partial(project_kernel, ks, own_rows, first, last), outs...  2.48 us
    pallas_call x1, Pallas kernels, square_body(): kernel(early_kernel, [shaped(stacked, LANES)] + [shaped(stacked, LANES, d...  1.46 us
    pallas_call x1, Pallas kernels, square_body(): kernel(pack_kernel, [shaped(rows, 2 * width)] * lines + [shaped(rows, 3 *...  1.39 us
    pallas_call x1, Pallas kernels, square_body(): kernel(fetch_kernel, [shaped(text, width)] * 2 + [shaped(1, out_width, dt...  1.26 us
  transfers between devices with their start and end apart: 23, of which 8 were waited for; matrix products, arithmetic and copies ran while one was open for 0% of the time, Pallas kernels for 10%

profile of v3, /device:TPU:0, one launch (start us, length us, event | category | flops | bytes accessed | tf_op | source)
XLA Modules:
  0.0 57.4 jit_solution(5544097532971585307)
XLA Ops:
  0.0 1.4 %shard_map.100 = (bf16[32,768]{1,0:T(8,128)(2,1)S(1)}, bf16[32,768]{1,0:T(8,128)(2,1)S(1)}, bf16[32,768]{1,0:T(8,128)(2,1)S(1)}, bf16[32,768]{1,0:T(8,128)(2,1)S...) custom-call(bf16[32,1536]{1,0:T(8,128)(2,1)} %q_ref.1, ...), custom_call_target="tpu_custom_call" | custom-call | tf_op jit(solution)/shard_map/pallas_call | solution.py:387
  1.4 5.1 %collective-permute-start.10 = (bf16[32,768]{1,0:T(8,128)(2,1)S(1)}, bf16[32,768]{1,0:T(8,128)(2,1)S(1)}, u32[]{:S(2)}, u32[]{:S(2)}) collective-permute-start(bf16[32,768]{1,0:T(8,128)(2,1)S(1)} %get-tuple-element.43), channel_id=1, source_target_pairs={{0,12},{1,13},{2,14},{3,15},{4,8},{5,9},{6,10},{7,11},{8,4},{9,5},... | collective-permute-start | bytes 147464 | tf_op jit(solution)/shard_map/ppermute | solution.py:153
  6.5 0.0 collective-permute-start.8
  6.5 0.4 collective-permute-start.9
  6.9 1.7 %collective-permute-start.1 = (bf16[96,1536]{1,0:T(8,128)(2,1)S(1)}, bf16[96,1536]{1,0:T(8,128)(2,1)S(1)}, u32[]{:S(2)}, u32[]{:S(2)}) collective-permute-start(bf16[96,1536]{1,0:T(8,128)(2,1)S(1)} %get-tuple-element.32), channel_id=1, source_target_pairs={{0,2},{1,3},{2,0},{3,1},{4,6},{5,7},{6,4},{7,5},{8,10},{9,11},{10,... | collective-permute-start | bytes 884744 | tf_op jit(solution)/shard_map/ppermute | solution.py:153
  9.2 0.0 copy-start
  9.2 1.3 %shard_map.101 = (bf16[226,384]{1,0:T(8,128)(2,1)S(1)}, bf16[226,384]{1,0:T(8,128)(2,1)S(1)}, f32[1,768]{1,0:T(1,128)S(1)}, bf16[96,1536]{1,0:T(8,128)(2,1)S(1)}) custom-call(s32[1]{0:T(128)S(6)} %copy.11.step_ref, bf16[226,1536]{1,0:T(8,128)(2,1)} %tk_ref.1, bf16[226,1536]{1,0:T(8,128)(2,1)} %tv_ref.1, f32[50,3072]{1,0:T(8,128)} %gate_ref.1, ...), custom_call_target="tpu_custom_call" | custom-call | tf_op jit(solution)/shard_map/pallas_call | solution.py:400
  10.5 0.4 collective-permute-start.2
  10.9 0.0 collective-permute-done.10.refs_3_.refs_7_
  10.9 0.0 copy-done
  10.9 0.0 collective-permute-start
  10.9 0.0 collective-permute-done.8.refs_1_.refs_5_
  10.9 0.9 %collective-permute-start.5 = (bf16[32,1152]{1,0:T(8,128)(2,1)S(1)}, bf16[32,1152]{1,0:T(8,128)(2,1)S(1)}, u32[]{:S(2)}, u32[]{:S(2)}) collective-permute-start(bf16[32,1152]{1,0:T(8,128)(2,1)S(1)} %get-tuple-element.37), channel_id=1, source_target_pairs={{0,5},{1,4},{2,7},{3,6},{4,1},{5,0},{6,3},{7,2},{8,13},{9,12},{10,... | collective-permute-start | bytes 221192 | tf_op jit(solution)/shard_map/ppermute | solution.py:153
  11.9 0.0 collective-permute-done.9.refs_2_.refs_6_
  11.9 1.6 %collective-permute-start.12 = (bf16[128,768]{1,0:T(8,128)(2,1)S(1)}, bf16[128,768]{1,0:T(8,128)(2,1)S(1)}, u32[]{:S(2)}, u32[]{:S(2)}) collective-permute-start(bf16[128,768]{1,0:T(8,128)(2,1)S(1)} %shard_map.102), channel_id=1, source_target_pairs={{0,2},{1,3},{2,0},{3,1},{4,6},{5,7},{6,4},{7,5},{8,10},{9,11},{10,... | collective-permute-start | bytes 589832 | tf_op jit(solution)/shard_map/ppermute | solution.py:153
  13.5 1.5 %collective-permute-done.5.refs_1_ = bf16[32,1152]{1,0:T(8,128)(2,1)S(1)} collective-permute-done((bf16[32,1152]{1,0:T(8,128)(2,1)S(1)}, bf16[32,1152]{1,0:T(8,128)(2,1)S(1)}, u32[]{:S(2)}, u32[]{:S(2)}) %collective-permute-start.5) | collective-permute-done | bytes 73760 | tf_op jit(solution)/shard_map/ppermute | solution.py:153
  15.0 2.9 %collective-permute-start.6 = (bf16[32,1152]{1,0:T(8,128)(2,1)S(1)}, bf16[32,1152]{1,0:T(8,128)(2,1)S(1)}, u32[]{:S(2)}, u32[]{:S(2)}) collective-permute-start(bf16[32,1152]{1,0:T(8,128)(2,1)S(1)} %get-tuple-element.38), channel_id=1, source_target_pairs={{0,9},{1,8},{2,11},{3,10},{4,13},{5,12},{6,15},{7,14},{8,1},{9,0},... | collective-permute-start | bytes 221192 | tf_op jit(solution)/shard_map/ppermute | solution.py:153
  17.9 2.2 %collective-permute-done.6.refs_2_ = bf16[32,1152]{1,0:T(8,128)(2,1)S(1)} collective-permute-done((bf16[32,1152]{1,0:T(8,128)(2,1)S(1)}, bf16[32,1152]{1,0:T(8,128)(2,1)S(1)}, u32[]{:S(2)}, u32[]{:S(2)}) %collective-permute-start.6) | collective-permute-done | bytes 73760 | tf_op jit(solution)/shard_map/ppermute | solution.py:153
  20.1 5.4 %collective-permute-start.7 = (bf16[32,1152]{1,0:T(8,128)(2,1)S(1)}, bf16[32,1152]{1,0:T(8,128)(2,1)S(1)}, u32[]{:S(2)}, u32[]{:S(2)}) collective-permute-start(bf16[32,1152]{1,0:T(8,128)(2,1)S(1)} %get-tuple-element.39), channel_id=1, source_target_pairs={{0,12},{1,13},{2,14},{3,15},{4,8},{5,9},{6,10},{7,11},{8,4},{9,5},... | collective-permute-start | bytes 221192 | tf_op jit(solution)/shard_map/ppermute | solution.py:153
  25.6 2.7 %collective-permute-done.7.refs_3_ = bf16[32,1152]{1,0:T(8,128)(2,1)S(1)} collective-permute-done((bf16[32,1152]{1,0:T(8,128)(2,1)S(1)}, bf16[32,1152]{1,0:T(8,128)(2,1)S(1)}, u32[]{:S(2)}, u32[]{:S(2)}) %collective-permute-start.7) | collective-permute-done | bytes 73760 | tf_op jit(solution)/shard_map/ppermute | solution.py:153
  28.2 0.0 collective-permute-start.11
  28.2 0.0 collective-permute-done.12.y_ref
  28.2 0.5 collective-permute-start.13
  28.7 0.0 collective-permute-done.1.refs_2_
  28.7 0.1 collective-permute-start.3
  28.8 0.0 collective-permute-done.2.refs_3_
  28.8 0.4 collective-permute-start.4
  29.2 0.4 collective-permute-done.11.refs_8_
  29.6 1.5 %shard_map.103 = (bf16[768,128]{1,0:T(8,128)(2,1)S(1)}, f32[768,128]{1,0:T(8,128)S(1)}, f32[768,128]{1,0:T(8,128)S(1)}, f32[768,128]{1,0:T(8,128)S(1)}) custom-call(bf16[226,384]{1,0:T(8,128)(2,1)S(1)} %get-tuple-element.34.tk_ref, bf16[226,384]{1,0:T(8,128)(2,1)S(1)} %get-tuple-element.35.tv_ref, bf16[32,1152]{1,0:T(8,128)(2,1)S(1)} %get-tuple-element.36.refs_0_, ...), custom_call_target="tpu_custom_call" | custom-call | tf_op jit(solution)/shard_map/pallas_call | solution.py:417
  31.1 0.0 collective-permute-done.13.both_ref
  31.1 0.8 %shard_map.104 = (bf16[128,384]{1,0:T(8,128)(2,1)S(1)}, bf16[96,384]{1,0:T(8,128)(2,1)S(1)}, bf16[96,384]{1,0:T(8,128)(2,1)S(1)}, bf16[96,384]{1,0:T(8,128)(2,1)...) custom-call(bf16[768,128]{1,0:T(8,128)(2,1)S(1)} %get-tuple-element.44.q_ref, ...), custom_call_target="tpu_custom_call" | custom-call | tf_op jit(solution)/shard_map/pallas_call | solution.py:422
  31.9 0.5 collective-permute-start.19
  32.4 3.4 %collective-permute-start.17 = (bf16[96,384]{1,0:T(8,128)(2,1)S(1)}, bf16[96,384]{1,0:T(8,128)(2,1)S(1)}, u32[]{:S(2)}, u32[]{:S(2)}) collective-permute-start(bf16[96,384]{1,0:T(8,128)(2,1)S(1)} %get-tuple-element.53), channel_id=1, source_target_pairs={{0,9},{1,8},{2,11},{3,10},{4,13},{5,12},{6,15},{7,14},{8,1},{9,0},... | collective-permute-start | bytes 221192 | tf_op jit(solution)/shard_map/ppermute | solution.py:153
  35.8 0.5 collective-permute-done.19.refs_7_
  36.2 4.7 %collective-permute-start.18 = (bf16[96,384]{1,0:T(8,128)(2,1)S(1)}, bf16[96,384]{1,0:T(8,128)(2,1)S(1)}, u32[]{:S(2)}, u32[]{:S(2)}) collective-permute-start(bf16[96,384]{1,0:T(8,128)(2,1)S(1)} %get-tuple-element.54), channel_id=1, source_target_pairs={{0,12},{1,13},{2,14},{3,15},{4,8},{5,9},{6,10},{7,11},{8,4},{9,5},... | collective-permute-start | bytes 221192 | tf_op jit(solution)/shard_map/ppermute | solution.py:153
  40.9 0.0 collective-permute-done.3.refs_4_
  40.9 0.0 collective-permute-start.14
  40.9 0.0 collective-permute-done.4.refs_5_
  40.9 0.0 collective-permute-done.refs_1_
  40.9 0.6 %shard_map.106.refs_8_ = f32[4,96,192]{2,1,0:T(8,128)S(1)} custom-call(bf16[192,1536]{1,0:T(8,128)(2,1)S(1)} %bitcast.4, bf16[192,1536]{1,0:T(8,128)(2,1)S(1)} %collective-permute-done.refs_1_, bf16[96,1536]{1,0:T(8,128)(2,1)S(1)} %collective-permute-done.1.refs_2_, bf16[96,1536]{1,0:T(8,128)(2,1)S(1)} %collective-permute-done.2.refs_3_, ...), custom_call_target="tpu_custom_call" | custom-call | tf_op jit(solution)/shard_map/pallas_call | solution.py:439
  41.6 0.0 collective-permute-done.17.refs_6_
  41.6 2.4 %collective-permute-done.18.refs_7_ = bf16[96,384]{1,0:T(8,128)(2,1)S(1)} collective-permute-done((bf16[96,384]{1,0:T(8,128)(2,1)S(1)}, bf16[96,384]{1,0:T(8,128)(2,1)S(1)}, u32[]{:S(2)}, u32[]{:S(2)}) %collective-permute-start.18) | collective-permute-done | bytes 73760 | tf_op jit(solution)/shard_map/ppermute | solution.py:153
  44.0 0.7 %shard_map.107 = (bf16[32,768]{1,0:T(8,128)(2,1)S(1)}, bf16[32,768]{1,0:T(8,128)(2,1)S(1)}, bf16[32,768]{1,0:T(8,128)(2,1)S(1)}) custom-call(bf16[192,1536]{1,0:T(8,128)(2,1)S(1)} %bitcast.5, bf16[192,1536]{1,0:T(8,128)(2,1)S(1)} %collective-permute-done.refs_1_, bf16[96,1536]{1,0:T(8,128)(2,1)S(1)} %collective-permute-done.1.refs_2_, ...), custom_call_target="tpu_custom_call" | custom-call | tf_op jit(solution)/shard_map/pallas_call | solution.py:439
  44.7 0.1 collective-permute-start.20
  44.8 3.8 %collective-permute-start.21 = (bf16[32,768]{1,0:T(8,128)(2,1)S(1)}, bf16[32,768]{1,0:T(8,128)(2,1)S(1)}, u32[]{:S(2)}, u32[]{:S(2)}) collective-permute-start(bf16[32,768]{1,0:T(8,128)(2,1)S(1)} %get-tuple-element.57), channel_id=1, source_target_pairs={{0,9},{1,8},{2,11},{3,10},{4,13},{5,12},{6,15},{7,14},{8,1},{9,0},... | collective-permute-start | bytes 147464 | tf_op jit(solution)/shard_map/ppermute | solution.py:153
  48.6 0.3 collective-permute-start.22
  48.9 1.0 %collective-permute-start.15 = (bf16[32,384]{1,0:T(8,128)(2,1)S(1)}, bf16[32,384]{1,0:T(8,128)(2,1)S(1)}, u32[]{:S(2)}, u32[]{:S(2)}) collective-permute-start(bf16[32,384]{1,0:T(8,128)(2,1)S(1)} %get-tuple-element.50), channel_id=1, source_target_pairs={{0,9},{1,8},{2,11},{3,10},{4,13},{5,12},{6,15},{7,14},{8,1},{9,0},... | collective-permute-start | bytes 73736 | tf_op jit(solution)/shard_map/ppermute | solution.py:153
  49.9 0.0 collective-permute-done.14.refs_7_
  49.9 2.6 %collective-permute-start.16 = (bf16[32,384]{1,0:T(8,128)(2,1)S(1)}, bf16[32,384]{1,0:T(8,128)(2,1)S(1)}, u32[]{:S(2)}, u32[]{:S(2)}) collective-permute-start(bf16[32,384]{1,0:T(8,128)(2,1)S(1)} %get-tuple-element.51), channel_id=1, source_target_pairs={{0,12},{1,13},{2,14},{3,15},{4,8},{5,9},{6,10},{7,11},{8,4},{9,5},... | collective-permute-start | bytes 73736 | tf_op jit(solution)/shard_map/ppermute | solution.py:153
  52.5 1.4 %collective-permute-done.15.refs_8_ = bf16[32,384]{1,0:T(8,128)(2,1)S(1)} collective-permute-done((bf16[32,384]{1,0:T(8,128)(2,1)S(1)}, bf16[32,384]{1,0:T(8,128)(2,1)S(1)}, u32[]{:S(2)}, u32[]{:S(2)}) %collective-permute-start.15) | collective-permute-done | bytes 24608 | tf_op jit(solution)/shard_map/ppermute | solution.py:153
  53.8 1.7 %collective-permute-done.16.refs_9_ = bf16[32,384]{1,0:T(8,128)(2,1)S(1)} collective-permute-done((bf16[32,384]{1,0:T(8,128)(2,1)S(1)}, bf16[32,384]{1,0:T(8,128)(2,1)S(1)}, u32[]{:S(2)}, u32[]{:S(2)}) %collective-permute-start.16) | collective-permute-done | bytes 24608 | tf_op jit(solution)/shard_map/ppermute | solution.py:153
  55.5 1.1 %shard_map.105.refs_0_ = bf16[32,768]{1,0:T(8,128)(2,1)S(1)} custom-call(bf16[192,1536]{1,0:T(8,128)(2,1)S(1)} %bitcast.6, bf16[192,1536]{1,0:T(8,128)(2,1)S(1)} %collective-permute-done.refs_1_, bf16[96,1536]{1,0:T(8,128)(2,1)S(1)} %collective-permute-done.1.refs_2_, bf16[96,1536]{1,0:T(8,128)(2,1)S(1)} %collective-permute-done.2.refs_3_, ...), custom_call_target="tpu_custom_call" | custom-call | tf_op jit(solution)/shard_map/pallas_call | solution.py:439
  56.7 0.0 collective-permute-done.20.refs_1_
  56.7 0.0 collective-permute-done.21.refs_2_
  56.7 0.0 collective-permute-done.22.refs_3_
  56.7 0.7 %place.1 = bf16[32,3072]{1,0:T(8,128)(2,1)} custom-call(bf16[32,768]{1,0:T(8,128)(2,1)S(1)} %shard_map.105.refs_0_, bf16[32,768]{1,0:T(8,128)(2,1)S(1)} %collective-permute-done.20.refs_1_, bf16[32,768]{1,0:T(8,128)(2,1)S(1)} %collective-permute-done.21.refs_2_, bf16[32,768]{1,0:T(8,128)(2,1)S(1)} %collective-permute-done.22.refs_3_), custom_call_target="tpu_custom_call" | custom-call | tf_op jit(solution)/shard_map/place/pallas_call | solution.py:454
  (1 shorter events, 0.0 us)
Async XLA Ops:
  1.4 9.5 %collective-permute-start.10 = (bf16[32,768]{1,0:T(8,128)(2,1)S(1)}, bf16[32,768]{1,0:T(8,128)(2,1)S(1)}, u32[]{:S(2)}, u32[]{:S(2)}) collective-permute-start(bf16[32,768]{1,0:T(8,128)(2,1)S(1)} %get-tuple-element.43), channel_id=1, source_target_pairs={{0,12},{1,13},{2,14},{3,15},{4,8},{5,9},{6,10},{7,11},{8,4},{9,5},... | collective-permute-start | bytes 147464 | tf_op jit(solution)/shard_map/ppermute | solution.py:153
  6.5 4.4 %collective-permute-start.8 = (bf16[32,768]{1,0:T(8,128)(2,1)S(1)}, bf16[32,768]{1,0:T(8,128)(2,1)S(1)}, u32[]{:S(2)}, u32[]{:S(2)}) collective-permute-start(bf16[32,768]{1,0:T(8,128)(2,1)S(1)} %get-tuple-element.41), channel_id=1, source_target_pairs={{0,5},{1,4},{2,7},{3,6},{4,1},{5,0},{6,3},{7,2},{8,13},{9,12},{10,... | collective-permute-start | bytes 147464 | tf_op jit(solution)/shard_map/ppermute | solution.py:153
  6.5 5.3 %collective-permute-start.9 = (bf16[32,768]{1,0:T(8,128)(2,1)S(1)}, bf16[32,768]{1,0:T(8,128)(2,1)S(1)}, u32[]{:S(2)}, u32[]{:S(2)}) collective-permute-start(bf16[32,768]{1,0:T(8,128)(2,1)S(1)} %get-tuple-element.42), channel_id=1, source_target_pairs={{0,9},{1,8},{2,11},{3,10},{4,13},{5,12},{6,15},{7,14},{8,1},{9,0},... | collective-permute-start | bytes 147464 | tf_op jit(solution)/shard_map/ppermute | solution.py:153
  6.9 21.8 %collective-permute-start.1 = (bf16[96,1536]{1,0:T(8,128)(2,1)S(1)}, bf16[96,1536]{1,0:T(8,128)(2,1)S(1)}, u32[]{:S(2)}, u32[]{:S(2)}) collective-permute-start(bf16[96,1536]{1,0:T(8,128)(2,1)S(1)} %get-tuple-element.32), channel_id=1, source_target_pairs={{0,2},{1,3},{2,0},{3,1},{4,6},{5,7},{6,4},{7,5},{8,10},{9,11},{10,... | collective-permute-start | bytes 884744 | tf_op jit(solution)/shard_map/ppermute | solution.py:153
  9.2 1.7 %copy-start = (bf16[1536,192]{0,1:T(8,128)(2,1)S(1)}, bf16[1536,192]{0,1:T(8,128)(2,1)}, u32[]{:S(2)}) copy-start(bf16[1536,192]{0,1:T(8,128)(2,1)} %param.17) | copy-start | bytes 1769476
  10.5 18.3 %collective-permute-start.2 = (bf16[96,1536]{1,0:T(8,128)(2,1)S(1)}, bf16[96,1536]{1,0:T(8,128)(2,1)S(1)}, u32[]{:S(2)}, u32[]{:S(2)}) collective-permute-start(bf16[96,1536]{1,0:T(8,128)(2,1)S(1)} %get-tuple-element.33), channel_id=1, source_target_pairs={{0,2},{1,3},{2,0},{3,1},{4,6},{5,7},{6,4},{7,5},{8,10},{9,11},{10,... | collective-permute-start | bytes 884744 | tf_op jit(solution)/shard_map/ppermute | solution.py:153
  10.9 30.0 %collective-permute-start = (bf16[192,1536]{1,0:T(8,128)(2,1)S(1)}, bf16[192,1536]{1,0:T(8,128)(2,1)S(1)}, u32[]{:S(2)}, u32[]{:S(2)}) collective-permute-start(bf16[192,1536]{1,0:T(8,128)(2,1)S(1)} %bitcast.3), channel_id=1, source_target_pairs={{0,1},{1,0},{2,3},{3,2},{4,5},{5,4},{6,7},{7,6},{8,9},{9,8},{10,11... | collective-permute-start | bytes 1769480 | tf_op jit(solution)/shard_map/ppermute | solution.py:153
  10.9 4.0 %collective-permute-start.5 = (bf16[32,1152]{1,0:T(8,128)(2,1)S(1)}, bf16[32,1152]{1,0:T(8,128)(2,1)S(1)}, u32[]{:S(2)}, u32[]{:S(2)}) collective-permute-start(bf16[32,1152]{1,0:T(8,128)(2,1)S(1)} %get-tuple-element.37), channel_id=1, source_target_pairs={{0,5},{1,4},{2,7},{3,6},{4,1},{5,0},{6,3},{7,2},{8,13},{9,12},{10,... | collective-permute-start | bytes 221192 | tf_op jit(solution)/shard_map/ppermute | solution.py:153
  11.9 16.3 %collective-permute-start.12 = (bf16[128,768]{1,0:T(8,128)(2,1)S(1)}, bf16[128,768]{1,0:T(8,128)(2,1)S(1)}, u32[]{:S(2)}, u32[]{:S(2)}) collective-permute-start(bf16[128,768]{1,0:T(8,128)(2,1)S(1)} %shard_map.102), channel_id=1, source_target_pairs={{0,2},{1,3},{2,0},{3,1},{4,6},{5,7},{6,4},{7,5},{8,10},{9,11},{10,... | collective-permute-start | bytes 589832 | tf_op jit(solution)/shard_map/ppermute | solution.py:153
  15.0 5.2 %collective-permute-start.6 = (bf16[32,1152]{1,0:T(8,128)(2,1)S(1)}, bf16[32,1152]{1,0:T(8,128)(2,1)S(1)}, u32[]{:S(2)}, u32[]{:S(2)}) collective-permute-start(bf16[32,1152]{1,0:T(8,128)(2,1)S(1)} %get-tuple-element.38), channel_id=1, source_target_pairs={{0,9},{1,8},{2,11},{3,10},{4,13},{5,12},{6,15},{7,14},{8,1},{9,0},... | collective-permute-start | bytes 221192 | tf_op jit(solution)/shard_map/ppermute | solution.py:153
  20.1 8.1 %collective-permute-start.7 = (bf16[32,1152]{1,0:T(8,128)(2,1)S(1)}, bf16[32,1152]{1,0:T(8,128)(2,1)S(1)}, u32[]{:S(2)}, u32[]{:S(2)}) collective-permute-start(bf16[32,1152]{1,0:T(8,128)(2,1)S(1)} %get-tuple-element.39), channel_id=1, source_target_pairs={{0,12},{1,13},{2,14},{3,15},{4,8},{5,9},{6,10},{7,11},{8,4},{9,5},... | collective-permute-start | bytes 221192 | tf_op jit(solution)/shard_map/ppermute | solution.py:153
  28.2 1.4 %collective-permute-start.11 = (bf16[128,768]{1,0:T(8,128)(2,1)S(1)}, bf16[128,768]{1,0:T(8,128)(2,1)S(1)}, u32[]{:S(2)}, u32[]{:S(2)}) collective-permute-start(bf16[128,768]{1,0:T(8,128)(2,1)S(1)} %shard_map.102), channel_id=1, source_target_pairs={{0,1},{1,0},{2,3},{3,2},{4,5},{5,4},{6,7},{7,6},{8,9},{9,8},{10,11... | collective-permute-start | bytes 589832 | tf_op jit(solution)/shard_map/ppermute | solution.py:153
  28.2 2.9 %collective-permute-start.13 = (bf16[128,768]{1,0:T(8,128)(2,1)S(1)}, bf16[128,768]{1,0:T(8,128)(2,1)S(1)}, u32[]{:S(2)}, u32[]{:S(2)}) collective-permute-start(bf16[128,768]{1,0:T(8,128)(2,1)S(1)} %collective-permute-done.12.y_ref), channel_id=1, source_target_pairs={{0,1},{1,0},{2,3},{3,2},{4,5},{5,4},{6,7},{7,6},{8,9},{9,8},{10,11... | collective-permute-start | bytes 589832 | tf_op jit(solution)/shard_map/ppermute | solution.py:153
  28.7 12.2 %collective-permute-start.3 = (bf16[96,1536]{1,0:T(8,128)(2,1)S(1)}, bf16[96,1536]{1,0:T(8,128)(2,1)S(1)}, u32[]{:S(2)}, u32[]{:S(2)}) collective-permute-start(bf16[96,1536]{1,0:T(8,128)(2,1)S(1)} %collective-permute-done.1.refs_2_), channel_id=1, source_target_pairs={{0,1},{1,0},{2,3},{3,2},{4,5},{5,4},{6,7},{7,6},{8,9},{9,8},{10,11... | collective-permute-start | bytes 884744 | tf_op jit(solution)/shard_map/ppermute | solution.py:153
  28.8 12.1 %collective-permute-start.4 = (bf16[96,1536]{1,0:T(8,128)(2,1)S(1)}, bf16[96,1536]{1,0:T(8,128)(2,1)S(1)}, u32[]{:S(2)}, u32[]{:S(2)}) collective-permute-start(bf16[96,1536]{1,0:T(8,128)(2,1)S(1)} %collective-permute-done.2.refs_3_), channel_id=1, source_target_pairs={{0,1},{1,0},{2,3},{3,2},{4,5},{5,4},{6,7},{7,6},{8,9},{9,8},{10,11... | collective-permute-start | bytes 884744 | tf_op jit(solution)/shard_map/ppermute | solution.py:153
  31.9 4.3 %collective-permute-start.19 = (bf16[96,384]{1,0:T(8,128)(2,1)S(1)}, bf16[96,384]{1,0:T(8,128)(2,1)S(1)}, u32[]{:S(2)}, u32[]{:S(2)}) collective-permute-start(bf16[96,384]{1,0:T(8,128)(2,1)S(1)} %get-tuple-element.55), channel_id=1, source_target_pairs={{0,5},{1,4},{2,7},{3,6},{4,1},{5,0},{6,3},{7,2},{8,13},{9,12},{10,... | collective-permute-start | bytes 221192 | tf_op jit(solution)/shard_map/ppermute | solution.py:153
  32.4 9.2 %collective-permute-start.17 = (bf16[96,384]{1,0:T(8,128)(2,1)S(1)}, bf16[96,384]{1,0:T(8,128)(2,1)S(1)}, u32[]{:S(2)}, u32[]{:S(2)}) collective-permute-start(bf16[96,384]{1,0:T(8,128)(2,1)S(1)} %get-tuple-element.53), channel_id=1, source_target_pairs={{0,9},{1,8},{2,11},{3,10},{4,13},{5,12},{6,15},{7,14},{8,1},{9,0},... | collective-permute-start | bytes 221192 | tf_op jit(solution)/shard_map/ppermute | solution.py:153
  36.2 7.8 %collective-permute-start.18 = (bf16[96,384]{1,0:T(8,128)(2,1)S(1)}, bf16[96,384]{1,0:T(8,128)(2,1)S(1)}, u32[]{:S(2)}, u32[]{:S(2)}) collective-permute-start(bf16[96,384]{1,0:T(8,128)(2,1)S(1)} %get-tuple-element.54), channel_id=1, source_target_pairs={{0,12},{1,13},{2,14},{3,15},{4,8},{5,9},{6,10},{7,11},{8,4},{9,5},... | collective-permute-start | bytes 221192 | tf_op jit(solution)/shard_map/ppermute | solution.py:153
  40.9 9.0 %collective-permute-start.14 = (bf16[32,384]{1,0:T(8,128)(2,1)S(1)}, bf16[32,384]{1,0:T(8,128)(2,1)S(1)}, u32[]{:S(2)}, u32[]{:S(2)}) collective-permute-start(bf16[32,384]{1,0:T(8,128)(2,1)S(1)} %get-tuple-element.49), channel_id=1, source_target_pairs={{0,5},{1,4},{2,7},{3,6},{4,1},{5,0},{6,3},{7,2},{8,13},{9,12},{10,... | collective-permute-start | bytes 73736 | tf_op jit(solution)/shard_map/ppermute | solution.py:153
  44.7 11.9 %collective-permute-start.20 = (bf16[32,768]{1,0:T(8,128)(2,1)S(1)}, bf16[32,768]{1,0:T(8,128)(2,1)S(1)}, u32[]{:S(2)}, u32[]{:S(2)}) collective-permute-start(bf16[32,768]{1,0:T(8,128)(2,1)S(1)} %get-tuple-element.56), channel_id=1, source_target_pairs={{0,5},{1,4},{2,7},{3,6},{4,1},{5,0},{6,3},{7,2},{8,13},{9,12},{10,... | collective-permute-start | bytes 147464 | tf_op jit(solution)/shard_map/ppermute | solution.py:153
  44.8 11.9 %collective-permute-start.21 = (bf16[32,768]{1,0:T(8,128)(2,1)S(1)}, bf16[32,768]{1,0:T(8,128)(2,1)S(1)}, u32[]{:S(2)}, u32[]{:S(2)}) collective-permute-start(bf16[32,768]{1,0:T(8,128)(2,1)S(1)} %get-tuple-element.57), channel_id=1, source_target_pairs={{0,9},{1,8},{2,11},{3,10},{4,13},{5,12},{6,15},{7,14},{8,1},{9,0},... | collective-permute-start | bytes 147464 | tf_op jit(solution)/shard_map/ppermute | solution.py:153
  48.6 8.1 %collective-permute-start.22 = (bf16[32,768]{1,0:T(8,128)(2,1)S(1)}, bf16[32,768]{1,0:T(8,128)(2,1)S(1)}, u32[]{:S(2)}, u32[]{:S(2)}) collective-permute-start(bf16[32,768]{1,0:T(8,128)(2,1)S(1)} %get-tuple-element.58), channel_id=1, source_target_pairs={{0,12},{1,13},{2,14},{3,15},{4,8},{5,9},{6,10},{7,11},{8,4},{9,5},... | collective-permute-start | bytes 147464 | tf_op jit(solution)/shard_map/ppermute | solution.py:153
  48.9 4.9 %collective-permute-start.15 = (bf16[32,384]{1,0:T(8,128)(2,1)S(1)}, bf16[32,384]{1,0:T(8,128)(2,1)S(1)}, u32[]{:S(2)}, u32[]{:S(2)}) collective-permute-start(bf16[32,384]{1,0:T(8,128)(2,1)S(1)} %get-tuple-element.50), channel_id=1, source_target_pairs={{0,9},{1,8},{2,11},{3,10},{4,13},{5,12},{6,15},{7,14},{8,1},{9,0},... | collective-permute-start | bytes 73736 | tf_op jit(solution)/shard_map/ppermute | solution.py:153
  49.9 5.6 %collective-permute-start.16 = (bf16[32,384]{1,0:T(8,128)(2,1)S(1)}, bf16[32,384]{1,0:T(8,128)(2,1)S(1)}, u32[]{:S(2)}, u32[]{:S(2)}) collective-permute-start(bf16[32,384]{1,0:T(8,128)(2,1)S(1)} %get-tuple-element.51), channel_id=1, source_target_pairs={{0,12},{1,13},{2,14},{3,15},{4,8},{5,9},{6,10},{7,11},{8,4},{9,5},... | collective-permute-start | bytes 73736 | tf_op jit(solution)/shard_map/ppermute | solution.py:153

commit v4 on v3

--- a/solution.py
+++ b/solution.py
@@ -236,7 +236,8 @@
         fresh_v = jnp.concatenate([ref[:, vcols] for ref in fresh], 0)
         own_k = jnp.concatenate([ref[:, cols] for ref in own], 0)
         own_v = jnp.concatenate([ref[:, kcols] for ref in own], 0)
-        s_near = jnp.where(same, dot(q, fresh_k, NT), dot(q, own_k, NT))
+        s_near = dot(q, jnp.concatenate([own_k, fresh_k], 0), NT)
+        s_near = jnp.where(same, s_near[:, count:], s_near[:, :count])
         s_core = dot(q, core[:, cols], NT)
         s_text = dot(q, tk_ref[:, cols], NT)
         top = jnp.maximum(
@@ -247,8 +248,8 @@
         total = jnp.sum(e_near + e_core, -1, keepdims=True) + jnp.sum(e_text, -1, keepdims=True)
         p_near = e_near.astype(jnp.bfloat16)
         none = jnp.zeros_like(p_near)
-        acc = dot(jnp.where(same, p_near, none), fresh_v, NN)
-        acc += dot(jnp.where(same, none, p_near), own_v, NN)
+        p_near = jnp.concatenate([jnp.where(same, none, p_near), jnp.where(same, p_near, none)], 1)
+        acc = dot(p_near, jnp.concatenate([own_v, fresh_v], 0), NN)
         acc += dot(e_core.astype(jnp.bfloat16), core[:, kcols], NN)
         acc += dot(e_text.astype(jnp.bfloat16), tv_ref[:, cols], NN)
         span = slice(2 * count * pair, 2 * count * (pair + 1))
@@ -275,8 +276,8 @@
         e = jnp.exp(s - jnp.concatenate([top] * (s.shape[1] // LANES), 1))
         total = sum_ref[span, :] * shrink + jnp.sum(e, -1, keepdims=True)
         acc = acc_ref[span, :] * shrink + dot(e.astype(jnp.bfloat16), values, NN)
-        acc = acc / total
-        both = jnp.where(low, acc[:count], acc[count:]).astype(outs[0].dtype)
+        acc = jnp.where(low, acc[:count], acc[count:])
+        both = (acc / jnp.where(low, total[:count], total[count:])).astype(outs[0].dtype)
         outs[0][:, cols] = both
         for k in range(1, lines):
             outs[k][: k * rows, cols] = both[: k * rows]
@@ -287,13 +288,12 @@
 
 def project_kernel(ks, own_rows, first, last, *refs):
     weights, refs = refs[: QUAD + 2], refs[QUAD + 2 :]
-    weights = [weights[:1], weights[1:2], weights[2:4], weights[4:6]]
     att, refs = refs[: len(ks)], refs[len(ks) :]
     index = lax.axis_index("patch")
     line = index // QUAD
-    acc = [None] * QUAD
+    acc = None
     if not first:
-        acc, refs = [refs[0][j] for j in range(QUAD)], refs[1:]
+        acc, refs = refs[0][...], refs[1:]
     width = att[0].shape[1]
 
     def block(ref, i, rows):
@@ -308,14 +308,13 @@
             spots = [(m ^ k) - ((m ^ k) > k) for m in range(1, QUAD)]
             a = jnp.concatenate([block(ref, i, ref.shape[0] // len(spots)) for i in spots], 0)
         span = pl.ds(pl.multiple_of((line ^ k) * width, LANES), width)
-        for j in range(QUAD):
-            weight = jnp.concatenate([part[:, span] for part in weights[j]], 0)
-            part = dot(a, weight, NT)
-            acc[j] = part if acc[j] is None else acc[j] + part
+        part = dot(a, jnp.concatenate([ref[:, span] for ref in weights], 0), NT)
+        acc = part if acc is None else acc + part
     if not last:
-        for j in range(QUAD):
-            refs[0][j] = acc[j]
+        refs[0][...] = acc
         return
+    seat_width = weights[0].shape[0]
+    acc = [acc[:, j * seat_width : (j + 1) * seat_width] for j in range(QUAD)]
     gate_ref, outs = refs[0], refs[1:]
     odd = (index & 1) == 1
     high = (index & 2) == 2
@@ -444,7 +443,7 @@
         )(*weights, *[attended[k] for k in ks], *more)
 
     near, far, every = (0, 1), tuple(range(2, lines)), tuple(range(lines))
-    sums = shaped(QUAD, count - rows, out_weight.shape[1], dtype=jnp.float32)
+    sums = shaped(count - rows, out_width, dtype=jnp.float32)
     made = shaped(rows, out_width)
     sums = project(near, False, theirs, None, sums)
     parts = [None, *project(far, False, theirs, sums, [made] * (lines - 1))]

time: 57.6 us -> 57.4 us (level)
  no operation moved by 1% of the time
where the time goes in v4:
time: 57.4 us; the launch traced here: 57.2 us
  starting transfers between devices  35.8 us (62%)
  waiting for transfers between devices  12.9 us (22%)
  Pallas kernels  7.76 us (14%)
  between operations  0.79 us (1%)
    ppermute x23, starting transfers between devices, swap(): return lax.ppermute(shard, 'patch', [(i, i ^ by) for i in range(peers)])  35.8 us
    ppermute x23, waiting for transfers between devices, swap(): return lax.ppermute(shard, 'patch', [(i, i ^ by) for i in range(peers)])  12.9 us
    pallas_call x3, Pallas kernels, project(): kernel(functools.partial(project_kernel, ks, own_rows, first, last), outs...  2.16 us
    pallas_call x1, Pallas kernels, square_body(): kernel(early_kernel, [shaped(stacked, LANES)] + [shaped(stacked, LANES, d...  1.44 us
    pallas_call x1, Pallas kernels, square_body(): kernel(pack_kernel, [shaped(rows, 2 * width)] * lines + [shaped(rows, 3 *...  1.39 us
    pallas_call x1, Pallas kernels, square_body(): kernel(fetch_kernel, [shaped(text, width)] * 2 + [shaped(1, out_width, dt...  1.26 us
  transfers between devices with their start and end apart: 23, of which 8 were waited for; matrix products, arithmetic and copies ran while one was open for 0% of the time, Pallas kernels for 10%

profile of v4, /device:TPU:0, one launch (start us, length us, event | category | flops | bytes accessed | tf_op | source)
XLA Modules:
  0.0 57.2 jit_solution(2479669389226100760)
XLA Ops:
  0.0 1.4 %shard_map.100 = (bf16[32,768]{1,0:T(8,128)(2,1)S(1)}, bf16[32,768]{1,0:T(8,128)(2,1)S(1)}, bf16[32,768]{1,0:T(8,128)(2,1)S(1)}, bf16[32,768]{1,0:T(8,128)(2,1)S...) custom-call(bf16[32,1536]{1,0:T(8,128)(2,1)} %q_ref.1, ...), custom_call_target="tpu_custom_call" | custom-call | tf_op jit(solution)/shard_map/pallas_call | solution.py:386
  1.4 5.1 %collective-permute-start.10 = (bf16[32,768]{1,0:T(8,128)(2,1)S(1)}, bf16[32,768]{1,0:T(8,128)(2,1)S(1)}, u32[]{:S(2)}, u32[]{:S(2)}) collective-permute-start(bf16[32,768]{1,0:T(8,128)(2,1)S(1)} %get-tuple-element.43), channel_id=1, source_target_pairs={{0,12},{1,13},{2,14},{3,15},{4,8},{5,9},{6,10},{7,11},{8,4},{9,5},... | collective-permute-start | bytes 147464 | tf_op jit(solution)/shard_map/ppermute | solution.py:153
  6.5 0.0 collective-permute-start.8
  6.5 0.4 collective-permute-start.9
  6.9 1.7 %collective-permute-start.1 = (bf16[96,1536]{1,0:T(8,128)(2,1)S(1)}, bf16[96,1536]{1,0:T(8,128)(2,1)S(1)}, u32[]{:S(2)}, u32[]{:S(2)}) collective-permute-start(bf16[96,1536]{1,0:T(8,128)(2,1)S(1)} %get-tuple-element.32), channel_id=1, source_target_pairs={{0,2},{1,3},{2,0},{3,1},{4,6},{5,7},{6,4},{7,5},{8,10},{9,11},{10,... | collective-permute-start | bytes 884744 | tf_op jit(solution)/shard_map/ppermute | solution.py:153
  9.2 0.0 copy-start
  9.2 1.3 %shard_map.101 = (bf16[226,384]{1,0:T(8,128)(2,1)S(1)}, bf16[226,384]{1,0:T(8,128)(2,1)S(1)}, f32[1,768]{1,0:T(1,128)S(1)}, bf16[96,1536]{1,0:T(8,128)(2,1)S(1)}) custom-call(s32[1]{0:T(128)S(6)} %copy.11.step_ref, bf16[226,1536]{1,0:T(8,128)(2,1)} %tk_ref.1, bf16[226,1536]{1,0:T(8,128)(2,1)} %tv_ref.1, f32[50,3072]{1,0:T(8,128)} %gate_ref.1, ...), custom_call_target="tpu_custom_call" | custom-call | tf_op jit(solution)/shard_map/pallas_call | solution.py:399
  10.5 0.4 collective-permute-start.2
  10.9 0.0 collective-permute-done.10.refs_3_.refs_7_
  10.9 0.0 copy-done
  10.9 0.0 collective-permute-start
  10.9 0.0 collective-permute-done.8.refs_1_.refs_5_
  10.9 0.9 %collective-permute-start.5 = (bf16[32,1152]{1,0:T(8,128)(2,1)S(1)}, bf16[32,1152]{1,0:T(8,128)(2,1)S(1)}, u32[]{:S(2)}, u32[]{:S(2)}) collective-permute-start(bf16[32,1152]{1,0:T(8,128)(2,1)S(1)} %get-tuple-element.37), channel_id=1, source_target_pairs={{0,5},{1,4},{2,7},{3,6},{4,1},{5,0},{6,3},{7,2},{8,13},{9,12},{10,... | collective-permute-start | bytes 221192 | tf_op jit(solution)/shard_map/ppermute | solution.py:153
  11.9 0.0 collective-permute-done.9.refs_2_.refs_6_
  11.9 1.6 %collective-permute-start.12 = (bf16[128,768]{1,0:T(8,128)(2,1)S(1)}, bf16[128,768]{1,0:T(8,128)(2,1)S(1)}, u32[]{:S(2)}, u32[]{:S(2)}) collective-permute-start(bf16[128,768]{1,0:T(8,128)(2,1)S(1)} %shard_map.102), channel_id=1, source_target_pairs={{0,2},{1,3},{2,0},{3,1},{4,6},{5,7},{6,4},{7,5},{8,10},{9,11},{10,... | collective-permute-start | bytes 589832 | tf_op jit(solution)/shard_map/ppermute | solution.py:153
  13.5 1.5 %collective-permute-done.5.refs_1_ = bf16[32,1152]{1,0:T(8,128)(2,1)S(1)} collective-permute-done((bf16[32,1152]{1,0:T(8,128)(2,1)S(1)}, bf16[32,1152]{1,0:T(8,128)(2,1)S(1)}, u32[]{:S(2)}, u32[]{:S(2)}) %collective-permute-start.5) | collective-permute-done | bytes 73760 | tf_op jit(solution)/shard_map/ppermute | solution.py:153
  15.0 2.9 %collective-permute-start.6 = (bf16[32,1152]{1,0:T(8,128)(2,1)S(1)}, bf16[32,1152]{1,0:T(8,128)(2,1)S(1)}, u32[]{:S(2)}, u32[]{:S(2)}) collective-permute-start(bf16[32,1152]{1,0:T(8,128)(2,1)S(1)} %get-tuple-element.38), channel_id=1, source_target_pairs={{0,9},{1,8},{2,11},{3,10},{4,13},{5,12},{6,15},{7,14},{8,1},{9,0},... | collective-permute-start | bytes 221192 | tf_op jit(solution)/shard_map/ppermute | solution.py:153
  17.9 2.2 %collective-permute-done.6.refs_2_ = bf16[32,1152]{1,0:T(8,128)(2,1)S(1)} collective-permute-done((bf16[32,1152]{1,0:T(8,128)(2,1)S(1)}, bf16[32,1152]{1,0:T(8,128)(2,1)S(1)}, u32[]{:S(2)}, u32[]{:S(2)}) %collective-permute-start.6) | collective-permute-done | bytes 73760 | tf_op jit(solution)/shard_map/ppermute | solution.py:153
  20.1 5.4 %collective-permute-start.7 = (bf16[32,1152]{1,0:T(8,128)(2,1)S(1)}, bf16[32,1152]{1,0:T(8,128)(2,1)S(1)}, u32[]{:S(2)}, u32[]{:S(2)}) collective-permute-start(bf16[32,1152]{1,0:T(8,128)(2,1)S(1)} %get-tuple-element.39), channel_id=1, source_target_pairs={{0,12},{1,13},{2,14},{3,15},{4,8},{5,9},{6,10},{7,11},{8,4},{9,5},... | collective-permute-start | bytes 221192 | tf_op jit(solution)/shard_map/ppermute | solution.py:153
  25.6 2.7 %collective-permute-done.7.refs_3_ = bf16[32,1152]{1,0:T(8,128)(2,1)S(1)} collective-permute-done((bf16[32,1152]{1,0:T(8,128)(2,1)S(1)}, bf16[32,1152]{1,0:T(8,128)(2,1)S(1)}, u32[]{:S(2)}, u32[]{:S(2)}) %collective-permute-start.7) | collective-permute-done | bytes 73760 | tf_op jit(solution)/shard_map/ppermute | solution.py:153
  28.2 0.0 collective-permute-start.11
  28.2 0.0 collective-permute-done.12.y_ref
  28.2 0.5 collective-permute-start.13
  28.7 0.0 collective-permute-done.1.refs_2_
  28.7 0.1 collective-permute-start.3
  28.8 0.0 collective-permute-done.2.refs_3_
  28.8 0.4 collective-permute-start.4
  29.2 0.4 collective-permute-done.11.refs_8_
  29.6 1.4 %shard_map.103 = (bf16[768,128]{1,0:T(8,128)(2,1)S(1)}, f32[768,128]{1,0:T(8,128)S(1)}, f32[768,128]{1,0:T(8,128)S(1)}, f32[768,128]{1,0:T(8,128)S(1)}) custom-call(bf16[226,384]{1,0:T(8,128)(2,1)S(1)} %get-tuple-element.34.tk_ref, bf16[226,384]{1,0:T(8,128)(2,1)S(1)} %get-tuple-element.35.tv_ref, bf16[32,1152]{1,0:T(8,128)(2,1)S(1)} %get-tuple-element.36.refs_0_, ...), custom_call_target="tpu_custom_call" | custom-call | tf_op jit(solution)/shard_map/pallas_call | solution.py:416
  31.1 0.0 collective-permute-done.13.both_ref
  31.1 0.8 %shard_map.104 = (bf16[128,384]{1,0:T(8,128)(2,1)S(1)}, bf16[96,384]{1,0:T(8,128)(2,1)S(1)}, bf16[96,384]{1,0:T(8,128)(2,1)S(1)}, bf16[96,384]{1,0:T(8,128)(2,1)...) custom-call(bf16[768,128]{1,0:T(8,128)(2,1)S(1)} %get-tuple-element.44.q_ref, ...), custom_call_target="tpu_custom_call" | custom-call | tf_op jit(solution)/shard_map/pallas_call | solution.py:421
  31.9 0.5 collective-permute-start.19
  32.4 3.4 %collective-permute-start.17 = (bf16[96,384]{1,0:T(8,128)(2,1)S(1)}, bf16[96,384]{1,0:T(8,128)(2,1)S(1)}, u32[]{:S(2)}, u32[]{:S(2)}) collective-permute-start(bf16[96,384]{1,0:T(8,128)(2,1)S(1)} %get-tuple-element.53), channel_id=1, source_target_pairs={{0,9},{1,8},{2,11},{3,10},{4,13},{5,12},{6,15},{7,14},{8,1},{9,0},... | collective-permute-start | bytes 221192 | tf_op jit(solution)/shard_map/ppermute | solution.py:153
  35.7 0.5 collective-permute-done.19.refs_7_
  36.2 4.7 %collective-permute-start.18 = (bf16[96,384]{1,0:T(8,128)(2,1)S(1)}, bf16[96,384]{1,0:T(8,128)(2,1)S(1)}, u32[]{:S(2)}, u32[]{:S(2)}) collective-permute-start(bf16[96,384]{1,0:T(8,128)(2,1)S(1)} %get-tuple-element.54), channel_id=1, source_target_pairs={{0,12},{1,13},{2,14},{3,15},{4,8},{5,9},{6,10},{7,11},{8,4},{9,5},... | collective-permute-start | bytes 221192 | tf_op jit(solution)/shard_map/ppermute | solution.py:153
  40.9 0.0 collective-permute-done.3.refs_4_
  40.9 0.0 collective-permute-start.14
  40.9 0.0 collective-permute-done.4.refs_5_
  40.9 0.0 collective-permute-done.refs_1_
  40.9 0.5 shard_map.106.refs_8_
  41.4 0.0 collective-permute-done.17.refs_6_
  41.4 2.6 %collective-permute-done.18.refs_7_ = bf16[96,384]{1,0:T(8,128)(2,1)S(1)} collective-permute-done((bf16[96,384]{1,0:T(8,128)(2,1)S(1)}, bf16[96,384]{1,0:T(8,128)(2,1)S(1)}, u32[]{:S(2)}, u32[]{:S(2)}) %collective-permute-start.18) | collective-permute-done | bytes 73760 | tf_op jit(solution)/shard_map/ppermute | solution.py:153
  44.0 0.7 %shard_map.107 = (bf16[32,768]{1,0:T(8,128)(2,1)S(1)}, bf16[32,768]{1,0:T(8,128)(2,1)S(1)}, bf16[32,768]{1,0:T(8,128)(2,1)S(1)}) custom-call(bf16[192,1536]{1,0:T(8,128)(2,1)S(1)} %bitcast.5, bf16[192,1536]{1,0:T(8,128)(2,1)S(1)} %collective-permute-done.refs_1_, bf16[96,1536]{1,0:T(8,128)(2,1)S(1)} %collective-permute-done.1.refs_2_, ...), custom_call_target="tpu_custom_call" | custom-call | tf_op jit(solution)/shard_map/pallas_call | solution.py:438
  44.7 0.1 collective-permute-start.20
  44.8 3.8 %collective-permute-start.21 = (bf16[32,768]{1,0:T(8,128)(2,1)S(1)}, bf16[32,768]{1,0:T(8,128)(2,1)S(1)}, u32[]{:S(2)}, u32[]{:S(2)}) collective-permute-start(bf16[32,768]{1,0:T(8,128)(2,1)S(1)} %get-tuple-element.57), channel_id=1, source_target_pairs={{0,9},{1,8},{2,11},{3,10},{4,13},{5,12},{6,15},{7,14},{8,1},{9,0},... | collective-permute-start | bytes 147464 | tf_op jit(solution)/shard_map/ppermute | solution.py:153
  48.6 0.3 collective-permute-start.22
  48.9 1.0 %collective-permute-start.15 = (bf16[32,384]{1,0:T(8,128)(2,1)S(1)}, bf16[32,384]{1,0:T(8,128)(2,1)S(1)}, u32[]{:S(2)}, u32[]{:S(2)}) collective-permute-start(bf16[32,384]{1,0:T(8,128)(2,1)S(1)} %get-tuple-element.50), channel_id=1, source_target_pairs={{0,9},{1,8},{2,11},{3,10},{4,13},{5,12},{6,15},{7,14},{8,1},{9,0},... | collective-permute-start | bytes 73736 | tf_op jit(solution)/shard_map/ppermute | solution.py:153
  49.9 0.0 collective-permute-done.14.refs_7_
  49.9 2.6 %collective-permute-start.16 = (bf16[32,384]{1,0:T(8,128)(2,1)S(1)}, bf16[32,384]{1,0:T(8,128)(2,1)S(1)}, u32[]{:S(2)}, u32[]{:S(2)}) collective-permute-start(bf16[32,384]{1,0:T(8,128)(2,1)S(1)} %get-tuple-element.51), channel_id=1, source_target_pairs={{0,12},{1,13},{2,14},{3,15},{4,8},{5,9},{6,10},{7,11},{8,4},{9,5},... | collective-permute-start | bytes 73736 | tf_op jit(solution)/shard_map/ppermute | solution.py:153
  52.4 1.4 %collective-permute-done.15.refs_8_ = bf16[32,384]{1,0:T(8,128)(2,1)S(1)} collective-permute-done((bf16[32,384]{1,0:T(8,128)(2,1)S(1)}, bf16[32,384]{1,0:T(8,128)(2,1)S(1)}, u32[]{:S(2)}, u32[]{:S(2)}) %collective-permute-start.15) | collective-permute-done | bytes 24608 | tf_op jit(solution)/shard_map/ppermute | solution.py:153
  53.8 1.7 %collective-permute-done.16.refs_9_ = bf16[32,384]{1,0:T(8,128)(2,1)S(1)} collective-permute-done((bf16[32,384]{1,0:T(8,128)(2,1)S(1)}, bf16[32,384]{1,0:T(8,128)(2,1)S(1)}, u32[]{:S(2)}, u32[]{:S(2)}) %collective-permute-start.16) | collective-permute-done | bytes 24608 | tf_op jit(solution)/shard_map/ppermute | solution.py:153
  55.5 1.0 %shard_map.105.refs_0_ = bf16[32,768]{1,0:T(8,128)(2,1)S(1)} custom-call(bf16[192,1536]{1,0:T(8,128)(2,1)S(1)} %bitcast.6, bf16[192,1536]{1,0:T(8,128)(2,1)S(1)} %collective-permute-done.refs_1_, bf16[96,1536]{1,0:T(8,128)(2,1)S(1)} %collective-permute-done.1.refs_2_, bf16[96,1536]{1,0:T(8,128)(2,1)S(1)} %collective-permute-done.2.refs_3_, ...), custom_call_target="tpu_custom_call" | custom-call | tf_op jit(solution)/shard_map/pallas_call | solution.py:438
  56.5 0.0 collective-permute-done.20.refs_1_
  56.5 0.0 collective-permute-done.21.refs_2_
  56.5 0.0 collective-permute-done.22.refs_3_
  56.5 0.7 %place.1 = bf16[32,3072]{1,0:T(8,128)(2,1)} custom-call(bf16[32,768]{1,0:T(8,128)(2,1)S(1)} %shard_map.105.refs_0_, bf16[32,768]{1,0:T(8,128)(2,1)S(1)} %collective-permute-done.20.refs_1_, bf16[32,768]{1,0:T(8,128)(2,1)S(1)} %collective-permute-done.21.refs_2_, bf16[32,768]{1,0:T(8,128)(2,1)S(1)} %collective-permute-done.22.refs_3_), custom_call_target="tpu_custom_call" | custom-call | tf_op jit(solution)/shard_map/place/pallas_call | solution.py:453
  (1 shorter events, 0.0 us)
Async XLA Ops:
  1.4 9.5 %collective-permute-start.10 = (bf16[32,768]{1,0:T(8,128)(2,1)S(1)}, bf16[32,768]{1,0:T(8,128)(2,1)S(1)}, u32[]{:S(2)}, u32[]{:S(2)}) collective-permute-start(bf16[32,768]{1,0:T(8,128)(2,1)S(1)} %get-tuple-element.43), channel_id=1, source_target_pairs={{0,12},{1,13},{2,14},{3,15},{4,8},{5,9},{6,10},{7,11},{8,4},{9,5},... | collective-permute-start | bytes 147464 | tf_op jit(solution)/shard_map/ppermute | solution.py:153
  6.5 4.4 %collective-permute-start.8 = (bf16[32,768]{1,0:T(8,128)(2,1)S(1)}, bf16[32,768]{1,0:T(8,128)(2,1)S(1)}, u32[]{:S(2)}, u32[]{:S(2)}) collective-permute-start(bf16[32,768]{1,0:T(8,128)(2,1)S(1)} %get-tuple-element.41), channel_id=1, source_target_pairs={{0,5},{1,4},{2,7},{3,6},{4,1},{5,0},{6,3},{7,2},{8,13},{9,12},{10,... | collective-permute-start | bytes 147464 | tf_op jit(solution)/shard_map/ppermute | solution.py:153
  6.5 5.3 %collective-permute-start.9 = (bf16[32,768]{1,0:T(8,128)(2,1)S(1)}, bf16[32,768]{1,0:T(8,128)(2,1)S(1)}, u32[]{:S(2)}, u32[]{:S(2)}) collective-permute-start(bf16[32,768]{1,0:T(8,128)(2,1)S(1)} %get-tuple-element.42), channel_id=1, source_target_pairs={{0,9},{1,8},{2,11},{3,10},{4,13},{5,12},{6,15},{7,14},{8,1},{9,0},... | collective-permute-start | bytes 147464 | tf_op jit(solution)/shard_map/ppermute | solution.py:153
  6.9 21.8 %collective-permute-start.1 = (bf16[96,1536]{1,0:T(8,128)(2,1)S(1)}, bf16[96,1536]{1,0:T(8,128)(2,1)S(1)}, u32[]{:S(2)}, u32[]{:S(2)}) collective-permute-start(bf16[96,1536]{1,0:T(8,128)(2,1)S(1)} %get-tuple-element.32), channel_id=1, source_target_pairs={{0,2},{1,3},{2,0},{3,1},{4,6},{5,7},{6,4},{7,5},{8,10},{9,11},{10,... | collective-permute-start | bytes 884744 | tf_op jit(solution)/shard_map/ppermute | solution.py:153
  9.2 1.7 %copy-start = (bf16[1536,192]{0,1:T(8,128)(2,1)S(1)}, bf16[1536,192]{0,1:T(8,128)(2,1)}, u32[]{:S(2)}) copy-start(bf16[1536,192]{0,1:T(8,128)(2,1)} %param.17) | copy-start | bytes 1769476
  10.5 18.3 %collective-permute-start.2 = (bf16[96,1536]{1,0:T(8,128)(2,1)S(1)}, bf16[96,1536]{1,0:T(8,128)(2,1)S(1)}, u32[]{:S(2)}, u32[]{:S(2)}) collective-permute-start(bf16[96,1536]{1,0:T(8,128)(2,1)S(1)} %get-tuple-element.33), channel_id=1, source_target_pairs={{0,2},{1,3},{2,0},{3,1},{4,6},{5,7},{6,4},{7,5},{8,10},{9,11},{10,... | collective-permute-start | bytes 884744 | tf_op jit(solution)/shard_map/ppermute | solution.py:153
  10.9 30.0 %collective-permute-start = (bf16[192,1536]{1,0:T(8,128)(2,1)S(1)}, bf16[192,1536]{1,0:T(8,128)(2,1)S(1)}, u32[]{:S(2)}, u32[]{:S(2)}) collective-permute-start(bf16[192,1536]{1,0:T(8,128)(2,1)S(1)} %bitcast.3), channel_id=1, source_target_pairs={{0,1},{1,0},{2,3},{3,2},{4,5},{5,4},{6,7},{7,6},{8,9},{9,8},{10,11... | collective-permute-start | bytes 1769480 | tf_op jit(solution)/shard_map/ppermute | solution.py:153
  10.9 4.0 %collective-permute-start.5 = (bf16[32,1152]{1,0:T(8,128)(2,1)S(1)}, bf16[32,1152]{1,0:T(8,128)(2,1)S(1)}, u32[]{:S(2)}, u32[]{:S(2)}) collective-permute-start(bf16[32,1152]{1,0:T(8,128)(2,1)S(1)} %get-tuple-element.37), channel_id=1, source_target_pairs={{0,5},{1,4},{2,7},{3,6},{4,1},{5,0},{6,3},{7,2},{8,13},{9,12},{10,... | collective-permute-start | bytes 221192 | tf_op jit(solution)/shard_map/ppermute | solution.py:153
  11.9 16.3 %collective-permute-start.12 = (bf16[128,768]{1,0:T(8,128)(2,1)S(1)}, bf16[128,768]{1,0:T(8,128)(2,1)S(1)}, u32[]{:S(2)}, u32[]{:S(2)}) collective-permute-start(bf16[128,768]{1,0:T(8,128)(2,1)S(1)} %shard_map.102), channel_id=1, source_target_pairs={{0,2},{1,3},{2,0},{3,1},{4,6},{5,7},{6,4},{7,5},{8,10},{9,11},{10,... | collective-permute-start | bytes 589832 | tf_op jit(solution)/shard_map/ppermute | solution.py:153
  15.0 5.2 %collective-permute-start.6 = (bf16[32,1152]{1,0:T(8,128)(2,1)S(1)}, bf16[32,1152]{1,0:T(8,128)(2,1)S(1)}, u32[]{:S(2)}, u32[]{:S(2)}) collective-permute-start(bf16[32,1152]{1,0:T(8,128)(2,1)S(1)} %get-tuple-element.38), channel_id=1, source_target_pairs={{0,9},{1,8},{2,11},{3,10},{4,13},{5,12},{6,15},{7,14},{8,1},{9,0},... | collective-permute-start | bytes 221192 | tf_op jit(solution)/shard_map/ppermute | solution.py:153
  20.1 8.1 %collective-permute-start.7 = (bf16[32,1152]{1,0:T(8,128)(2,1)S(1)}, bf16[32,1152]{1,0:T(8,128)(2,1)S(1)}, u32[]{:S(2)}, u32[]{:S(2)}) collective-permute-start(bf16[32,1152]{1,0:T(8,128)(2,1)S(1)} %get-tuple-element.39), channel_id=1, source_target_pairs={{0,12},{1,13},{2,14},{3,15},{4,8},{5,9},{6,10},{7,11},{8,4},{9,5},... | collective-permute-start | bytes 221192 | tf_op jit(solution)/shard_map/ppermute | solution.py:153
  28.2 1.4 %collective-permute-start.11 = (bf16[128,768]{1,0:T(8,128)(2,1)S(1)}, bf16[128,768]{1,0:T(8,128)(2,1)S(1)}, u32[]{:S(2)}, u32[]{:S(2)}) collective-permute-start(bf16[128,768]{1,0:T(8,128)(2,1)S(1)} %shard_map.102), channel_id=1, source_target_pairs={{0,1},{1,0},{2,3},{3,2},{4,5},{5,4},{6,7},{7,6},{8,9},{9,8},{10,11... | collective-permute-start | bytes 589832 | tf_op jit(solution)/shard_map/ppermute | solution.py:153
  28.2 2.9 %collective-permute-start.13 = (bf16[128,768]{1,0:T(8,128)(2,1)S(1)}, bf16[128,768]{1,0:T(8,128)(2,1)S(1)}, u32[]{:S(2)}, u32[]{:S(2)}) collective-permute-start(bf16[128,768]{1,0:T(8,128)(2,1)S(1)} %collective-permute-done.12.y_ref), channel_id=1, source_target_pairs={{0,1},{1,0},{2,3},{3,2},{4,5},{5,4},{6,7},{7,6},{8,9},{9,8},{10,11... | collective-permute-start | bytes 589832 | tf_op jit(solution)/shard_map/ppermute | solution.py:153
  28.7 12.2 %collective-permute-start.3 = (bf16[96,1536]{1,0:T(8,128)(2,1)S(1)}, bf16[96,1536]{1,0:T(8,128)(2,1)S(1)}, u32[]{:S(2)}, u32[]{:S(2)}) collective-permute-start(bf16[96,1536]{1,0:T(8,128)(2,1)S(1)} %collective-permute-done.1.refs_2_), channel_id=1, source_target_pairs={{0,1},{1,0},{2,3},{3,2},{4,5},{5,4},{6,7},{7,6},{8,9},{9,8},{10,11... | collective-permute-start | bytes 884744 | tf_op jit(solution)/shard_map/ppermute | solution.py:153
  28.8 12.1 %collective-permute-start.4 = (bf16[96,1536]{1,0:T(8,128)(2,1)S(1)}, bf16[96,1536]{1,0:T(8,128)(2,1)S(1)}, u32[]{:S(2)}, u32[]{:S(2)}) collective-permute-start(bf16[96,1536]{1,0:T(8,128)(2,1)S(1)} %collective-permute-done.2.refs_3_), channel_id=1, source_target_pairs={{0,1},{1,0},{2,3},{3,2},{4,5},{5,4},{6,7},{7,6},{8,9},{9,8},{10,11... | collective-permute-start | bytes 884744 | tf_op jit(solution)/shard_map/ppermute | solution.py:153
  31.9 4.3 %collective-permute-start.19 = (bf16[96,384]{1,0:T(8,128)(2,1)S(1)}, bf16[96,384]{1,0:T(8,128)(2,1)S(1)}, u32[]{:S(2)}, u32[]{:S(2)}) collective-permute-start(bf16[96,384]{1,0:T(8,128)(2,1)S(1)} %get-tuple-element.55), channel_id=1, source_target_pairs={{0,5},{1,4},{2,7},{3,6},{4,1},{5,0},{6,3},{7,2},{8,13},{9,12},{10,... | collective-permute-start | bytes 221192 | tf_op jit(solution)/shard_map/ppermute | solution.py:153
  32.4 9.0 %collective-permute-start.17 = (bf16[96,384]{1,0:T(8,128)(2,1)S(1)}, bf16[96,384]{1,0:T(8,128)(2,1)S(1)}, u32[]{:S(2)}, u32[]{:S(2)}) collective-permute-start(bf16[96,384]{1,0:T(8,128)(2,1)S(1)} %get-tuple-element.53), channel_id=1, source_target_pairs={{0,9},{1,8},{2,11},{3,10},{4,13},{5,12},{6,15},{7,14},{8,1},{9,0},... | collective-permute-start | bytes 221192 | tf_op jit(solution)/shard_map/ppermute | solution.py:153
  36.2 7.8 %collective-permute-start.18 = (bf16[96,384]{1,0:T(8,128)(2,1)S(1)}, bf16[96,384]{1,0:T(8,128)(2,1)S(1)}, u32[]{:S(2)}, u32[]{:S(2)}) collective-permute-start(bf16[96,384]{1,0:T(8,128)(2,1)S(1)} %get-tuple-element.54), channel_id=1, source_target_pairs={{0,12},{1,13},{2,14},{3,15},{4,8},{5,9},{6,10},{7,11},{8,4},{9,5},... | collective-permute-start | bytes 221192 | tf_op jit(solution)/shard_map/ppermute | solution.py:153
  40.9 9.0 %collective-permute-start.14 = (bf16[32,384]{1,0:T(8,128)(2,1)S(1)}, bf16[32,384]{1,0:T(8,128)(2,1)S(1)}, u32[]{:S(2)}, u32[]{:S(2)}) collective-permute-start(bf16[32,384]{1,0:T(8,128)(2,1)S(1)} %get-tuple-element.49), channel_id=1, source_target_pairs={{0,5},{1,4},{2,7},{3,6},{4,1},{5,0},{6,3},{7,2},{8,13},{9,12},{10,... | collective-permute-start | bytes 73736 | tf_op jit(solution)/shard_map/ppermute | solution.py:153
  44.7 11.8 %collective-permute-start.20 = (bf16[32,768]{1,0:T(8,128)(2,1)S(1)}, bf16[32,768]{1,0:T(8,128)(2,1)S(1)}, u32[]{:S(2)}, u32[]{:S(2)}) collective-permute-start(bf16[32,768]{1,0:T(8,128)(2,1)S(1)} %get-tuple-element.56), channel_id=1, source_target_pairs={{0,5},{1,4},{2,7},{3,6},{4,1},{5,0},{6,3},{7,2},{8,13},{9,12},{10,... | collective-permute-start | bytes 147464 | tf_op jit(solution)/shard_map/ppermute | solution.py:153
  44.8 11.7 %collective-permute-start.21 = (bf16[32,768]{1,0:T(8,128)(2,1)S(1)}, bf16[32,768]{1,0:T(8,128)(2,1)S(1)}, u32[]{:S(2)}, u32[]{:S(2)}) collective-permute-start(bf16[32,768]{1,0:T(8,128)(2,1)S(1)} %get-tuple-element.57), channel_id=1, source_target_pairs={{0,9},{1,8},{2,11},{3,10},{4,13},{5,12},{6,15},{7,14},{8,1},{9,0},... | collective-permute-start | bytes 147464 | tf_op jit(solution)/shard_map/ppermute | solution.py:153
  48.6 7.9 %collective-permute-start.22 = (bf16[32,768]{1,0:T(8,128)(2,1)S(1)}, bf16[32,768]{1,0:T(8,128)(2,1)S(1)}, u32[]{:S(2)}, u32[]{:S(2)}) collective-permute-start(bf16[32,768]{1,0:T(8,128)(2,1)S(1)} %get-tuple-element.58), channel_id=1, source_target_pairs={{0,12},{1,13},{2,14},{3,15},{4,8},{5,9},{6,10},{7,11},{8,4},{9,5},... | collective-permute-start | bytes 147464 | tf_op jit(solution)/shard_map/ppermute | solution.py:153
  48.9 4.9 %collective-permute-start.15 = (bf16[32,384]{1,0:T(8,128)(2,1)S(1)}, bf16[32,384]{1,0:T(8,128)(2,1)S(1)}, u32[]{:S(2)}, u32[]{:S(2)}) collective-permute-start(bf16[32,384]{1,0:T(8,128)(2,1)S(1)} %get-tuple-element.50), channel_id=1, source_target_pairs={{0,9},{1,8},{2,11},{3,10},{4,13},{5,12},{6,15},{7,14},{8,1},{9,0},... | collective-permute-start | bytes 73736 | tf_op jit(solution)/shard_map/ppermute | solution.py:153
  49.9 5.6 %collective-permute-start.16 = (bf16[32,384]{1,0:T(8,128)(2,1)S(1)}, bf16[32,384]{1,0:T(8,128)(2,1)S(1)}, u32[]{:S(2)}, u32[]{:S(2)}) collective-permute-start(bf16[32,384]{1,0:T(8,128)(2,1)S(1)} %get-tuple-element.51), channel_id=1, source_target_pairs={{0,12},{1,13},{2,14},{3,15},{4,8},{5,9},{6,10},{7,11},{8,4},{9,5},... | collective-permute-start | bytes 73736 | tf_op jit(solution)/shard_map/ppermute | solution.py:153
